TPU v7x, 32 devices: a whole 2x2x4 slice. The times are simulated.
32 devices in a mesh: dp: 2 (over x), seq: 8 (over z, y), mp: 2 (over core).
Axes of the slice: x: 2, y: 2, z: 4, core: 2. Of those that a mesh axis runs over, the one named last changes fastest.
Arguments:
- inputs: bfloat16 [2, 2, 1024, 2304], P(None, 'dp', 'seq'), may hold values from -6 to 6
- cotangent: bfloat16 [2, 2, 1024, 2304], P(None, 'dp', 'seq'), may hold values from -6 to 6
- pre_attention: float32 [2304], replicated, may hold values from 0.5 to 1.5
- post_attention: float32 [2304], replicated, may hold values from 0.5 to 1.5
- pre_feedforward: float32 [2304], replicated, may hold values from 0.5 to 1.5
- post_feedforward: float32 [2304], replicated, may hold values from 0.5 to 1.5
- query_weight: bfloat16 [2304, 2048], P(('dp', 'seq'), 'mp'), may hold values from -0.625 to 0.625
- key_matrix: bfloat16 [2304, 1024], P(('dp', 'seq'), 'mp'), may hold values from -0.125 to 0.125
- value_matrix: bfloat16 [2304, 1024], P(('dp', 'seq'), 'mp'), may hold values from -0.125 to 0.125
- output_weight: bfloat16 [2048, 2304], P('mp', ('dp', 'seq')), may hold values from -0.125 to 0.125
- gate_weight: bfloat16 [2304, 9216], P(('dp', 'seq'), 'mp'), may hold values from -0.125 to 0.125
- up_weight: bfloat16 [2304, 9216], P(('dp', 'seq'), 'mp'), may hold values from -0.125 to 0.125
- down_weight: bfloat16 [9216, 2304], P('mp', ('dp', 'seq')), may hold values from -0.0625 to 0.0625
- adapter_down: bfloat16 [8, 16, 22784], replicated, may hold values from -0.125 to 0.125
- adapter_up: bfloat16 [8, 16, 27136], replicated, may hold values from -0.75 to 0.75
- prefix_lengths: int32 [2, 2], P(None, 'dp'), may hold values from 102 to 512
- adapter_choice: int32 [2, 2, 7], P(None, 'dp'), may hold values from 0 to 7
Outputs:
- outputs: bfloat16 [2, 2, 1024, 2304], P(None, 'dp', 'seq')
- input_gradient: bfloat16 [2, 2, 1024, 2304], P(None, 'dp', 'seq')
- down_gradient: float32 [8, 16, 22784], P(None, None, ('dp', 'seq', 'mp'))
- up_gradient: float32 [8, 16, 27136], P(None, None, ('dp', 'seq', 'mp'))
All inputs are finite; a program needn't handle non-finite values.
Results may differ from a plain program's by a relative error of at most 0.02.
The roundings to bfloat16 on the way count: a program that leaves them out, or rounds other values in their place, can miss the bound.
Values may be sent and summed in bfloat16 or wider, within the bound.
A program may use at most 384 MiB of HBM per device.

v0:
```python
import jax
import jax.numpy as jnp
from jax import lax
from jax.sharding import PartitionSpec as P

MODEL_WIDTH = 2304
QUERY_HEADS_COUNT = 8
KEY_VALUE_HEADS = 4
HEAD_SIZE = 256
FF = 9216


HIGH = lax.Precision.HIGHEST
EPSILON = 1e-06
SOFT_CAP = 50.0
WIDE = jnp.float32
NARROW = jnp.bfloat16


def normalize(value, gain):
    factor = lax.rsqrt(jnp.mean(value * value, axis=-1, keepdims=True) + EPSILON)
    return value * factor * gain


def normalize_back(value, gain, upstream):
    factor = lax.rsqrt(jnp.mean(value * value, axis=-1, keepdims=True) + EPSILON)
    scaled = upstream * gain
    inner = jnp.mean(value * scaled, axis=-1, keepdims=True)
    return factor * scaled - value * (factor * factor * factor) * inner


def angles(positions):
    half = HEAD_SIZE // 2
    rates = 10000.0 ** (-(jnp.arange(half, dtype=WIDE) * 2.0) / HEAD_SIZE)
    turns = positions.astype(WIDE)[:, None] * rates[None, :]
    return (jnp.cos(turns)[:, None, :], jnp.sin(turns)[:, None, :])


def apply_rotation(head_stack, cosine_table, sine_table):
    half = HEAD_SIZE // 2
    first = head_stack[..., :half]
    second = head_stack[..., half:]
    return jnp.concatenate(
        [first * cosine_table - second * sine_table, second * cosine_table + first * sine_table],
        axis=-1,
    )


def rotate_back(grads, cosine_table, sine_table):
    half = HEAD_SIZE // 2
    first = grads[..., :half]
    second = grads[..., half:]
    return jnp.concatenate(
        [first * cosine_table + second * sine_table, second * cosine_table - first * sine_table],
        axis=-1,
    )


def pick(table, index, start_index, size):
    return lax.dynamic_slice(table, (index, 0, start_index), (1, table.shape[1], size))[0]


def deposit(total, index, start_index, piece):
    current = pick(total, index, start_index, piece.shape[1])
    return lax.dynamic_update_slice(total, (current + piece)[None], (index, 0, start_index))


def activate(gate_value, up_value):
    return jax.nn.gelu(gate_value, approximate=True) * up_value


def combine_rows(main_part, inner_part):
    return lax.psum((main_part, inner_part), "mp")


def combine_input(partial_value):
    return lax.psum(partial_value, "mp")


def column_forward(inputs_low, weight, down_part, up_part):
    main = jnp.dot(inputs_low, weight, preferred_element_type=WIDE)
    inner = jnp.einsum("td,rd->tr", inputs_low, down_part, preferred_element_type=WIDE).astype(
        NARROW
    )
    return (main + jnp.dot(inner, up_part, preferred_element_type=WIDE), inner)


def row_forward(inputs_low, weight, down_part, up_part):
    main_part = jnp.dot(inputs_low, weight, preferred_element_type=WIDE)
    inner_part = jnp.einsum("tq,rq->tr", inputs_low, down_part, preferred_element_type=WIDE)
    main, inner = combine_rows(main_part, inner_part)
    inner_low = inner.astype(NARROW)
    return (main + jnp.dot(inner_low, up_part, preferred_element_type=WIDE), inner_low)


def column_back(grad_out, weight, down_part, up_part, inputs_low, inner_low):
    inner_grad = jnp.einsum("to,ro->tr", grad_out, up_part, preferred_element_type=WIDE)
    back = jnp.einsum("to,do->td", grad_out, weight, preferred_element_type=WIDE)
    back = back + jnp.dot(inner_grad, down_part.astype(WIDE), precision=HIGH)
    down_grad = jnp.einsum("tr,td->rd", inner_grad, inputs_low.astype(WIDE), precision=HIGH)
    up_grad = jnp.einsum("tr,to->ro", inner_low, grad_out, preferred_element_type=WIDE)
    return (back, down_grad, up_grad)


def row_back(grad_out, weight, down_part, up_part, inputs_low, inner_low, part, half):
    inner_grad = jnp.einsum("td,rd->tr", grad_out, up_part, preferred_element_type=WIDE)
    back = jnp.einsum("td,qd->tq", grad_out, weight, preferred_element_type=WIDE)
    back = back + jnp.dot(inner_grad, down_part.astype(WIDE), precision=HIGH)
    down_grad = jnp.einsum("tr,tq->rq", inner_grad, inputs_low.astype(WIDE), precision=HIGH)
    own_columns = lax.dynamic_slice_in_dim(grad_out, part * half, half, 1)
    up_grad = jnp.einsum("tr,tc->rc", inner_low, own_columns, preferred_element_type=WIDE)
    return (back, down_grad, up_grad)


def shards(
    inputs,
    cotangent,
    pre_attention,
    post_attention,
    pre_feedforward,
    post_feedforward,
    query_weight,
    key_matrix,
    value_matrix,
    output_weight,
    gate_weight,
    up_weight,
    down_weight,
    adapter_down,
    adapter_up,
    prefix_lengths,
    adapter_choice,
):
    parts = lax.axis_size("mp")
    part = lax.axis_index("mp")
    rows = inputs.shape[2]
    length = rows * lax.axis_size("seq")
    positions = lax.axis_index("seq") * rows + jnp.arange(rows, dtype=jnp.int32)
    key_positions = jnp.arange(length, dtype=jnp.int32)
    cosine_table, sine_table = angles(positions)
    query_width = QUERY_HEADS_COUNT * HEAD_SIZE
    key_span_width = KEY_VALUE_HEADS * HEAD_SIZE
    query_local = query_width // parts
    key_local = key_span_width // parts
    hidden_local = FF // parts
    half = MODEL_WIDTH // parts
    head_groups = QUERY_HEADS_COUNT // KEY_VALUE_HEADS
    query_heads = query_local // HEAD_SIZE
    key_heads = key_local // HEAD_SIZE
    scale = HEAD_SIZE ** (-0.5)
    in_output = 3 * MODEL_WIDTH + part * query_local
    in_gate = 3 * MODEL_WIDTH + query_width
    in_up = 4 * MODEL_WIDTH + query_width
    in_down = 5 * MODEL_WIDTH + query_width + part * hidden_local
    out_query = part * query_local
    out_key = query_width + part * key_local
    out_value = query_width + key_span_width + part * key_local
    out_output = query_width + 2 * key_span_width
    out_gate = query_width + 2 * key_span_width + MODEL_WIDTH + part * hidden_local
    out_up = query_width + 2 * key_span_width + MODEL_WIDTH + FF + part * hidden_local
    out_down = query_width + 2 * key_span_width + MODEL_WIDTH + 2 * FF
    grad_down = jnp.zeros(adapter_down.shape, WIDE)
    grad_up = jnp.zeros(adapter_up.shape, WIDE)
    results = []
    input_grads = []
    for batch in range(inputs.shape[0]):
        first = (
            lax.all_gather(query_weight, ("dp", "seq"), axis=0, tiled=True),
            lax.all_gather(key_matrix, ("dp", "seq"), axis=0, tiled=True),
            lax.all_gather(value_matrix, ("dp", "seq"), axis=0, tiled=True),
            lax.all_gather(output_weight, ("dp", "seq"), axis=1, tiled=True),
            lax.all_gather(gate_weight, ("dp", "seq"), axis=0, tiled=True),
            lax.all_gather(up_weight, ("dp", "seq"), axis=0, tiled=True),
            lax.all_gather(down_weight, ("dp", "seq"), axis=1, tiled=True),
        )
        query_full, key_full, value_full, output_full, gate_full, up_full, down_full = first
        slots = adapter_choice[batch, 0]
        prefix_length = prefix_lengths[batch, 0]
        down_query = pick(adapter_down, slots[0], 0, MODEL_WIDTH)
        down_key = pick(adapter_down, slots[1], MODEL_WIDTH, MODEL_WIDTH)
        down_value = pick(adapter_down, slots[2], 2 * MODEL_WIDTH, MODEL_WIDTH)
        down_output = pick(adapter_down, slots[3], in_output, query_local)
        down_gate = pick(adapter_down, slots[4], in_gate, MODEL_WIDTH)
        down_up = pick(adapter_down, slots[5], in_up, MODEL_WIDTH)
        down_down = pick(adapter_down, slots[6], in_down, hidden_local)
        up_query = pick(adapter_up, slots[0], out_query, query_local)
        up_key = pick(adapter_up, slots[1], out_key, key_local)
        up_value = pick(adapter_up, slots[2], out_value, key_local)
        up_output = pick(adapter_up, slots[3], out_output, MODEL_WIDTH)
        up_gate = pick(adapter_up, slots[4], out_gate, hidden_local)
        up_upper = pick(adapter_up, slots[5], out_up, hidden_local)
        up_down = pick(adapter_up, slots[6], out_down, MODEL_WIDTH)
        source = inputs[batch, 0].astype(WIDE)
        normed = normalize(source, pre_attention).astype(NARROW)
        query, inner_query = column_forward(normed, query_full, down_query, up_query)
        key_rows, inner_key = column_forward(normed, key_full, down_key, up_key)
        value_rows, inner_value = column_forward(normed, value_full, down_value, up_value)
        rotated_query = apply_rotation(
            query.reshape(rows, query_heads, HEAD_SIZE), cosine_table, sine_table
        ).astype(NARROW)
        rotated_keys = (
            apply_rotation(key_rows.reshape(rows, key_heads, HEAD_SIZE), cosine_table, sine_table)
            .astype(NARROW)
            .reshape(rows, key_local)
        )
        values_low = value_rows.astype(NARROW)
        keys_all, values_all = (
            lax.all_gather(rotated_keys, "seq", axis=0, tiled=True),
            lax.all_gather(values_low, "seq", axis=0, tiled=True),
        )
        query_four = rotated_query.reshape(rows, key_heads, head_groups, HEAD_SIZE)
        keys_three = keys_all.reshape(length, key_heads, HEAD_SIZE)
        values_three = values_all.reshape(length, key_heads, HEAD_SIZE)
        visible = (key_positions[None, :] <= positions[:, None]) | (
            key_positions[None, :] < prefix_length
        )
        raw = (
            jnp.einsum("tkgd,skd->kgts", query_four, keys_three, preferred_element_type=WIDE)
            * scale
        )
        masked = jnp.where(visible, SOFT_CAP * jnp.tanh(raw / SOFT_CAP), -1e30)
        top = jnp.max(masked, axis=-1, keepdims=True)
        expo = jnp.exp(masked - top)
        total = jnp.sum(expo, axis=-1, keepdims=True)
        log_total = top + jnp.log(total)
        prob_low = (expo / total).astype(NARROW)
        head_stack = jnp.einsum(
            "kgts,skd->tkgd", prob_low, values_three, preferred_element_type=WIDE
        )
        head_stack = head_stack.reshape(rows, query_local).astype(NARROW)
        attention_out, inner_output = row_forward(head_stack, output_full, down_output, up_output)
        middle = source + normalize(attention_out, post_attention)
        normed_ffw = normalize(middle, pre_feedforward).astype(NARROW)
        gate, inner_gate = column_forward(normed_ffw, gate_full, down_gate, up_gate)
        upper, inner_upper = column_forward(normed_ffw, up_full, down_up, up_upper)
        hidden = activate(gate, upper).astype(NARROW)
        ffw_out, inner_down = row_forward(hidden, down_full, down_down, up_down)
        results.append((middle + normalize(ffw_out, post_feedforward)).astype(NARROW))
        second = (
            lax.all_gather(query_weight, ("dp", "seq"), axis=0, tiled=True),
            lax.all_gather(key_matrix, ("dp", "seq"), axis=0, tiled=True),
            lax.all_gather(value_matrix, ("dp", "seq"), axis=0, tiled=True),
            lax.all_gather(output_weight, ("dp", "seq"), axis=1, tiled=True),
            lax.all_gather(gate_weight, ("dp", "seq"), axis=0, tiled=True),
            lax.all_gather(up_weight, ("dp", "seq"), axis=0, tiled=True),
            lax.all_gather(down_weight, ("dp", "seq"), axis=1, tiled=True),
        )
        query_back, key_back, value_back, output_back, gate_back, up_back, down_back = second
        seed_grad = cotangent[batch, 0].astype(WIDE)
        grad_ffw = normalize_back(ffw_out, post_feedforward, seed_grad).astype(NARROW)
        grad_hidden, piece_down, piece_up = row_back(
            grad_ffw, down_back, down_down, up_down, hidden, inner_down, part, half
        )
        grad_down = deposit(grad_down, slots[6], in_down, piece_down)
        grad_up = deposit(grad_up, slots[6], out_down + part * half, piece_up)
        pull = jax.vjp(activate, gate, upper)[1]
        grad_gate, grad_upper = pull(grad_hidden)
        grad_gate = grad_gate.astype(NARROW)
        grad_upper = grad_upper.astype(NARROW)
        back_gate, piece_down, piece_up = column_back(
            grad_gate, gate_back, down_gate, up_gate, normed_ffw, inner_gate
        )
        grad_down = deposit(grad_down, slots[4], in_gate, piece_down)
        grad_up = deposit(grad_up, slots[4], out_gate, piece_up)
        back_upper, piece_down, piece_up = column_back(
            grad_upper, up_back, down_up, up_upper, normed_ffw, inner_upper
        )
        grad_down = deposit(grad_down, slots[5], in_up, piece_down)
        grad_up = deposit(grad_up, slots[5], out_up, piece_up)
        grad_normed_ffw = combine_input(back_gate + back_upper)
        grad_middle = seed_grad + normalize_back(middle, pre_feedforward, grad_normed_ffw)
        grad_attention = normalize_back(attention_out, post_attention, grad_middle).astype(NARROW)
        grad_heads, piece_down, piece_up = row_back(
            grad_attention,
            output_back,
            down_output,
            up_output,
            head_stack,
            inner_output,
            part,
            half,
        )
        grad_down = deposit(grad_down, slots[3], in_output, piece_down)
        grad_up = deposit(grad_up, slots[3], out_output + part * half, piece_up)
        grad_heads_four = grad_heads.astype(NARROW).reshape(rows, key_heads, head_groups, HEAD_SIZE)
        prob = jnp.exp(masked - log_total)
        grad_prob = jnp.einsum(
            "tkgd,skd->kgts", grad_heads_four, values_three, preferred_element_type=WIDE
        )
        grad_capped = prob * (grad_prob - jnp.sum(prob * grad_prob, axis=-1, keepdims=True))
        bend = jnp.tanh(raw / SOFT_CAP)
        grad_raw = (grad_capped * (1.0 - bend * bend)).astype(NARROW)
        grad_query_rot = (
            jnp.einsum("kgts,skd->tkgd", grad_raw, keys_three, preferred_element_type=WIDE) * scale
        )
        grad_key_part = (
            jnp.einsum("kgts,tkgd->skd", grad_raw, query_four, preferred_element_type=WIDE) * scale
        )
        grad_value_part = jnp.einsum(
            "kgts,tkgd->skd", prob_low, grad_heads_four, preferred_element_type=WIDE
        )
        key_grad, value_grad = (
            lax.psum_scatter(
                grad_key_part.reshape(length, key_local), "seq", scatter_dimension=0, tiled=True
            ),
            lax.psum_scatter(
                grad_value_part.reshape(length, key_local), "seq", scatter_dimension=0, tiled=True
            ),
        )
        grad_query = (
            rotate_back(
                grad_query_rot.reshape(rows, query_heads, HEAD_SIZE), cosine_table, sine_table
            )
            .reshape(rows, query_local)
            .astype(NARROW)
        )
        grad_key = (
            rotate_back(key_grad.reshape(rows, key_heads, HEAD_SIZE), cosine_table, sine_table)
            .reshape(rows, key_local)
            .astype(NARROW)
        )
        grad_value = value_grad.astype(NARROW)
        back_query, piece_down, piece_up = column_back(
            grad_query, query_back, down_query, up_query, normed, inner_query
        )
        grad_down = deposit(grad_down, slots[0], 0, piece_down)
        grad_up = deposit(grad_up, slots[0], out_query, piece_up)
        back_key, piece_down, piece_up = column_back(
            grad_key, key_back, down_key, up_key, normed, inner_key
        )
        grad_down = deposit(grad_down, slots[1], MODEL_WIDTH, piece_down)
        grad_up = deposit(grad_up, slots[1], out_key, piece_up)
        back_value, piece_down, piece_up = column_back(
            grad_value, value_back, down_value, up_value, normed, inner_value
        )
        grad_down = deposit(grad_down, slots[2], 2 * MODEL_WIDTH, piece_down)
        grad_up = deposit(grad_up, slots[2], out_value, piece_up)
        grad_normed = combine_input(back_query + back_key + back_value)
        input_grads.append(
            (grad_middle + normalize_back(source, pre_attention, grad_normed)).astype(NARROW)
        )
    down_total, up_total = (
        lax.psum_scatter(grad_down, ("dp", "seq", "mp"), scatter_dimension=2, tiled=True),
        lax.psum_scatter(grad_up, ("dp", "seq", "mp"), scatter_dimension=2, tiled=True),
    )
    outputs = jnp.stack(results)[:, None]
    input_gradient = jnp.stack(input_grads)[:, None]
    return (outputs, input_gradient, down_total, up_total)


def solution(mesh):
    return jax.shard_map(
        shards,
        mesh=mesh,
        in_specs=(
            P(None, "dp", "seq", None),
            P(None, "dp", "seq", None),
            P(),
            P(),
            P(),
            P(),
            P(("dp", "seq"), "mp"),
            P(("dp", "seq"), "mp"),
            P(("dp", "seq"), "mp"),
            P("mp", ("dp", "seq")),
            P(("dp", "seq"), "mp"),
            P(("dp", "seq"), "mp"),
            P("mp", ("dp", "seq")),
            P(),
            P(),
            P(None, "dp"),
            P(None, "dp", None),
        ),
        out_specs=(
            P(None, "dp", "seq", None),
            P(None, "dp", "seq", None),
            P(None, None, ("dp", "seq", "mp")),
            P(None, None, ("dp", "seq", "mp")),
        ),
        check_vma=False,
    )
```

profile of v0, /device:TPU:0, one launch (start us, length us, event | category | flops | bytes accessed | tf_op | source)
XLA Modules:
  0.0 2112.5 jit_solution(5309520047929277934)
XLA Ops:
  15.9 59.8 %all-gather.12.cloned.1.call-done = bf16[2304,512]{1,0:T(8,128)(2,1)} async-done(((bf16[144,512]{1,0:T(8,128)(2,1)}), bf16[2304,512]{1,0:T(8,128)(2,1)}) %all-gather.12.cloned.1.call-update) | async-done | bytes 2359312 | tf_op jit(solution)/shard_map/all_gather | solution.py:170
  94.7 44.3 %all-gather.16.cloned.1.call-done = bf16[2304,512]{1,0:T(8,128)(2,1)} async-done(((bf16[144,512]{1,0:T(8,128)(2,1)}), bf16[2304,512]{1,0:T(8,128)(2,1)}) %all-gather.16.cloned.1.call-update) | async-done | bytes 2359312 | tf_op jit(solution)/shard_map/all_gather | solution.py:169
  160.2 20.3 all-gather.30.cloned.1.call-done
  182.6 39.4 %all-gather.14.cloned.1.call-done = bf16[1024,512]{1,0:T(8,128)(2,1)} async-done(((bf16[128,512]{1,0:T(8,128)(2,1)}), bf16[1024,512]{1,0:T(8,128)(2,1)}) %all-gather.14.cloned.1.call-update) | async-done | bytes 1048592 | tf_op jit(solution)/shard_map/all_gather | solution.py:209
  224.2 78.8 %all-gather.20.cloned.1.call-done = bf16[2304,1024]{1,0:T(8,128)(2,1)} async-done(((bf16[144,1024]{1,0:T(8,128)(2,1)}), bf16[2304,1024]{1,0:T(8,128)(2,1)}) %all-gather.20.cloned.1.call-update) | async-done | bytes 4718608 | tf_op jit(solution)/shard_map/all_gather | solution.py:168
  315.0 28.6 %all-gather.32.cloned.1.call-done = bf16[1024,512]{0,1:T(8,128)(2,1)} async-done(((bf16[128,512]{0,1:T(8,128)(2,1)}), bf16[1024,512]{0,1:T(8,128)(2,1)}) %all-gather.32.cloned.1.call-update) | async-done | bytes 1048592 | tf_op jit(solution)/shard_map/all_gather | solution.py:208
  346.3 38.4 %all-gather.18.cloned.1.call-done = bf16[1024,512]{0,1:T(8,128)(2,1)} async-done(((bf16[128,512]{0,1:T(8,128)(2,1)}), bf16[1024,512]{0,1:T(8,128)(2,1)}) %all-gather.18.cloned.1.call-update) | async-done | bytes 1048592 | tf_op jit(solution)/shard_map/all_gather | solution.py:208
  391.5 74.7 %all-gather.22.cloned.1.call-done = bf16[1024,2304]{0,1:T(8,128)(2,1)} async-done(((bf16[1024,144]{0,1:T(8,128)(2,1)}), bf16[1024,2304]{0,1:T(8,128)(2,1)}) %all-gather.22.cloned.1.call-update) | async-done | bytes 4718608 | tf_op jit(solution)/shard_map/all_gather | solution.py:171
  505.8 225.9 %all-gather.24.cloned.1.call-done = bf16[2304,4608]{1,0:T(8,128)(2,1)} async-done(((bf16[144,4608]{1,0:T(8,128)(2,1)}), bf16[2304,4608]{1,0:T(8,128)(2,1)}) %all-gather.24.cloned.1.call-update) | async-done | bytes 21233680 | tf_op jit(solution)/shard_map/all_gather | solution.py:172
  752.6 213.2 %all-gather.26.cloned.1.call-done = bf16[2304,4608]{1,0:T(8,128)(2,1)} async-done(((bf16[144,4608]{1,0:T(8,128)(2,1)}), bf16[2304,4608]{1,0:T(8,128)(2,1)}) %all-gather.26.cloned.1.call-update) | async-done | bytes 21233680 | tf_op jit(solution)/shard_map/all_gather | solution.py:173
  989.8 209.9 %all-gather.28.cloned.1.call-done = bf16[4608,2304]{0,1:T(8,128)(2,1)} async-done(((bf16[4608,144]{0,1:T(8,128)(2,1)}), bf16[4608,2304]{0,1:T(8,128)(2,1)}) %all-gather.28.cloned.1.call-update) | async-done | bytes 21233680 | tf_op jit(solution)/shard_map/all_gather | solution.py:174
  1199.7 12.4 fusion.488
  1212.1 12.0 fusion.492
  1252.7 11.5 fusion.498
  1286.9 10.9 fusion.494
  1311.9 10.9 fusion.495
  1339.4 22.9 %all-reduce.17.cloned.1.call-done = (f32[128,2304]{1,0:T(8,128)}, f32[128,2304]{1,0:T(8,128)}) async-done(((f32[128,2304]{1,0:T(8,128)}, f32[128,2304]{1,0:T(8,128)}), (f32[128,2304]{1,0:T(8,128)}, f32[128,2304]{1,0:T(8,128)})) %all-reduce.17.cloned.1.call-update) | async-done | bytes 2359312 | tf_op jit(solution)/shard_map/psum | solution.py:77
  1458.6 66.4 %reduce-scatter.9.cloned.1.call-done = f32[128,512]{0,1:T(8,128)} async-done(((f32[1024,512]{0,1:T(8,128)}), f32[128,512]{0,1:T(8,128)}) %reduce-scatter.9.cloned.1.call-update) | async-done | bytes 262160 | tf_op jit(solution)/shard_map/reduce_scatter | solution.py:303
  1533.9 62.4 %reduce-scatter.11.cloned.1.call-done = f32[128,512]{0,1:T(8,128)} async-done(((f32[1024,512]{0,1:T(8,128)}), f32[128,512]{0,1:T(8,128)}) %reduce-scatter.11.cloned.1.call-update) | async-done | bytes 262160 | tf_op jit(solution)/shard_map/reduce_scatter | solution.py:306
  1605.1 62.5 %reduce-scatter.15.cloned.1.call-done = f32[128,512]{0,1:T(8,128)} async-done(((f32[1024,512]{0,1:T(8,128)}), f32[128,512]{0,1:T(8,128)}) %reduce-scatter.15.cloned.1.call-update) | async-done | bytes 262160 | tf_op jit(solution)/shard_map/reduce_scatter | solution.py:306
  1720.9 51.6 %copy.159 = f32[8,16,27136]{1,0,2:T(8,128)} copy(f32[8,16,27136]{2,1,0:T(8,128)} %fusion.123) | data formatting | bytes 27787264
  1772.5 69.0 %reshape.511 = f32[27136,128]{1,0:T(8,128)} reshape(f32[27136,8,16]{2,1,0:T(8,128)} %bitcast.170) | data formatting | bytes 27787264
  1849.7 90.4 %all-reduce.13.cloned.1.call-done = f32[8,16,22784]{2,1,0:T(8,128)} async-done(((f32[8,16,22784]{2,1,0:T(8,128)}), f32[8,16,22784]{2,1,0:T(8,128)}) %all-reduce.13.cloned.1.call-update) | async-done | bytes 11665424
  1942.0 159.2 %reduce-scatter.17.cloned.1.call-done = f32[848,128]{1,0:T(8,128)} async-done(((f32[27136,128]{1,0:T(8,128)}), f32[848,128]{1,0:T(8,128)}) %reduce-scatter.17.cloned.1.call-update) | async-done | bytes 434192
  (606 shorter events, 394.3 us)
Async XLA Ops:
  7.2 68.5 %all-gather.12.cloned.1.call-start = ((), (), s32[]{:S(2)}) async-start(), calls=%async_computation.5 | async-start | bytes 2506752 | tf_op jit(solution)/shard_map/all_gather | solution.py:170
  7.9 131.1 %all-gather.16.cloned.1.call-start = ((), (), s32[]{:S(2)}) async-start(), calls=%async_computation.7 | async-start | bytes 2506752 | tf_op jit(solution)/shard_map/all_gather | solution.py:169
  8.7 171.8 %all-gather.30.cloned.1.call-start = ((), (), s32[]{:S(2)}) async-start(), calls=%async_computation.14 | async-start | bytes 1179648 | tf_op jit(solution)/shard_map/all_gather | solution.py:209
  79.7 142.3 %all-gather.14.cloned.1.call-start = ((), (), s32[]{:S(2)}) async-start(), calls=%async_computation.6 | async-start | bytes 1179648 | tf_op jit(solution)/shard_map/all_gather | solution.py:209
  85.7 217.3 %all-gather.20.cloned.1.call-start = ((), (), s32[]{:S(2)}) async-start(), calls=%async_computation.9 | async-start | bytes 5013504 | tf_op jit(solution)/shard_map/all_gather | solution.py:168
  86.3 257.3 %all-gather.32.cloned.1.call-start = ((), (), s32[]{:S(2)}) async-start(), calls=%async_computation.15 | async-start | bytes 1179648 | tf_op jit(solution)/shard_map/all_gather | solution.py:208
  149.4 235.2 %all-gather.18.cloned.1.call-start = ((), (), s32[]{:S(2)}) async-start(), calls=%async_computation.8 | async-start | bytes 1179648 | tf_op jit(solution)/shard_map/all_gather | solution.py:208
  150.4 315.7 %all-gather.22.cloned.1.call-start = ((), (), s32[]{:S(2)}) async-start(), calls=%async_computation.10 | async-start | bytes 5013504 | tf_op jit(solution)/shard_map/all_gather | solution.py:171
  151.2 343.6 %all-reduce.21.cloned.1.call-start = ((), (), s32[]{:S(2)}) async-start(), calls=%async_computation.25 | async-start | bytes 4718592 | tf_op jit(solution)/shard_map/psum | solution.py:73
  474.1 257.6 %all-gather.24.cloned.1.call-start = ((), (), s32[]{:S(2)}) async-start(), calls=%async_computation.11 | async-start | bytes 22560768 | tf_op jit(solution)/shard_map/all_gather | solution.py:172
  474.7 491.1 %all-gather.26.cloned.1.call-start = ((), (), s32[]{:S(2)}) async-start(), calls=%async_computation.12 | async-start | bytes 22560768 | tf_op jit(solution)/shard_map/all_gather | solution.py:173
  475.4 724.3 %all-gather.28.cloned.1.call-start = ((), (), s32[]{:S(2)}) async-start(), calls=%async_computation.13 | async-start | bytes 22560768 | tf_op jit(solution)/shard_map/all_gather | solution.py:174
  476.0 768.4 %all-reduce.19.cloned.1.call-start = ((), (), s32[]{:S(2)}) async-start(), calls=%async_computation.24 | async-start | bytes 4718592 | tf_op jit(solution)/shard_map/psum | solution.py:73
  502.3 472.2 %copy-start.103 = (bf16[128,16]{0,1:T(8,128)(2,1)}, bf16[128,16]{0,1:T(8,128)(2,1)S(1)}, u32[]{:S(2)}) copy-start(bf16[128,16]{0,1:T(8,128)(2,1)S(1)} %convolution_convert_fusion.7) | copy-start | bytes 12292
  504.6 480.5 %copy-start.99 = (bf16[128,16]{0,1:T(8,128)(2,1)}, bf16[128,16]{0,1:T(8,128)(2,1)S(1)}, u32[]{:S(2)}) copy-start(bf16[128,16]{0,1:T(8,128)(2,1)S(1)} %convolution_convert_fusion.2) | copy-start | bytes 12292
  1224.2 138.1 %all-reduce.17.cloned.1.call-start = ((), (), s32[]{:S(2)}) async-start(), calls=%async_computation.23 | async-start | bytes 4718592 | tf_op jit(solution)/shard_map/psum | solution.py:77
  1339.1 114.6 %reduce-scatter.13.cloned.1.call-start = ((), (), s32[]{:S(2)}) async-start(), calls=%async_computation.18 | async-start | bytes 2359296 | tf_op jit(solution)/shard_map/reduce_scatter | solution.py:303
  1383.4 141.6 %reduce-scatter.9.cloned.1.call-start = ((), (), s32[]{:S(2)}) async-start(), calls=%async_computation.16 | async-start | bytes 2359296 | tf_op jit(solution)/shard_map/reduce_scatter | solution.py:303
  1400.1 196.3 %reduce-scatter.11.cloned.1.call-start = ((), (), s32[]{:S(2)}) async-start(), calls=%async_computation.17 | async-start | bytes 2359296 | tf_op jit(solution)/shard_map/reduce_scatter | solution.py:306
  1408.4 259.3 %reduce-scatter.15.cloned.1.call-start = ((), (), s32[]{:S(2)}) async-start(), calls=%async_computation.19 | async-start | bytes 2359296 | tf_op jit(solution)/shard_map/reduce_scatter | solution.py:306
  1436.4 250.2 %copy-start.46 = (bf16[16,8,4,256]{3,1,2,0:T(8,128)(2,1)}, bf16[16,8,4,256]{3,1,2,0:T(8,128)(2,1)S(1)}, u32[]{:S(2)}) copy-start(bf16[16,8,4,256]{3,1,2,0:T(8,128)(2,1)S(1)} %copy.173) | copy-start | bytes 786436
  1439.3 404.6 %all-reduce.15.cloned.1.call-start = ((), (), s32[]{:S(2)}) async-start(), calls=%async_computation.22 | async-start | bytes 4718592 | tf_op jit(solution)/shard_map/psum | solution.py:77
  1689.4 250.7 %all-reduce.13.cloned.1.call-start = ((), (), s32[]{:S(2)}) async-start(), calls=%async_computation.21 | async-start | bytes 23330816
  1699.8 401.5 %reduce-scatter.17.cloned.1.call-start = ((), (), s32[]{:S(2)}) async-start(), calls=%async_computation.20 | async-start | bytes 14327808
  (160 other events, 3072.2 us)
Sparse Core Ops, SparseCore 0:
  10.7 65.0 all-gather.11
  78.4 60.6 all-gather.15
  141.8 38.6 all-gather.29
  183.0 38.9 all-gather.13
  224.6 78.4 all-gather.19
  305.5 38.0 all-gather.31
  346.2 38.3 all-gather.17
  387.4 78.7 all-gather.21
  474.2 20.4 all-reduce.20
  497.3 234.3 all-gather.23
  734.4 231.3 all-gather.25
  968.3 231.3 all-gather.27
  1224.3 20.0 all-reduce.18
  1339.2 23.0 all-reduce.16
  1383.6 70.0 reduce-scatter.12
  1457.1 67.9 reduce-scatter.8
  1528.4 67.9 reduce-scatter.10
  1599.7 67.9 reduce-scatter.14
  1689.5 20.8 all-reduce.14
  1716.6 223.4 all-reduce.12
  1942.4 158.7 reduce-scatter.16
where the time goes:
time: 2120 us; the launch traced here: 2110 us
  waiting for transfers between devices  1520 us (72%)
  matrix products  314 us (15%)
  local copies, waits for them, and re-layouts  200 us (9%)
  between operations  42.7 us (2%)
  other arithmetic  29.3 us (1%)
    unnamed x23, waiting for transfers between devices  254 us
    all_gather x1, waiting for transfers between devices, shards(): lax.all_gather(gate_weight, ('dp', 'seq'), axis=0, tiled=True)  226 us
    all_gather x1, waiting for transfers between devices, shards(): lax.all_gather(up_weight, ('dp', 'seq'), axis=0, tiled=True)  213 us
    all_gather x1, waiting for transfers between devices, shards(): lax.all_gather(down_weight, ('dp', 'seq'), axis=1, tiled=True)  210 us
    unnamed x343, local copies, waits for them, and re-layouts  147 us
    reduce_scatter x2, waiting for transfers between devices, shards(): lax.psum_scatter(grad_value_part.reshape(length, key_local), 'seq', scatt...  125 us
    all_gather x1, waiting for transfers between devices, shards(): lax.all_gather(query_weight, ('dp', 'seq'), axis=0, tiled=True)  78.8 us
    all_gather x1, waiting for transfers between devices, shards(): lax.all_gather(output_weight, ('dp', 'seq'), axis=1, tiled=True)  74.7 us
  transfers between devices with their start and end apart: 21, of which 20 were waited for; matrix products, arithmetic and copies ran while one was open for 17% of the time, Pallas kernels for 0%

commit v1 on v0

--- a/solution.py
+++ b/solution.py
@@ -60,9 +60,45 @@
     return lax.dynamic_slice(table, (index, 0, start_index), (1, table.shape[1], size))[0]
 
 
-def deposit(total, index, start_index, piece):
-    current = pick(total, index, start_index, piece.shape[1])
-    return lax.dynamic_update_slice(total, (current + piece)[None], (index, 0, start_index))
+def deposit(total, start_index, piece):
+    return lax.dynamic_update_slice(total, piece, (0, start_index))
+
+
+def segment_of(columns, widths):
+    bounds = []
+    edge = 0
+    for width in widths[:-1]:
+        edge += width
+        bounds.append(edge)
+    seg = jnp.zeros(columns.shape, jnp.int32)
+    for edge in bounds:
+        seg = seg + (columns >= edge).astype(jnp.int32)
+    return seg
+
+
+def spread(compact, choices, widths, adapters):
+    flat = lax.axis_index(("dp", "seq", "mp"))
+    cols = compact.shape[-1]
+    columns = flat * cols + jnp.arange(cols, dtype=jnp.int32)
+    seg = segment_of(columns, widths)
+    chosen = jnp.take_along_axis(
+        choices[:, :, None, :], jnp.broadcast_to(seg[None, None, :, None], choices.shape[:2] + (cols, 1)), axis=3
+    )[..., 0]
+    hits = chosen[None] == jnp.arange(adapters, dtype=jnp.int32)[:, None, None, None]
+    picked = jnp.where(hits[:, :, None], compact[None], 0.0)
+    return jnp.sum(picked, axis=(1, 3))
+
+
+def settle(compact, choices, widths, adapters):
+    mbs, rows, cols = compact.shape
+    groups = lax.axis_size("dp")
+    inner = lax.axis_size("seq") * lax.axis_size("mp")
+    chunk = cols // (groups * inner)
+    arranged = compact.reshape(mbs, rows, groups, inner, chunk)
+    reduced = lax.psum_scatter(arranged, ("seq", "mp"), scatter_dimension=3, tiled=True)
+    reduced = reduced.reshape(mbs, rows, groups, chunk)
+    swapped = lax.all_to_all(reduced, "dp", 2, 2, tiled=True)
+    return spread(swapped, choices, widths, adapters)
 
 
 def activate(gate_value, up_value):
@@ -159,8 +195,8 @@
     out_gate = query_width + 2 * key_span_width + MODEL_WIDTH + part * hidden_local
     out_up = query_width + 2 * key_span_width + MODEL_WIDTH + FF + part * hidden_local
     out_down = query_width + 2 * key_span_width + MODEL_WIDTH + 2 * FF
-    grad_down = jnp.zeros(adapter_down.shape, WIDE)
-    grad_up = jnp.zeros(adapter_up.shape, WIDE)
+    down_list = []
+    up_list = []
     results = []
     input_grads = []
     for batch in range(inputs.shape[0]):
@@ -204,10 +240,8 @@
             .reshape(rows, key_local)
         )
         values_low = value_rows.astype(NARROW)
-        keys_all, values_all = (
-            lax.all_gather(rotated_keys, "seq", axis=0, tiled=True),
-            lax.all_gather(values_low, "seq", axis=0, tiled=True),
-        )
+        both_all = lax.all_gather(jnp.stack([rotated_keys, values_low]), "seq", axis=1, tiled=True)
+        keys_all, values_all = both_all[0], both_all[1]
         query_four = rotated_query.reshape(rows, key_heads, head_groups, HEAD_SIZE)
         keys_three = keys_all.reshape(length, key_heads, HEAD_SIZE)
         values_three = values_all.reshape(length, key_heads, HEAD_SIZE)
@@ -246,13 +280,15 @@
             lax.all_gather(down_weight, ("dp", "seq"), axis=1, tiled=True),
         )
         query_back, key_back, value_back, output_back, gate_back, up_back, down_back = second
+        grad_down = jnp.zeros(adapter_down.shape[1:], WIDE)
+        grad_up = jnp.zeros(adapter_up.shape[1:], WIDE)
         seed_grad = cotangent[batch, 0].astype(WIDE)
         grad_ffw = normalize_back(ffw_out, post_feedforward, seed_grad).astype(NARROW)
         grad_hidden, piece_down, piece_up = row_back(
             grad_ffw, down_back, down_down, up_down, hidden, inner_down, part, half
         )
-        grad_down = deposit(grad_down, slots[6], in_down, piece_down)
-        grad_up = deposit(grad_up, slots[6], out_down + part * half, piece_up)
+        grad_down = deposit(grad_down, in_down, piece_down)
+        grad_up = deposit(grad_up, out_down + part * half, piece_up)
         pull = jax.vjp(activate, gate, upper)[1]
         grad_gate, grad_upper = pull(grad_hidden)
         grad_gate = grad_gate.astype(NARROW)
@@ -260,13 +296,13 @@
         back_gate, piece_down, piece_up = column_back(
             grad_gate, gate_back, down_gate, up_gate, normed_ffw, inner_gate
         )
-        grad_down = deposit(grad_down, slots[4], in_gate, piece_down)
-        grad_up = deposit(grad_up, slots[4], out_gate, piece_up)
+        grad_down = deposit(grad_down, in_gate, piece_down)
+        grad_up = deposit(grad_up, out_gate, piece_up)
         back_upper, piece_down, piece_up = column_back(
             grad_upper, up_back, down_up, up_upper, normed_ffw, inner_upper
         )
-        grad_down = deposit(grad_down, slots[5], in_up, piece_down)
-        grad_up = deposit(grad_up, slots[5], out_up, piece_up)
+        grad_down = deposit(grad_down, in_up, piece_down)
+        grad_up = deposit(grad_up, out_up, piece_up)
         grad_normed_ffw = combine_input(back_gate + back_upper)
         grad_middle = seed_grad + normalize_back(middle, pre_feedforward, grad_normed_ffw)
         grad_attention = normalize_back(attention_out, post_attention, grad_middle).astype(NARROW)
@@ -280,8 +316,8 @@
             part,
             half,
         )
-        grad_down = deposit(grad_down, slots[3], in_output, piece_down)
-        grad_up = deposit(grad_up, slots[3], out_output + part * half, piece_up)
+        grad_down = deposit(grad_down, in_output, piece_down)
+        grad_up = deposit(grad_up, out_output + part * half, piece_up)
         grad_heads_four = grad_heads.astype(NARROW).reshape(rows, key_heads, head_groups, HEAD_SIZE)
         prob = jnp.exp(masked - log_total)
         grad_prob = jnp.einsum(
@@ -299,14 +335,13 @@
         grad_value_part = jnp.einsum(
             "kgts,tkgd->skd", prob_low, grad_heads_four, preferred_element_type=WIDE
         )
-        key_grad, value_grad = (
-            lax.psum_scatter(
-                grad_key_part.reshape(length, key_local), "seq", scatter_dimension=0, tiled=True
-            ),
-            lax.psum_scatter(
-                grad_value_part.reshape(length, key_local), "seq", scatter_dimension=0, tiled=True
-            ),
-        )
+        both_grad = lax.psum_scatter(
+            jnp.stack([grad_key_part.reshape(length, key_local), grad_value_part.reshape(length, key_local)]),
+            "seq",
+            scatter_dimension=1,
+            tiled=True,
+        )
+        key_grad, value_grad = both_grad[0], both_grad[1]
         grad_query = (
             rotate_back(
                 grad_query_rot.reshape(rows, query_heads, HEAD_SIZE), cosine_table, sine_table
@@ -323,26 +358,29 @@
         back_query, piece_down, piece_up = column_back(
             grad_query, query_back, down_query, up_query, normed, inner_query
         )
-        grad_down = deposit(grad_down, slots[0], 0, piece_down)
-        grad_up = deposit(grad_up, slots[0], out_query, piece_up)
+        grad_down = deposit(grad_down, 0, piece_down)
+        grad_up = deposit(grad_up, out_query, piece_up)
         back_key, piece_down, piece_up = column_back(
             grad_key, key_back, down_key, up_key, normed, inner_key
         )
-        grad_down = deposit(grad_down, slots[1], MODEL_WIDTH, piece_down)
-        grad_up = deposit(grad_up, slots[1], out_key, piece_up)
+        grad_down = deposit(grad_down, MODEL_WIDTH, piece_down)
+        grad_up = deposit(grad_up, out_key, piece_up)
         back_value, piece_down, piece_up = column_back(
             grad_value, value_back, down_value, up_value, normed, inner_value
         )
-        grad_down = deposit(grad_down, slots[2], 2 * MODEL_WIDTH, piece_down)
-        grad_up = deposit(grad_up, slots[2], out_value, piece_up)
+        grad_down = deposit(grad_down, 2 * MODEL_WIDTH, piece_down)
+        grad_up = deposit(grad_up, out_value, piece_up)
         grad_normed = combine_input(back_query + back_key + back_value)
+        down_list.append(grad_down)
+        up_list.append(grad_up)
         input_grads.append(
             (grad_middle + normalize_back(source, pre_attention, grad_normed)).astype(NARROW)
         )
-    down_total, up_total = (
-        lax.psum_scatter(grad_down, ("dp", "seq", "mp"), scatter_dimension=2, tiled=True),
-        lax.psum_scatter(grad_up, ("dp", "seq", "mp"), scatter_dimension=2, tiled=True),
-    )
+    choices = lax.all_gather(adapter_choice[:, 0], "dp", axis=1, tiled=False)
+    down_widths = (MODEL_WIDTH, MODEL_WIDTH, MODEL_WIDTH, query_width, MODEL_WIDTH, MODEL_WIDTH, FF)
+    up_widths = (query_width, key_span_width, key_span_width, MODEL_WIDTH, FF, FF, MODEL_WIDTH)
+    down_total = settle(jnp.stack(down_list), choices, down_widths, adapter_down.shape[0])
+    up_total = settle(jnp.stack(up_list), choices, up_widths, adapter_up.shape[0])
     outputs = jnp.stack(results)[:, None]
     input_gradient = jnp.stack(input_grads)[:, None]
     return (outputs, input_gradient, down_total, up_total)

time: 2120 us -> 1730 us (0.82)
  waiting for transfers between devices: 1520 us -> 1150 us
  local copies, waits for them, and re-layouts: 200 us -> 149 us
  other arithmetic: 29.3 us -> 52.8 us
    unnamed x23 -> x17, waiting for transfers between devices: 254 us -> 4.51 us
    unnamed x343 -> x332, local copies, waits for them, and re-layouts: 147 us -> 17.9 us
    gather x0 -> x6, local copies, waits for them, and re-layouts: none -> 71.3 us  [spread(): jnp.take_along_axis(choices[:, :, None, :], jnp.broadcast_to(seg[None, No...]
    all_gather x4 -> x2, waiting for transfers between devices: 127 us -> 71.2 us  [shards(): lax.all_gather(jnp.stack([rotated_keys, values_low]), 'seq', axis=1, tile...]
    reduce_scatter x4, waiting for transfers between devices: 196 us -> 152 us  [the longest x2 113 us: shards(): lax.psum_scatter(jnp.stack([grad_key_part.reshape(length, key_local), gra...]
    dynamic_slice x26 -> x0, local copies, waits for them, and re-layouts: 24.3 us -> none  [pick(): lax.dynamic_slice(table, (index, 0, start_index), (1, table.shape[1], size))]
    reshape x2 -> x6, local copies, waits for them, and re-layouts: 4.33 us -> 26.6 us  [the longest x4 23.3 us: settle(): arranged = compact.reshape(mbs, rows, groups, inner, chunk)]
  transfers between devices with their start and end apart: 21 -> 19, of which waited for: 20 -> 16; matrix products, arithmetic and copies ran while one was open for 17% -> 18% of each run, Pallas kernels for 0% -> 0%
where the time goes in v1:
time: 1730 us; the launch traced here: 1720 us
  waiting for transfers between devices  1150 us (66%)
  matrix products  309 us (18%)
  local copies, waits for them, and re-layouts  149 us (9%)
  other arithmetic  52.8 us (3%)
  between operations  42.6 us (2%)
    all_gather x1, waiting for transfers between devices, shards(): lax.all_gather(gate_weight, ('dp', 'seq'), axis=0, tiled=True)  226 us
    all_gather x1, waiting for transfers between devices, shards(): lax.all_gather(up_weight, ('dp', 'seq'), axis=0, tiled=True)  213 us
    all_gather x1, waiting for transfers between devices, shards(): lax.all_gather(down_weight, ('dp', 'seq'), axis=1, tiled=True)  210 us
    reduce_scatter x2, waiting for transfers between devices, shards(): lax.psum_scatter(jnp.stack([grad_key_part.reshape(length, key_local), gra...  113 us
    all_gather x1, waiting for transfers between devices, shards(): lax.all_gather(query_weight, ('dp', 'seq'), axis=0, tiled=True)  72.6 us
    gather x6, local copies, waits for them, and re-layouts, spread(): jnp.take_along_axis(choices[:, :, None, :], jnp.broadcast_to(seg[None, No...  71.3 us
    all_gather x2, waiting for transfers between devices, shards(): lax.all_gather(jnp.stack([rotated_keys, values_low]), 'seq', axis=1, tile...  71.2 us
    all_gather x1, waiting for transfers between devices, shards(): lax.all_gather(output_weight, ('dp', 'seq'), axis=1, tiled=True)  57.1 us
  transfers between devices with their start and end apart: 19, of which 16 were waited for; matrix products, arithmetic and copies ran while one was open for 18% of the time, Pallas kernels for 0%

profile of v1, /device:TPU:0, one launch (start us, length us, event | category | flops | bytes accessed | tf_op | source)
XLA Modules:
  0.0 1719.3 jit_solution(1575235428574747468)
XLA Ops:
  25.1 50.7 %all-gather.10.cloned.1.call-done = bf16[2304,512]{1,0:T(8,128)(2,1)} async-done(((bf16[144,512]{1,0:T(8,128)(2,1)}), bf16[2304,512]{1,0:T(8,128)(2,1)}) %all-gather.10.cloned.1.call-update) | async-done | bytes 2359312 | tf_op jit(solution)/shard_map/all_gather | solution.py:205
  86.7 52.4 %all-gather.12.cloned.1.call-done = bf16[2304,512]{1,0:T(8,128)(2,1)} async-done(((bf16[144,512]{1,0:T(8,128)(2,1)}), bf16[2304,512]{1,0:T(8,128)(2,1)}) %all-gather.12.cloned.1.call-update) | async-done | bytes 2359312 | tf_op jit(solution)/shard_map/all_gather | solution.py:206
  162.9 28.0 %all-gather.26.cloned.1.call-done = bf16[2,1024,512]{2,1,0:T(8,128)(2,1)} async-done(((bf16[2,128,512]{2,1,0:T(8,128)(2,1)}), bf16[2,1024,512]{2,1,0:T(8,128)(2,1)}) %all-gather.26.cloned.1.call-update) | async-done | bytes 2097168 | tf_op jit(solution)/shard_map/all_gather | solution.py:243
  197.9 43.2 %all-gather.14.cloned.1.call-done = bf16[2,1024,512]{2,1,0:T(8,128)(2,1)} async-done(((bf16[2,128,512]{2,1,0:T(8,128)(2,1)}), bf16[2,1024,512]{2,1,0:T(8,128)(2,1)}) %all-gather.14.cloned.1.call-update) | async-done | bytes 2097168 | tf_op jit(solution)/shard_map/all_gather | solution.py:243
  249.3 72.6 %all-gather.16.cloned.1.call-done = bf16[2304,1024]{1,0:T(8,128)(2,1)} async-done(((bf16[144,1024]{1,0:T(8,128)(2,1)}), bf16[2304,1024]{1,0:T(8,128)(2,1)}) %all-gather.16.cloned.1.call-update) | async-done | bytes 4718608 | tf_op jit(solution)/shard_map/all_gather | solution.py:204
  345.8 57.1 %all-gather.18.cloned.1.call-done = bf16[1024,2304]{0,1:T(8,128)(2,1)} async-done(((bf16[1024,144]{0,1:T(8,128)(2,1)}), bf16[1024,2304]{0,1:T(8,128)(2,1)}) %all-gather.18.cloned.1.call-update) | async-done | bytes 4718608 | tf_op jit(solution)/shard_map/all_gather | solution.py:207
  442.9 225.6 %all-gather.20.cloned.1.call-done = bf16[2304,4608]{1,0:T(8,128)(2,1)} async-done(((bf16[144,4608]{1,0:T(8,128)(2,1)}), bf16[2304,4608]{1,0:T(8,128)(2,1)}) %all-gather.20.cloned.1.call-update) | async-done | bytes 21233680 | tf_op jit(solution)/shard_map/all_gather | solution.py:208
  668.5 8.8 fusion.488
  689.4 213.2 %all-gather.22.cloned.1.call-done = bf16[2304,4608]{1,0:T(8,128)(2,1)} async-done(((bf16[144,4608]{1,0:T(8,128)(2,1)}), bf16[2304,4608]{1,0:T(8,128)(2,1)}) %all-gather.22.cloned.1.call-update) | async-done | bytes 21233680 | tf_op jit(solution)/shard_map/all_gather | solution.py:209
  926.7 209.9 %all-gather.24.cloned.1.call-done = bf16[4608,2304]{0,1:T(8,128)(2,1)} async-done(((bf16[4608,144]{0,1:T(8,128)(2,1)}), bf16[4608,2304]{0,1:T(8,128)(2,1)}) %all-gather.24.cloned.1.call-update) | async-done | bytes 21233680 | tf_op jit(solution)/shard_map/all_gather | solution.py:210
  1136.6 12.2 fusion.490
  1148.8 12.1 fusion.486
  1171.7 9.4 all-reduce.15.cloned.1.call-done
  1188.2 11.5 fusion.496
  1223.8 10.9 fusion.497
  1236.3 10.9 fusion.492
  1248.8 10.9 fusion.498
  1262.4 10.9 fusion.493
  1277.2 21.9 %all-reduce.13.cloned.1.call-done = (f32[128,2304]{1,0:T(8,128)}, f32[128,2304]{1,0:T(8,128)}) async-done(((f32[128,2304]{1,0:T(8,128)}, f32[128,2304]{1,0:T(8,128)}), (f32[128,2304]{1,0:T(8,128)}, f32[128,2304]{1,0:T(8,128)})) %all-reduce.13.cloned.1.call-update) | async-done | bytes 2359312 | tf_op jit(solution)/shard_map/psum | solution.py:113
  1392.2 24.8 %reduce-scatter.7.cloned.1.call-done = f32[2,128,512]{1,2,0:T(8,128)} async-done(((f32[2,1024,512]{1,2,0:T(8,128)}), f32[2,128,512]{1,2,0:T(8,128)}) %reduce-scatter.7.cloned.1.call-update) | async-done | bytes 524304 | tf_op jit(solution)/shard_map/reduce_scatter | solution.py:338
  1420.7 88.1 %reduce-scatter.5.cloned.1.call-done = f32[2,128,512]{1,2,0:T(8,128)} async-done(((f32[2,1024,512]{1,2,0:T(8,128)}), f32[2,128,512]{1,2,0:T(8,128)}) %reduce-scatter.5.cloned.1.call-update) | async-done | bytes 524304 | tf_op jit(solution)/shard_map/reduce_scatter | solution.py:338
  1578.9 39.7 %gather_fusion = s32[2848]{0:T(1024)S(1)} fusion(s32[2,2,7]{2,0,1:T(2,128)S(1)} %all_gather.29, s32[2848]{0:T(1024)S(1)} %reshape.673), kind=kCustom, calls=%fused_computation | custom fusion | bytes 56960 | tf_op jit(solution)/shard_map/jit(take_along_axis)/gather | solution.py:84
  1618.9 31.3 %gather_fusion.1 = s32[3392]{0:T(1024)S(1)} fusion(s32[2,2,7]{2,0,1:T(2,128)S(1)} %all_gather.29, s32[3392]{0:T(1024)S(1)} %reshape.681), kind=kCustom, calls=%fused_computation.1 | custom fusion | bytes 67840 | tf_op jit(solution)/shard_map/jit(take_along_axis)/gather | solution.py:84
  1662.6 38.9 %reduce-scatter.11.cloned.1.call-done = f32[2,16,2,1,848]{4,1,2,0,3:T(8,128)} async-done(((f32[2,16,2,16,848]{4,1,2,0,3:T(8,128)}), f32[2,16,2,1,848]{4,1,2,0,3:T(8,128)}) %reduce-scatter.11.cloned.1.call-update) | async-done | bytes 217104 | tf_op jit(solution)/shard_map/reduce_scatter | solution.py:98
  (607 shorter events, 381.5 us)
Async XLA Ops:
  7.2 68.6 %all-gather.10.cloned.1.call-start = ((), (), s32[]{:S(2)}) async-start(), calls=%async_computation.6 | async-start | bytes 2506752 | tf_op jit(solution)/shard_map/all_gather | solution.py:205
  7.9 131.2 %all-gather.12.cloned.1.call-start = ((), (), s32[]{:S(2)}) async-start(), calls=%async_computation.7 | async-start | bytes 2506752 | tf_op jit(solution)/shard_map/all_gather | solution.py:206
  8.7 182.2 %all-gather.26.cloned.1.call-start = ((), (), s32[]{:S(2)}) async-start(), calls=%async_computation.14 | async-start | bytes 2359296 | tf_op jit(solution)/shard_map/all_gather | solution.py:243
  143.2 97.9 %all-gather.14.cloned.1.call-start = ((), (), s32[]{:S(2)}) async-start(), calls=%async_computation.8 | async-start | bytes 2359296 | tf_op jit(solution)/shard_map/all_gather | solution.py:243
  152.7 169.3 %all-gather.16.cloned.1.call-start = ((), (), s32[]{:S(2)}) async-start(), calls=%async_computation.9 | async-start | bytes 5013504 | tf_op jit(solution)/shard_map/all_gather | solution.py:204
  153.3 249.6 %all-gather.18.cloned.1.call-start = ((), (), s32[]{:S(2)}) async-start(), calls=%async_computation.10 | async-start | bytes 5013504 | tf_op jit(solution)/shard_map/all_gather | solution.py:207
  153.8 277.6 %all-reduce.17.cloned.1.call-start = ((), (), s32[]{:S(2)}) async-start(), calls=%async_computation.22 | async-start | bytes 4718592 | tf_op jit(solution)/shard_map/psum | solution.py:109
  160.4 181.8 %copy-start.63 = (pred[128,1024]{0,1:T(8,128)(4,1)}, pred[128,1024]{0,1:T(8,128)(4,1)S(1)}, u32[]{:S(2)}) copy-start(pred[128,1024]{0,1:T(8,128)(4,1)S(1)} %get-tuple-element.141) | copy-start | bytes 393220
  161.6 163.5 %copy-start.115 = (bf16[128,16]{0,1:T(8,128)(2,1)}, bf16[128,16]{0,1:T(8,128)(2,1)S(1)}, u32[]{:S(2)}) copy-start(bf16[128,16]{0,1:T(8,128)(2,1)S(1)} %convolution_convert_fusion.9) | copy-start | bytes 12292
  162.9 169.4 %copy-start.117 = (bf16[128,16]{0,1:T(8,128)(2,1)}, bf16[128,16]{0,1:T(8,128)(2,1)S(1)}, u32[]{:S(2)}) copy-start(bf16[128,16]{0,1:T(8,128)(2,1)S(1)} %convolution_convert_fusion.4) | copy-start | bytes 12292
  410.8 257.7 %all-gather.20.cloned.1.call-start = ((), (), s32[]{:S(2)}) async-start(), calls=%async_computation.11 | async-start | bytes 22560768 | tf_op jit(solution)/shard_map/all_gather | solution.py:208
  411.6 491.1 %all-gather.22.cloned.1.call-start = ((), (), s32[]{:S(2)}) async-start(), calls=%async_computation.12 | async-start | bytes 22560768 | tf_op jit(solution)/shard_map/all_gather | solution.py:209
  412.3 724.3 %all-gather.24.cloned.1.call-start = ((), (), s32[]{:S(2)}) async-start(), calls=%async_computation.13 | async-start | bytes 22560768 | tf_op jit(solution)/shard_map/all_gather | solution.py:210
  412.9 768.2 %all-reduce.15.cloned.1.call-start = ((), (), s32[]{:S(2)}) async-start(), calls=%async_computation.21 | async-start | bytes 4718592 | tf_op jit(solution)/shard_map/psum | solution.py:109
  439.4 237.9 %copy-start.89 = (bf16[128,16]{0,1:T(8,128)(2,1)}, bf16[128,16]{0,1:T(8,128)(2,1)S(1)}, u32[]{:S(2)}) copy-start(bf16[128,16]{0,1:T(8,128)(2,1)S(1)} %convolution_convert_fusion.3) | copy-start | bytes 12292
  441.8 244.8 %copy-start.87 = (bf16[128,16]{0,1:T(8,128)(2,1)}, bf16[128,16]{0,1:T(8,128)(2,1)S(1)}, u32[]{:S(2)}) copy-start(bf16[128,16]{0,1:T(8,128)(2,1)S(1)} %convolution_convert_fusion.8) | copy-start | bytes 12292
  1160.9 138.3 %all-reduce.13.cloned.1.call-start = ((), (), s32[]{:S(2)}) async-start(), calls=%async_computation.20 | async-start | bytes 4718592 | tf_op jit(solution)/shard_map/psum | solution.py:113
  1276.0 141.0 %reduce-scatter.7.cloned.1.call-start = ((), (), s32[]{:S(2)}) async-start(), calls=%async_computation.16 | async-start | bytes 4718592 | tf_op jit(solution)/shard_map/reduce_scatter | solution.py:338
  1327.0 181.9 %reduce-scatter.5.cloned.1.call-start = ((), (), s32[]{:S(2)}) async-start(), calls=%async_computation.15 | async-start | bytes 4718592 | tf_op jit(solution)/shard_map/reduce_scatter | solution.py:338
  1347.6 304.0 %all-reduce.11.cloned.1.call-start = ((), (), s32[]{:S(2)}) async-start(), calls=%async_computation.19 | async-start | bytes 4718592 | tf_op jit(solution)/shard_map/psum | solution.py:113
  1537.5 119.0 %reduce-scatter.9.cloned.1.call-start = ((), (), s32[]{:S(2)}) async-start(), calls=%async_computation.17 | async-start | bytes 3342336 | tf_op jit(solution)/shard_map/reduce_scatter | solution.py:98
  1552.6 148.8 %reduce-scatter.11.cloned.1.call-start = ((), (), s32[]{:S(2)}) async-start(), calls=%async_computation.18 | async-start | bytes 3899392 | tf_op jit(solution)/shard_map/reduce_scatter | solution.py:98
  1658.0 45.1 %all-to-all-start = ((f32[2,16,2,712]{3,1,0,2:T(8,128)}), f32[2,16,2,712]{3,1,0,2:T(8,128)S(1)}, u32[]{:S(2)}, u32[]{:S(2)}) async-start(f32[2,16,2,712]{3,1,0,2:T(8,128)} %copy.205), calls=%async_computation.3 | async-start | bytes 393216 | tf_op jit(solution)/shard_map/all_to_all | solution.py:100
  1703.1 8.4 all-to-all-start.1
  (154 other events, 1504.6 us)
Sparse Core Ops, SparseCore 0:
  10.7 65.0 all-gather.9
  78.5 60.5 all-gather.11
  143.4 47.4 all-gather.25
  193.5 47.5 all-gather.13
  243.6 78.2 all-gather.15
  324.5 78.3 all-gather.17
  410.9 20.4 all-reduce.16
  434.1 234.3 all-gather.19
  671.2 231.3 all-gather.21
  905.2 231.3 all-gather.23
  1161.0 20.0 all-reduce.14
  1276.1 23.0 all-reduce.12
  1327.1 89.8 reduce-scatter.6
  1420.5 88.3 reduce-scatter.4
  1537.6 21.4 all-reduce.10
  1562.8 67.4 reduce-scatter.8
  1634.0 67.4 reduce-scatter.10

commit v2 on v0

v2 whole, which is shorter than its diff:
```python
import jax
import jax.numpy as jnp
from jax import lax
from jax.sharding import PartitionSpec as P

MODEL_WIDTH = 2304
QUERY_HEADS_COUNT = 8
KEY_VALUE_HEADS = 4
HEAD_SIZE = 256
FF = 9216


HIGH = lax.Precision.HIGHEST
EPSILON = 1e-06
SOFT_CAP = 50.0
WIDE = jnp.float32
NARROW = jnp.bfloat16


def normalize(value, gain):
    factor = lax.rsqrt(jnp.mean(value * value, axis=-1, keepdims=True) + EPSILON)
    return value * factor * gain


def normalize_back(value, gain, upstream):
    factor = lax.rsqrt(jnp.mean(value * value, axis=-1, keepdims=True) + EPSILON)
    scaled = upstream * gain
    inner = jnp.mean(value * scaled, axis=-1, keepdims=True)
    return factor * scaled - value * (factor * factor * factor) * inner


def angles(positions):
    half = HEAD_SIZE // 2
    rates = 10000.0 ** (-(jnp.arange(half, dtype=WIDE) * 2.0) / HEAD_SIZE)
    turns = positions.astype(WIDE)[:, None] * rates[None, :]
    return (jnp.cos(turns)[:, None, :], jnp.sin(turns)[:, None, :])


def apply_rotation(head_stack, cosine_table, sine_table):
    half = HEAD_SIZE // 2
    first = head_stack[..., :half]
    second = head_stack[..., half:]
    return jnp.concatenate(
        [first * cosine_table - second * sine_table, second * cosine_table + first * sine_table],
        axis=-1,
    )


def rotate_back(grads, cosine_table, sine_table):
    half = HEAD_SIZE // 2
    first = grads[..., :half]
    second = grads[..., half:]
    return jnp.concatenate(
        [first * cosine_table + second * sine_table, second * cosine_table - first * sine_table],
        axis=-1,
    )


def pick(table, index, start_index, size):
    return lax.dynamic_slice(table, (index, 0, start_index), (1, table.shape[1], size))[0]


def picks(table, slots, start_index, size):
    return jnp.stack([pick(table, slots[e], start_index, size) for e in range(slots.shape[0])])


def place(total, piece, start_index):
    return lax.dynamic_update_slice(total, piece, (0, 0, start_index))


def place_own(total, piece, own, start_index):
    return lax.dynamic_update_slice(total, piece[None], (own, 0, start_index))


def activate(gate_value, up_value):
    return jax.nn.gelu(gate_value, approximate=True) * up_value


def segment_of(columns, widths):
    seg = jnp.zeros(columns.shape, jnp.int32)
    edge = 0
    for width in widths[:-1]:
        edge += width
        seg = seg + (columns >= edge).astype(jnp.int32)
    return seg


def settle(compact, choices, widths, adapters):
    mbs, seqs, rows, cols = compact.shape
    devices = lax.axis_size(("dp", "seq", "mp"))
    chunk = cols // devices
    arranged = compact.reshape(mbs, seqs, rows, devices, chunk)
    reduced = lax.psum_scatter(arranged, ("dp", "seq", "mp"), scatter_dimension=3, tiled=True)
    reduced = reduced.reshape(mbs, seqs, rows, chunk)
    flat = lax.axis_index(("dp", "seq", "mp"))
    columns = flat * chunk + jnp.arange(chunk, dtype=jnp.int32)
    seg = segment_of(columns, widths)
    chosen = jnp.take_along_axis(
        choices[:, :, None, :], jnp.broadcast_to(seg[None, None, :, None], (mbs, seqs, chunk, 1)), axis=3
    )[..., 0]
    hits = chosen[None] == jnp.arange(adapters, dtype=jnp.int32)[:, None, None, None]
    picked = jnp.where(hits[:, :, :, None, :], reduced[None], 0.0)
    return jnp.sum(picked, axis=(1, 2))


def to_owner(partial):
    mine = lax.psum_scatter(partial, "dp", scatter_dimension=0, tiled=True)[0]
    return lax.psum(mine, "mp")


def shards(
    inputs,
    cotangent,
    pre_attention,
    post_attention,
    pre_feedforward,
    post_feedforward,
    query_weight,
    key_matrix,
    value_matrix,
    output_weight,
    gate_weight,
    up_weight,
    down_weight,
    adapter_down,
    adapter_up,
    prefix_lengths,
    adapter_choice,
):
    groups = lax.axis_size("dp")
    parts = lax.axis_size("mp")
    blocks = lax.axis_size("seq")
    quarters = groups * parts
    own = lax.axis_index("dp")
    part = lax.axis_index("mp")
    quarter = part * groups + own
    rows = inputs.shape[2]
    length = rows * blocks
    positions = lax.axis_index("seq") * rows + jnp.arange(rows, dtype=jnp.int32)
    key_positions = jnp.arange(length, dtype=jnp.int32)
    cosine_table, sine_table = angles(positions)
    query_width = QUERY_HEADS_COUNT * HEAD_SIZE
    key_span_width = KEY_VALUE_HEADS * HEAD_SIZE
    query_local = query_width // quarters
    key_local = key_span_width // quarters
    hidden_local = FF // quarters
    half = MODEL_WIDTH // parts
    head_groups = QUERY_HEADS_COUNT // KEY_VALUE_HEADS
    query_heads = query_local // HEAD_SIZE
    key_heads = key_local // HEAD_SIZE
    row_block = MODEL_WIDTH // (groups * blocks)
    scale = HEAD_SIZE ** (-0.5)
    in_output = 3 * MODEL_WIDTH + quarter * query_local
    in_gate = 3 * MODEL_WIDTH + query_width
    in_up = 4 * MODEL_WIDTH + query_width
    in_down = 5 * MODEL_WIDTH + query_width + quarter * hidden_local
    out_query = quarter * query_local
    out_key = query_width + quarter * key_local
    out_value = query_width + key_span_width + quarter * key_local
    out_output = query_width + 2 * key_span_width
    out_gate = query_width + 2 * key_span_width + MODEL_WIDTH + quarter * hidden_local
    out_up = query_width + 2 * key_span_width + MODEL_WIDTH + FF + quarter * hidden_local
    out_down = query_width + 2 * key_span_width + MODEL_WIDTH + 2 * FF
    tokens = groups * rows

    def permute(value):
        lead = value.shape[:-1]
        moved = value.reshape(lead + (groups, blocks, row_block))
        return jnp.swapaxes(moved, -3, -2).reshape(lead + (MODEL_WIDTH,))

    def unpermute(value):
        lead = value.shape[:-1]
        moved = value.reshape(lead + (blocks, groups, row_block))
        return jnp.swapaxes(moved, -3, -2).reshape(lead + (MODEL_WIDTH,))

    def column_weight(weight):
        swapped = lax.all_to_all(weight, "dp", 1, 0, tiled=True)
        return lax.all_gather(swapped, "seq", axis=0, tiled=True)

    def row_weight(weight):
        swapped = lax.all_to_all(weight, "dp", 0, 1, tiled=True)
        return lax.all_gather(swapped, "seq", axis=1, tiled=True)

    query_full = column_weight(query_weight)
    key_full = column_weight(key_matrix)
    value_full = column_weight(value_matrix)
    output_full = row_weight(output_weight)
    gate_full = column_weight(gate_weight)
    up_full = column_weight(up_weight)
    down_full = row_weight(down_weight)

    sources_all = lax.all_gather(inputs[:, 0], "dp", axis=1, tiled=False)
    prefix_all = lax.all_gather(prefix_lengths[:, 0], "dp", axis=1, tiled=False)
    choices = lax.all_gather(adapter_choice[:, 0], "dp", axis=1, tiled=False)

    def column_forward(inputs_low, weight, down_part, up_part):
        main = jnp.dot(permute(inputs_low).reshape(tokens, MODEL_WIDTH), weight, preferred_element_type=WIDE)
        inner = jnp.einsum("etd,erd->etr", inputs_low, down_part, preferred_element_type=WIDE).astype(NARROW)
        low = jnp.einsum("etr,ero->eto", inner, up_part, preferred_element_type=WIDE)
        return (main.reshape(groups, rows, -1) + low, inner)

    def row_forward(inputs_low, weight, down_part, up_own):
        width = inputs_low.shape[-1]
        main_part = jnp.dot(inputs_low.reshape(tokens, width), weight, preferred_element_type=WIDE)
        inner_part = jnp.einsum("etq,erq->etr", inputs_low, down_part, preferred_element_type=WIDE)
        both = jnp.concatenate([main_part.reshape(groups, rows, MODEL_WIDTH), inner_part], axis=-1)
        both = to_owner(both)
        main = unpermute(both[:, :MODEL_WIDTH])
        inner_low = both[:, MODEL_WIDTH:].astype(NARROW)
        return (main + jnp.dot(inner_low, up_own, preferred_element_type=WIDE), inner_low)

    def column_back(grad_out, weight, down_part, up_part, inputs_low, inner_low):
        inner_grad = jnp.einsum("eto,ero->etr", grad_out, up_part, preferred_element_type=WIDE)
        width = grad_out.shape[-1]
        back = jnp.einsum("to,do->td", grad_out.reshape(tokens, width), weight, preferred_element_type=WIDE)
        back = unpermute(back.reshape(groups, rows, MODEL_WIDTH))
        back = back + jnp.einsum("etr,erd->etd", inner_grad, down_part.astype(WIDE), precision=HIGH)
        down_grad = jnp.einsum("etr,etd->erd", inner_grad, inputs_low.astype(WIDE), precision=HIGH)
        up_grad = jnp.einsum("etr,eto->ero", inner_low, grad_out, preferred_element_type=WIDE)
        return (back, down_grad, up_grad)

    def row_back(grad_all, grad_own, weight, down_part, up_part, inputs_low, inner_own):
        inner_grad = jnp.einsum("etd,erd->etr", grad_all, up_part, preferred_element_type=WIDE)
        back = jnp.einsum(
            "td,qd->tq", permute(grad_all).reshape(tokens, MODEL_WIDTH), weight, preferred_element_type=WIDE
        )
        back = back.reshape(groups, rows, -1)
        back = back + jnp.einsum("etr,erq->etq", inner_grad, down_part.astype(WIDE), precision=HIGH)
        down_grad = jnp.einsum("etr,etq->erq", inner_grad, inputs_low.astype(WIDE), precision=HIGH)
        own_columns = lax.dynamic_slice_in_dim(grad_own, part * half, half, 1)
        up_grad = jnp.einsum("tr,tc->rc", inner_own, own_columns, preferred_element_type=WIDE)
        return (back, down_grad, up_grad)

    down_list = []
    up_list = []
    results = []
    input_grads = []
    for batch in range(inputs.shape[0]):
        slots = choices[batch]
        own_slots = adapter_choice[batch, 0]
        prefix_length = prefix_all[batch]
        down_query = picks(adapter_down, slots[:, 0], 0, MODEL_WIDTH)
        down_key = picks(adapter_down, slots[:, 1], MODEL_WIDTH, MODEL_WIDTH)
        down_value = picks(adapter_down, slots[:, 2], 2 * MODEL_WIDTH, MODEL_WIDTH)
        down_output = picks(adapter_down, slots[:, 3], in_output, query_local)
        down_gate = picks(adapter_down, slots[:, 4], in_gate, MODEL_WIDTH)
        down_up = picks(adapter_down, slots[:, 5], in_up, MODEL_WIDTH)
        down_down = picks(adapter_down, slots[:, 6], in_down, hidden_local)
        up_query = picks(adapter_up, slots[:, 0], out_query, query_local)
        up_key = picks(adapter_up, slots[:, 1], out_key, key_local)
        up_value = picks(adapter_up, slots[:, 2], out_value, key_local)
        up_output = picks(adapter_up, slots[:, 3], out_output, MODEL_WIDTH)
        up_gate = picks(adapter_up, slots[:, 4], out_gate, hidden_local)
        up_upper = picks(adapter_up, slots[:, 5], out_up, hidden_local)
        up_down = picks(adapter_up, slots[:, 6], out_down, MODEL_WIDTH)
        up_output_own = pick(adapter_up, own_slots[3], out_output, MODEL_WIDTH)
        up_down_own = pick(adapter_up, own_slots[6], out_down, MODEL_WIDTH)

        source = inputs[batch, 0].astype(WIDE)
        normed = normalize(sources_all[batch].astype(WIDE), pre_attention).astype(NARROW)
        query, inner_query = column_forward(normed, query_full, down_query, up_query)
        key_rows, inner_key = column_forward(normed, key_full, down_key, up_key)
        value_rows, inner_value = column_forward(normed, value_full, down_value, up_value)
        rotated_query = apply_rotation(
            query.reshape(groups, rows, query_heads, HEAD_SIZE), cosine_table, sine_table
        ).astype(NARROW)
        rotated_keys = (
            apply_rotation(key_rows.reshape(groups, rows, key_heads, HEAD_SIZE), cosine_table, sine_table)
            .astype(NARROW)
            .reshape(groups, rows, key_local)
        )
        values_low = value_rows.astype(NARROW)
        both_all = lax.all_gather(jnp.stack([rotated_keys, values_low]), "seq", axis=2, tiled=True)
        keys_three = both_all[0].reshape(groups, length, key_heads, HEAD_SIZE)
        values_three = both_all[1].reshape(groups, length, key_heads, HEAD_SIZE)
        query_four = rotated_query.reshape(groups, rows, key_heads, head_groups, HEAD_SIZE)
        visible = (key_positions[None, None, :] <= positions[None, :, None]) | (
            key_positions[None, None, :] < prefix_length[:, None, None]
        )
        visible = visible[:, None, None]
        raw = (
            jnp.einsum("etkgd,eskd->ekgts", query_four, keys_three, preferred_element_type=WIDE)
            * scale
        )
        masked = jnp.where(visible, SOFT_CAP * jnp.tanh(raw / SOFT_CAP), -1e30)
        top = jnp.max(masked, axis=-1, keepdims=True)
        expo = jnp.exp(masked - top)
        total = jnp.sum(expo, axis=-1, keepdims=True)
        log_total = top + jnp.log(total)
        prob_low = (expo / total).astype(NARROW)
        head_stack = jnp.einsum(
            "ekgts,eskd->etkgd", prob_low, values_three, preferred_element_type=WIDE
        )
        head_stack = head_stack.reshape(groups, rows, query_local).astype(NARROW)
        attention_out, inner_output = row_forward(head_stack, output_full, down_output, up_output_own)
        middle = source + normalize(attention_out, post_attention)
        normed_ffw_own = normalize(middle, pre_feedforward).astype(NARROW)
        normed_ffw = lax.all_gather(normed_ffw_own, "dp", axis=0, tiled=False)
        gate, inner_gate = column_forward(normed_ffw, gate_full, down_gate, up_gate)
        upper, inner_upper = column_forward(normed_ffw, up_full, down_up, up_upper)
        hidden = activate(gate, upper).astype(NARROW)
        ffw_out, inner_down = row_forward(hidden, down_full, down_down, up_down_own)
        results.append((middle + normalize(ffw_out, post_feedforward)).astype(NARROW))

        grad_down = jnp.zeros((groups,) + adapter_down.shape[1:], WIDE)
        grad_up = jnp.zeros((groups,) + adapter_up.shape[1:], WIDE)
        seed_grad = cotangent[batch, 0].astype(WIDE)
        grad_ffw_own = normalize_back(ffw_out, post_feedforward, seed_grad).astype(NARROW)
        grad_ffw = lax.all_gather(grad_ffw_own, "dp", axis=0, tiled=False)
        grad_hidden, piece_down, piece_up = row_back(
            grad_ffw, grad_ffw_own, down_full, down_down, up_down, hidden, inner_down
        )
        grad_down = place(grad_down, piece_down, in_down)
        grad_up = place_own(grad_up, piece_up, own, out_down + part * half)
        pull = jax.vjp(activate, gate, upper)[1]
        grad_gate, grad_upper = pull(grad_hidden)
        grad_gate = grad_gate.astype(NARROW)
        grad_upper = grad_upper.astype(NARROW)
        back_gate, piece_down, piece_up = column_back(
            grad_gate, gate_full, down_gate, up_gate, normed_ffw, inner_gate
        )
        grad_down = place(grad_down, piece_down, in_gate)
        grad_up = place(grad_up, piece_up, out_gate)
        back_upper, piece_down, piece_up = column_back(
            grad_upper, up_full, down_up, up_upper, normed_ffw, inner_upper
        )
        grad_down = place(grad_down, piece_down, in_up)
        grad_up = place(grad_up, piece_up, out_up)
        grad_normed_ffw = to_owner(back_gate + back_upper)
        grad_middle = seed_grad + normalize_back(middle, pre_feedforward, grad_normed_ffw)
        grad_attention_own = normalize_back(attention_out, post_attention, grad_middle).astype(NARROW)
        grad_attention = lax.all_gather(grad_attention_own, "dp", axis=0, tiled=False)
        grad_heads, piece_down, piece_up = row_back(
            grad_attention,
            grad_attention_own,
            output_full,
            down_output,
            up_output,
            head_stack,
            inner_output,
        )
        grad_down = place(grad_down, piece_down, in_output)
        grad_up = place_own(grad_up, piece_up, own, out_output + part * half)
        grad_heads_four = grad_heads.astype(NARROW).reshape(groups, rows, key_heads, head_groups, HEAD_SIZE)
        prob = jnp.exp(masked - log_total)
        grad_prob = jnp.einsum(
            "etkgd,eskd->ekgts", grad_heads_four, values_three, preferred_element_type=WIDE
        )
        grad_capped = prob * (grad_prob - jnp.sum(prob * grad_prob, axis=-1, keepdims=True))
        bend = jnp.tanh(raw / SOFT_CAP)
        grad_raw = (grad_capped * (1.0 - bend * bend)).astype(NARROW)
        grad_query_rot = (
            jnp.einsum("ekgts,eskd->etkgd", grad_raw, keys_three, preferred_element_type=WIDE) * scale
        )
        grad_key_part = (
            jnp.einsum("ekgts,etkgd->eskd", grad_raw, query_four, preferred_element_type=WIDE) * scale
        )
        grad_value_part = jnp.einsum(
            "ekgts,etkgd->eskd", prob_low, grad_heads_four, preferred_element_type=WIDE
        )
        both_grad = lax.psum_scatter(
            jnp.stack(
                [
                    grad_key_part.reshape(groups, length, key_local),
                    grad_value_part.reshape(groups, length, key_local),
                ]
            ),
            "seq",
            scatter_dimension=2,
            tiled=True,
        )
        key_grad, value_grad = both_grad[0], both_grad[1]
        grad_query = (
            rotate_back(
                grad_query_rot.reshape(groups, rows, query_heads, HEAD_SIZE), cosine_table, sine_table
            )
            .reshape(groups, rows, query_local)
            .astype(NARROW)
        )
        grad_key = (
            rotate_back(key_grad.reshape(groups, rows, key_heads, HEAD_SIZE), cosine_table, sine_table)
            .reshape(groups, rows, key_local)
            .astype(NARROW)
        )
        grad_value = value_grad.astype(NARROW)
        back_query, piece_down, piece_up = column_back(
            grad_query, query_full, down_query, up_query, normed, inner_query
        )
        grad_down = place(grad_down, piece_down, 0)
        grad_up = place(grad_up, piece_up, out_query)
        back_key, piece_down, piece_up = column_back(
            grad_key, key_full, down_key, up_key, normed, inner_key
        )
        grad_down = place(grad_down, piece_down, MODEL_WIDTH)
        grad_up = place(grad_up, piece_up, out_key)
        back_value, piece_down, piece_up = column_back(
            grad_value, value_full, down_value, up_value, normed, inner_value
        )
        grad_down = place(grad_down, piece_down, 2 * MODEL_WIDTH)
        grad_up = place(grad_up, piece_up, out_value)
        grad_normed = to_owner(back_query + back_key + back_value)
        down_list.append(grad_down)
        up_list.append(grad_up)
        input_grads.append(
            (grad_middle + normalize_back(source, pre_attention, grad_normed)).astype(NARROW)
        )
    down_widths = (MODEL_WIDTH, MODEL_WIDTH, MODEL_WIDTH, query_width, MODEL_WIDTH, MODEL_WIDTH, FF)
    up_widths = (query_width, key_span_width, key_span_width, MODEL_WIDTH, FF, FF, MODEL_WIDTH)
    down_total = settle(jnp.stack(down_list), choices, down_widths, adapter_down.shape[0])
    up_total = settle(jnp.stack(up_list), choices, up_widths, adapter_up.shape[0])
    outputs = jnp.stack(results)[:, None]
    input_gradient = jnp.stack(input_grads)[:, None]
    return (outputs, input_gradient, down_total, up_total)


def solution(mesh):
    return jax.shard_map(
        shards,
        mesh=mesh,
        in_specs=(
            P(None, "dp", "seq", None),
            P(None, "dp", "seq", None),
            P(),
            P(),
            P(),
            P(),
            P(("dp", "seq"), "mp"),
            P(("dp", "seq"), "mp"),
            P(("dp", "seq"), "mp"),
            P("mp", ("dp", "seq")),
            P(("dp", "seq"), "mp"),
            P(("dp", "seq"), "mp"),
            P("mp", ("dp", "seq")),
            P(),
            P(),
            P(None, "dp"),
            P(None, "dp", None),
        ),
        out_specs=(
            P(None, "dp", "seq", None),
            P(None, "dp", "seq", None),
            P(None, None, ("dp", "seq", "mp")),
            P(None, None, ("dp", "seq", "mp")),
        ),
        check_vma=False,
    )
```

time: 2120 us -> 1940 us (0.915)
  waiting for transfers between devices: 1520 us -> 1190 us
  matrix products: 314 us -> 198 us
  blocking collectives: 6.78 us -> 116 us
  local copies, waits for them, and re-layouts: 200 us -> 279 us
  between operations: 42.7 us -> 80.2 us
  other arithmetic: 29.3 us -> 63.5 us
    all_gather x11 -> x16, waiting for transfers between devices: 1030 us -> 638 us  [the longest x5 312 us: column_weight(): return lax.all_gather(swapped, 'seq', axis=0, tiled=True)]
    reduce_scatter x4 -> x12, waiting for transfers between devices: 196 us -> 482 us  [the longest x8 179 us: to_owner(): mine = lax.psum_scatter(partial, 'dp', scatter_dimension=0, tiled=True)[0]]
    unnamed x23 -> x32, waiting for transfers between devices: 254 us -> 1.61 us
    unnamed x343 -> x633, local copies, waits for them, and re-layouts: 147 us -> 23.3 us
    dot_general x124, matrix products: 314 us -> 198 us  [the longest x10 33.3 us: column_forward(): jnp.dot(permute(inputs_low).reshape(tokens, MODEL_WIDTH), weight, preferr...]
    all_to_all x0 -> x6, blocking collectives: none -> 103 us  [the longest x4 79.6 us: column_weight(): swapped = lax.all_to_all(weight, 'dp', 1, 0, tiled=True)]
    reshape x8 -> x25, local copies, waits for them, and re-layouts: 7.15 us -> 101 us  [the longest x14 40 us: unpermute(): return jnp.swapaxes(moved, -3, -2).reshape(lead + (MODEL_WIDTH,))]
    gather x0 -> x6, local copies, waits for them, and re-layouts: none -> 71.3 us  [settle(): jnp.take_along_axis(choices[:, :, None, :], jnp.broadcast_to(seg[None, No...]
  transfers between devices with their start and end apart: 21 -> 33, of which waited for: 20 -> 24; matrix products, arithmetic and copies ran while one was open for 17% -> 23% of each run, Pallas kernels for 0% -> 0%
where the time goes in v2:
time: 1940 us; the launch traced here: 1930 us
  waiting for transfers between devices  1190 us (61%)
  local copies, waits for them, and re-layouts  279 us (14%)
  matrix products  198 us (10%)
  blocking collectives  116 us (6%)
  between operations  80.2 us (4%)
  other arithmetic  63.5 us (3%)
    all_gather x5, waiting for transfers between devices, column_weight(): return lax.all_gather(swapped, 'seq', axis=0, tiled=True)  312 us
    all_gather x2, waiting for transfers between devices, row_weight(): return lax.all_gather(swapped, 'seq', axis=1, tiled=True)  189 us
    reduce_scatter x8, waiting for transfers between devices, to_owner(): mine = lax.psum_scatter(partial, 'dp', scatter_dimension=0, tiled=True)[0]  179 us
    reduce_scatter x2, waiting for transfers between devices, settle(): lax.psum_scatter(arranged, ('dp', 'seq', 'mp'), scatter_dimension=3, tile...  157 us
    reduce_scatter x2, waiting for transfers between devices, shards(): lax.psum_scatter(jnp.stack([grad_key_part.reshape(groups, length, key_loc...  146 us
    all_gather x2, waiting for transfers between devices, shards(): lax.all_gather(jnp.stack([rotated_keys, values_low]), 'seq', axis=2, tile...  85.1 us
    all_to_all x4, blocking collectives, column_weight(): swapped = lax.all_to_all(weight, 'dp', 1, 0, tiled=True)  79.6 us
    gather x6, local copies, waits for them, and re-layouts, settle(): jnp.take_along_axis(choices[:, :, None, :], jnp.broadcast_to(seg[None, No...  71.3 us
  transfers between devices with their start and end apart: 33, of which 24 were waited for; matrix products, arithmetic and copies ran while one was open for 23% of the time, Pallas kernels for 0%

profile of v2, /device:TPU:0, one launch (start us, length us, event | category | flops | bytes accessed | tf_op | source)
XLA Modules:
  0.0 1930.4 jit_solution(17110588752438615256)
XLA Ops:
  108.7 30.5 %all-gather.26.cloned.1.call-done = bf16[2304,256]{1,0:T(8,128)(2,1)} async-done(((bf16[288,256]{1,0:T(8,128)(2,1)}), bf16[2304,256]{1,0:T(8,128)(2,1)}) %all-gather.26.cloned.1.call-update) | async-done | bytes 1179664 | tf_op jit(solution)/shard_map/all_gather | solution.py:178
  203.0 39.5 %all-gather.42.cloned.1.call-done = bf16[2,2,1024,256]{3,2,1,0:T(8,128)(2,1)} async-done(((bf16[2,2,128,256]{3,2,1,0:T(8,128)(2,1)}), bf16[2,2,1024,256]{3,2,1,0:T(8,128)(2,1)}) %all-gather.42.cloned.1.call-update) | async-done | bytes 2097168 | tf_op jit(solution)/shard_map/all_gather | solution.py:273
  248.2 46.8 %all-gather.34.cloned.1.call-done = bf16[512,2304]{0,1:T(8,128)(2,1)} async-done(((bf16[512,288]{0,1:T(8,128)(2,1)}), bf16[512,2304]{0,1:T(8,128)(2,1)}) %all-gather.34.cloned.1.call-update) | async-done | bytes 2359312 | tf_op jit(solution)/shard_map/all_gather | solution.py:182
  299.3 45.5 %all-gather.30.cloned.1.call-done = bf16[2,2,1024,256]{3,2,1,0:T(8,128)(2,1)} async-done(((bf16[2,2,128,256]{3,2,1,0:T(8,128)(2,1)}), bf16[2,2,1024,256]{3,2,1,0:T(8,128)(2,1)}) %all-gather.30.cloned.1.call-update) | async-done | bytes 2097168 | tf_op jit(solution)/shard_map/all_gather | solution.py:273
  353.3 28.5 %reduce-scatter.17.cloned.1.call-done = f32[1,128,2320]{2,1,0:T(8,128)} async-done(((f32[2,128,2320]{2,1,0:T(8,128)}), f32[1,128,2320]{2,1,0:T(8,128)}) %reduce-scatter.17.cloned.1.call-update) | async-done | bytes 1187856 | tf_op jit(solution)/shard_map/reduce_scatter | solution.py:107
  381.8 38.5 %reduce-scatter.13.cloned.1.call-done = f32[1,128,2320]{2,1,0:T(8,128)} async-done(((f32[2,128,2320]{2,1,0:T(8,128)}), f32[1,128,2320]{2,1,0:T(8,128)}) %reduce-scatter.13.cloned.1.call-update) | async-done | bytes 1187856 | tf_op jit(solution)/shard_map/reduce_scatter | solution.py:107
  425.4 19.3 %all-reduce.15.cloned.1.call-done = (f32[128,2320]{1,0:T(8,128)}, f32[128,2320]{1,0:T(8,128)}) async-done(((f32[128,2320]{1,0:T(8,128)}, f32[128,2320]{1,0:T(8,128)}), (f32[128,2320]{1,0:T(8,128)}, f32[128,2320]{1,0:T(8,128)})) %all-reduce.15.cloned.1.call-update) | async-done | bytes 2375696 | tf_op jit(solution)/shard_map/psum | solution.py:108
  468.8 32.6 %all_to_all.136 = bf16[144,2,2304]{2,0,1:T(8,128)(2,1)} all-to-all(bf16[144,2,2304]{2,0,1:T(8,128)(2,1)S(1)} %bitcast.952), channel_id=1, replica_groups=mesh['dp'=2,'seq'=8,'mp'=2] {'dp'}, dimensions={1} | all-to-all | bytes 2654208 | tf_op jit(solution)/shard_map/all_to_all | solution.py:177
  502.9 29.0 %all_to_all.137 = bf16[144,2,2304]{2,0,1:T(8,128)(2,1)} all-to-all(bf16[144,2,2304]{2,0,1:T(8,128)(2,1)S(1)} %bitcast.953), channel_id=1, replica_groups=mesh['dp'=2,'seq'=8,'mp'=2] {'dp'}, dimensions={1} | all-to-all | bytes 2654208 | tf_op jit(solution)/shard_map/all_to_all | solution.py:177
  563.9 126.3 %all-gather.36.cloned.1.call-done = bf16[2304,2304]{1,0:T(8,128)(2,1)} async-done(((bf16[288,2304]{1,0:T(8,128)(2,1)}), bf16[2304,2304]{1,0:T(8,128)(2,1)}) %all-gather.36.cloned.1.call-update) | async-done | bytes 10616848 | tf_op jit(solution)/shard_map/all_gather | solution.py:178
  698.2 144.4 %all-gather.38.cloned.1.call-done = bf16[2304,2304]{1,0:T(8,128)(2,1)} async-done(((bf16[288,2304]{1,0:T(8,128)(2,1)}), bf16[2304,2304]{1,0:T(8,128)(2,1)}) %all-gather.38.cloned.1.call-update) | async-done | bytes 10616848 | tf_op jit(solution)/shard_map/all_gather | solution.py:178
  852.4 142.5 %all-gather.40.cloned.1.call-done = bf16[2304,2304]{0,1:T(8,128)(2,1)} async-done(((bf16[2304,288]{0,1:T(8,128)(2,1)}), bf16[2304,2304]{0,1:T(8,128)(2,1)}) %all-gather.40.cloned.1.call-update) | async-done | bytes 10616848 | tf_op jit(solution)/shard_map/all_gather | solution.py:182
  1037.2 38.4 %reduce-scatter.15.cloned.1.call-done = f32[1,128,2320]{2,1,0:T(8,128)} async-done(((f32[2,128,2320]{2,1,0:T(8,128)}), f32[1,128,2320]{2,1,0:T(8,128)}) %reduce-scatter.15.cloned.1.call-update) | async-done | bytes 1187856 | tf_op jit(solution)/shard_map/reduce_scatter | solution.py:107
  1079.5 20.3 %all-reduce.13.cloned.1.call-done = (f32[128,2320]{1,0:T(8,128)}, f32[128,2320]{1,0:T(8,128)}) async-done(((f32[128,2320]{1,0:T(8,128)}, f32[128,2320]{1,0:T(8,128)}), (f32[128,2320]{1,0:T(8,128)}, f32[128,2320]{1,0:T(8,128)})) %all-reduce.13.cloned.1.call-update) | async-done | bytes 2375696 | tf_op jit(solution)/shard_map/psum | solution.py:108
  1122.1 23.5 %all-gather.52.cloned.1.call-done = bf16[256,2304]{1,0:T(8,128)(2,1)} async-done(((bf16[128,2304]{1,0:T(8,128)(2,1)}), bf16[256,2304]{1,0:T(8,128)(2,1)}) %all-gather.52.cloned.1.call-update) | async-done | bytes 1179664 | tf_op jit(solution)/shard_map/all_gather | solution.py:309
  1236.9 35.0 %reduce-scatter.21.cloned.1.call-done = f32[1,128,2304]{2,1,0:T(8,128)} async-done(((f32[2,128,2304]{2,1,0:T(8,128)}), f32[1,128,2304]{2,1,0:T(8,128)}) %reduce-scatter.21.cloned.1.call-update) | async-done | bytes 1179664 | tf_op jit(solution)/shard_map/reduce_scatter | solution.py:107
  1271.9 24.2 %all-reduce.11.cloned.1.call-done = (f32[128,2304]{1,0:T(8,128)}, f32[128,2304]{1,0:T(8,128)}) async-done(((f32[128,2304]{1,0:T(8,128)}, f32[128,2304]{1,0:T(8,128)}), (f32[128,2304]{1,0:T(8,128)}, f32[128,2304]{1,0:T(8,128)})) %all-reduce.11.cloned.1.call-update) | async-done | bytes 2359312 | tf_op jit(solution)/shard_map/psum | solution.py:108
  1304.9 23.3 %all-gather.54.cloned.1.call-done = bf16[256,2304]{1,0:T(8,128)(2,1)} async-done(((bf16[128,2304]{1,0:T(8,128)(2,1)}), bf16[256,2304]{1,0:T(8,128)(2,1)}) %all-gather.54.cloned.1.call-update) | async-done | bytes 1179664 | tf_op jit(solution)/shard_map/all_gather | solution.py:332
  1382.9 61.8 %reduce-scatter.29.cloned.1.call-done = f32[2,2,128,256]{3,2,1,0:T(8,128)} async-done(((f32[2,2,1024,256]{3,2,1,0:T(8,128)}), f32[2,2,128,256]{3,2,1,0:T(8,128)}) %reduce-scatter.29.cloned.1.call-update) | async-done | bytes 524304 | tf_op jit(solution)/shard_map/reduce_scatter | solution.py:361
  1452.7 83.9 %reduce-scatter.23.cloned.1.call-done = f32[2,2,128,256]{3,2,1,0:T(8,128)} async-done(((f32[2,2,1024,256]{3,2,1,0:T(8,128)}), f32[2,2,128,256]{3,2,1,0:T(8,128)}) %reduce-scatter.23.cloned.1.call-update) | async-done | bytes 524304 | tf_op jit(solution)/shard_map/reduce_scatter | solution.py:361
  1595.8 30.1 %reduce-scatter.25.cloned.1.call-done = f32[1,128,2304]{2,1,0:T(8,128)} async-done(((f32[2,128,2304]{2,1,0:T(8,128)}), f32[1,128,2304]{2,1,0:T(8,128)}) %reduce-scatter.25.cloned.1.call-update) | async-done | bytes 1179664 | tf_op jit(solution)/shard_map/reduce_scatter | solution.py:107
  1682.3 39.7 %gather_fusion = s32[2848]{0:T(1024)S(1)} fusion(s32[2,2,7]{2,0,1:T(2,128)S(1)} %copy-done.1, s32[2848]{0:T(1024)S(1)} %reshape.1164), kind=kCustom, calls=%fused_computation | custom fusion | bytes 56960 | tf_op jit(solution)/shard_map/jit(take_along_axis)/gather | solution.py:98
  1722.4 31.3 %gather_fusion.1 = s32[3392]{0:T(1024)S(1)} fusion(s32[2,2,7]{2,0,1:T(2,128)S(1)} %copy-done.1, s32[3392]{0:T(1024)S(1)} %reshape.1172), kind=kCustom, calls=%fused_computation.1 | custom fusion | bytes 67840 | tf_op jit(solution)/shard_map/jit(take_along_axis)/gather | solution.py:98
  1773.7 147.7 %reduce-scatter.35.cloned.1.call-done = f32[2,2,16,1,848]{4,2,1,0,3:T(8,128)} async-done(((f32[2,2,16,32,848]{4,2,1,0,3:T(8,128)}), f32[2,2,16,1,848]{4,2,1,0,3:T(8,128)}) %reduce-scatter.35.cloned.1.call-update) | async-done | bytes 217104 | tf_op jit(solution)/shard_map/reduce_scatter | solution.py:93
  (1016 shorter events, 567.7 us)
Async XLA Ops:
  7.2 90.9 %all-gather.24.cloned.1.call-start = ((), (), s32[]{:S(2)}) async-start(), calls=%async_computation.19 | async-start | bytes 3538944 | tf_op jit(solution)/shard_map/all_gather | solution.py:192
  9.7 96.5 %all-gather.28.cloned.1.call-start = ((), (), s32[]{:S(2)}) async-start(), calls=%async_computation.21 | async-start | bytes 1327104 | tf_op jit(solution)/shard_map/all_gather | solution.py:178
  18.5 120.6 %all-gather.26.cloned.1.call-start = ((), (), s32[]{:S(2)}) async-start(), calls=%async_computation.20 | async-start | bytes 1327104 | tf_op jit(solution)/shard_map/all_gather | solution.py:178
  32.2 160.1 %all-gather.32.cloned.1.call-start = ((), (), s32[]{:S(2)}) async-start(), calls=%async_computation.23 | async-start | bytes 2654208 | tf_op jit(solution)/shard_map/all_gather | solution.py:178
  98.0 144.6 %all-gather.42.cloned.1.call-start = ((), (), s32[]{:S(2)}) async-start(), calls=%async_computation.30 | async-start | bytes 2359296 | tf_op jit(solution)/shard_map/all_gather | solution.py:273
  143.4 151.5 %all-gather.34.cloned.1.call-start = ((), (), s32[]{:S(2)}) async-start(), calls=%async_computation.24 | async-start | bytes 2654208 | tf_op jit(solution)/shard_map/all_gather | solution.py:182
  152.9 191.8 %all-gather.30.cloned.1.call-start = ((), (), s32[]{:S(2)}) async-start(), calls=%async_computation.22 | async-start | bytes 2359296 | tf_op jit(solution)/shard_map/all_gather | solution.py:273
  175.3 206.5 %reduce-scatter.17.cloned.1.call-start = ((), (), s32[]{:S(2)}) async-start(), calls=%async_computation.31 | async-start | bytes 3735552 | tf_op jit(solution)/shard_map/reduce_scatter | solution.py:107
  299.2 121.1 %reduce-scatter.13.cloned.1.call-start = ((), (), s32[]{:S(2)}) async-start(), calls=%async_computation.25 | async-start | bytes 3735552 | tf_op jit(solution)/shard_map/reduce_scatter | solution.py:107
  353.2 91.4 %all-reduce.15.cloned.1.call-start = ((), (), s32[]{:S(2)}) async-start(), calls=%async_computation.50 | async-start | bytes 4980736 | tf_op jit(solution)/shard_map/psum | solution.py:108
  420.4 130.5 %all-gather.46.cloned.1.call-start = ((), (), s32[]{:S(2)}) async-start(), calls=%async_computation.42 | async-start | bytes 1769472 | tf_op jit(solution)/shard_map/all_gather | solution.py:298
  466.7 94.7 %all-gather.44.cloned.1.call-start = ((), (), s32[]{:S(2)}) async-start(), calls=%async_computation.41 | async-start | bytes 1769472 | tf_op jit(solution)/shard_map/all_gather | solution.py:298
  467.3 222.8 %all-gather.36.cloned.1.call-start = ((), (), s32[]{:S(2)}) async-start(), calls=%async_computation.26 | async-start | bytes 11943936 | tf_op jit(solution)/shard_map/all_gather | solution.py:178
  501.4 341.1 %all-gather.38.cloned.1.call-start = ((), (), s32[]{:S(2)}) async-start(), calls=%async_computation.27 | async-start | bytes 11943936 | tf_op jit(solution)/shard_map/all_gather | solution.py:178
  531.9 463.0 %all-gather.40.cloned.1.call-start = ((), (), s32[]{:S(2)}) async-start(), calls=%async_computation.28 | async-start | bytes 11943936 | tf_op jit(solution)/shard_map/all_gather | solution.py:182
  548.4 488.8 %reduce-scatter.19.cloned.1.call-start = ((), (), s32[]{:S(2)}) async-start(), calls=%async_computation.32 | async-start | bytes 3735552 | tf_op jit(solution)/shard_map/reduce_scatter | solution.py:107
  1122.0 114.9 %reduce-scatter.27.cloned.1.call-start = ((), (), s32[]{:S(2)}) async-start(), calls=%async_computation.36 | async-start | bytes 3538944 | tf_op jit(solution)/shard_map/reduce_scatter | solution.py:107
  1191.1 80.8 %reduce-scatter.21.cloned.1.call-start = ((), (), s32[]{:S(2)}) async-start(), calls=%async_computation.33 | async-start | bytes 3538944 | tf_op jit(solution)/shard_map/reduce_scatter | solution.py:107
  1304.8 139.9 %reduce-scatter.29.cloned.1.call-start = ((), (), s32[]{:S(2)}) async-start(), calls=%async_computation.37 | async-start | bytes 4718592 | tf_op jit(solution)/shard_map/reduce_scatter | solution.py:361
  1346.9 189.6 %reduce-scatter.23.cloned.1.call-start = ((), (), s32[]{:S(2)}) async-start(), calls=%async_computation.34 | async-start | bytes 4718592 | tf_op jit(solution)/shard_map/reduce_scatter | solution.py:361
  1371.6 224.2 %reduce-scatter.31.cloned.1.call-start = ((), (), s32[]{:S(2)}) async-start(), calls=%async_computation.38 | async-start | bytes 3538944 | tf_op jit(solution)/shard_map/reduce_scatter | solution.py:107
  1581.7 174.6 %all-reduce.9.cloned.1.call-start = ((), (), s32[]{:S(2)}) async-start(), calls=%async_computation.47 | async-start | bytes 4718592 | tf_op jit(solution)/shard_map/psum | solution.py:108
  1625.9 145.9 %reduce-scatter.33.cloned.1.call-start = ((), (), s32[]{:S(2)}) async-start(), calls=%async_computation.39 | async-start | bytes 6488064 | tf_op jit(solution)/shard_map/reduce_scatter | solution.py:93
  1649.8 271.6 %reduce-scatter.35.cloned.1.call-start = ((), (), s32[]{:S(2)}) async-start(), calls=%async_computation.40 | async-start | bytes 7569408 | tf_op jit(solution)/shard_map/reduce_scatter | solution.py:93
  (322 other events, 3080.7 us)
Sparse Core Ops, SparseCore 0:
  10.1 43.3 all-gather.23
  55.7 41.3 all-gather.27
  99.3 39.8 all-gather.25
  141.8 50.4 all-gather.31
  194.9 47.5 all-gather.41
  244.6 50.3 all-gather.33
  297.1 47.5 all-gather.29
  347.0 34.7 reduce-scatter.16
  384.1 36.2 reduce-scatter.12
  466.9 35.3 all-gather.45
  503.6 31.9 all-gather.43
  537.8 152.3 all-gather.35
  692.2 150.2 all-gather.37
  844.5 150.2 all-gather.39
  1002.7 34.3 reduce-scatter.18
  1039.3 36.2 reduce-scatter.14
  1191.2 34.7 reduce-scatter.26
  1236.7 35.0 reduce-scatter.20
  1356.0 88.7 reduce-scatter.28
  1448.3 88.2 reduce-scatter.22
  1554.3 34.4 reduce-scatter.30
  1591.0 34.7 reduce-scatter.24
  1655.6 116.1 reduce-scatter.32
  1774.1 147.2 reduce-scatter.34
  (8 shorter events, 180.7 us)

commit v3 on v2

--- a/solution.py
+++ b/solution.py
@@ -1,3 +1,4 @@
+import numpy as np
 import jax
 import jax.numpy as jnp
 from jax import lax
@@ -85,30 +86,118 @@
     return seg
 
 
-def settle(compact, choices, widths, adapters):
-    mbs, seqs, rows, cols = compact.shape
-    devices = lax.axis_size(("dp", "seq", "mp"))
-    chunk = cols // devices
-    arranged = compact.reshape(mbs, seqs, rows, devices, chunk)
-    reduced = lax.psum_scatter(arranged, ("dp", "seq", "mp"), scatter_dimension=3, tiled=True)
-    reduced = reduced.reshape(mbs, seqs, rows, chunk)
-    flat = lax.axis_index(("dp", "seq", "mp"))
-    columns = flat * chunk + jnp.arange(chunk, dtype=jnp.int32)
+def spread(compact, choices, widths, adapters, start):
+    columns = start + jnp.arange(compact.shape[-1], dtype=jnp.int32)
     seg = segment_of(columns, widths)
-    chosen = jnp.take_along_axis(
-        choices[:, :, None, :], jnp.broadcast_to(seg[None, None, :, None], (mbs, seqs, chunk, 1)), axis=3
-    )[..., 0]
-    hits = chosen[None] == jnp.arange(adapters, dtype=jnp.int32)[:, None, None, None]
-    picked = jnp.where(hits[:, :, :, None, :], reduced[None], 0.0)
-    return jnp.sum(picked, axis=(1, 2))
-
-
-def to_owner(partial):
-    mine = lax.psum_scatter(partial, "dp", scatter_dimension=0, tiled=True)[0]
-    return lax.psum(mine, "mp")
+    chosen = jnp.zeros((choices.shape[0], compact.shape[-1]), jnp.int32)
+    for index in range(len(widths)):
+        chosen = chosen + jnp.where(seg == index, choices[:, index : index + 1], 0)
+    hits = chosen[None] == jnp.arange(adapters, dtype=jnp.int32)[:, None, None]
+    picked = jnp.where(hits[:, :, None, :], compact[None], 0.0)
+    return jnp.sum(picked, axis=1)
+
+
+def snake(sizes):
+    if not sizes:
+        return [()]
+    inner = snake(sizes[1:])
+    order = []
+    for value in range(sizes[0]):
+        steps = inner if value % 2 == 0 else inner[::-1]
+        order.extend((value,) + rest for rest in steps)
+    return order
+
+
+def ring_order(mesh):
+    names = tuple(mesh.axis_names)
+    count = mesh.shape["seq"]
+    where = [0] * len(names)
+    members = []
+    for index in range(count):
+        where[names.index("seq")] = index
+        members.append(mesh.devices[tuple(where)])
+    try:
+        coords = np.array([list(dev.coords) + [int(getattr(dev, "core_on_chip", 0))] for dev in members])
+    except Exception:
+        return list(range(count))
+    varying = [k for k in range(coords.shape[1]) if len(set(coords[:, k].tolist())) > 1]
+    sizes = [len(set(coords[:, k].tolist())) for k in varying]
+    if int(np.prod(sizes)) != count:
+        return list(range(count))
+    lowest = coords[:, varying].min(axis=0)
+    lookup = {tuple((coords[i, varying] - lowest).tolist()): i for i in range(count)}
+    if len(lookup) != count:
+        return list(range(count))
+    pairs = [k for k in range(len(sizes)) if sizes[k] == 2]
+    if pairs:
+        pivot = pairs[-1]
+        rest = [sizes[k] for k in range(len(sizes)) if k != pivot]
+        path = snake(rest)
+        order = []
+        for value, steps in ((0, path), (1, path[::-1])):
+            for point in steps:
+                full = list(point)
+                full.insert(pivot, value)
+                order.append(full)
+    else:
+        order = [list(point) for point in snake(sizes)]
+    return [lookup[tuple(point)] for point in order]
+
+
+def shift(value, axis, size, step):
+    return lax.ppermute(value, axis, [(a, (a + step) % size) for a in range(size)])
+
+
+def gather_pairs(value, axis, size, me):
+    out = jnp.zeros((size,) + value.shape, value.dtype)
+    out = lax.dynamic_update_index_in_dim(out, value, me, 0)
+    for step in range(1, size):
+        got = shift(value, axis, size, step)
+        out = lax.dynamic_update_index_in_dim(out, got, (me - step) % size, 0)
+    return out
+
+
+def scatter_pairs(partial, axis, size, me):
+    mine = lax.dynamic_index_in_dim(partial, me, 0, keepdims=False)
+    for step in range(1, size):
+        send = lax.dynamic_index_in_dim(partial, (me + step) % size, 0, keepdims=False)
+        mine = mine + shift(send, axis, size, step)
+    return mine
+
+
+def sum_pairs(value, axis, size):
+    total = value
+    for step in range(1, size):
+        total = total + shift(value, axis, size, step)
+    return total
+
+
+def ring_gather(value, ring, me):
+    count = len(ring)
+    places = [0] * count
+    for k, member in enumerate(ring):
+        places[member] = k
+    ring_table = jnp.array(ring, jnp.int32)
+    here = jnp.array(places, jnp.int32)[me]
+    forward = [(ring[k], ring[(k + 1) % count]) for k in range(count)]
+    backward = [(ring[(k + 1) % count], ring[k]) for k in range(count)]
+    rows = value.shape[0]
+    half_rows = rows // 2
+    out = jnp.zeros((count,) + value.shape, value.dtype)
+    out = lax.dynamic_update_slice(out, value[None], (me, 0, 0))
+    ahead, behind = value[:half_rows], value[half_rows:]
+    for step in range(1, count):
+        ahead = lax.ppermute(ahead, "seq", forward)
+        behind = lax.ppermute(behind, "seq", backward)
+        source_a = ring_table[(here - step) % count]
+        source_b = ring_table[(here + step) % count]
+        out = lax.dynamic_update_slice(out, ahead[None], (source_a, 0, 0))
+        out = lax.dynamic_update_slice(out, behind[None], (source_b, half_rows, 0))
+    return out.reshape((count * rows,) + value.shape[1:])
 
 
 def shards(
+    ring,
     inputs,
     cotangent,
     pre_attention,
@@ -162,6 +251,40 @@
     out_up = query_width + 2 * key_span_width + MODEL_WIDTH + FF + quarter * hidden_local
     out_down = query_width + 2 * key_span_width + MODEL_WIDTH + 2 * FF
     tokens = groups * rows
+    down_widths = (MODEL_WIDTH, MODEL_WIDTH, MODEL_WIDTH, query_width, MODEL_WIDTH, MODEL_WIDTH, FF)
+    up_widths = (query_width, key_span_width, key_span_width, MODEL_WIDTH, FF, FF, MODEL_WIDTH)
+
+    def settle(own_down, own_up, choices_now):
+        inner = blocks * parts
+        down_chunk = own_down.shape[-1] // (groups * inner)
+        up_chunk = own_up.shape[-1] // (groups * inner)
+        both = jnp.concatenate(
+            [
+                own_down.reshape(-1, groups, inner, down_chunk),
+                own_up.reshape(-1, groups, inner, up_chunk),
+            ],
+            axis=-1,
+        )
+        reduced = lax.psum_scatter(both, ("seq", "mp"), scatter_dimension=2, tiled=True)[:, :, 0]
+        reduced = jnp.swapaxes(reduced, 0, 1)
+        mine = lax.dynamic_update_index_in_dim(
+            jnp.zeros_like(reduced), lax.dynamic_index_in_dim(reduced, own, 0, keepdims=False), own, 0
+        )
+        for step in range(1, groups):
+            send = lax.dynamic_index_in_dim(reduced, (own + step) % groups, 0, keepdims=False)
+            got = shift(send, "dp", groups, step)
+            mine = lax.dynamic_update_index_in_dim(mine, got, (own - step) % groups, 0)
+        flat = lax.axis_index(("dp", "seq", "mp"))
+        down_part = spread(
+            mine[:, :, :down_chunk], choices_now, down_widths, adapter_down.shape[0], flat * down_chunk
+        )
+        up_part = spread(
+            mine[:, :, down_chunk:], choices_now, up_widths, adapter_up.shape[0], flat * up_chunk
+        )
+        return down_part, up_part
+
+    def to_owner(partial):
+        return sum_pairs(scatter_pairs(partial, "dp", groups, own), "mp", parts)
 
     def permute(value):
         lead = value.shape[:-1]
@@ -173,25 +296,48 @@
         moved = value.reshape(lead + (blocks, groups, row_block))
         return jnp.swapaxes(moved, -3, -2).reshape(lead + (MODEL_WIDTH,))
 
-    def column_weight(weight):
-        swapped = lax.all_to_all(weight, "dp", 1, 0, tiled=True)
-        return lax.all_gather(swapped, "seq", axis=0, tiled=True)
-
-    def row_weight(weight):
-        swapped = lax.all_to_all(weight, "dp", 0, 1, tiled=True)
-        return lax.all_gather(swapped, "seq", axis=1, tiled=True)
-
-    query_full = column_weight(query_weight)
-    key_full = column_weight(key_matrix)
-    value_full = column_weight(value_matrix)
-    output_full = row_weight(output_weight)
-    gate_full = column_weight(gate_weight)
-    up_full = column_weight(up_weight)
-    down_full = row_weight(down_weight)
-
-    sources_all = lax.all_gather(inputs[:, 0], "dp", axis=1, tiled=False)
-    prefix_all = lax.all_gather(prefix_lengths[:, 0], "dp", axis=1, tiled=False)
-    choices = lax.all_gather(adapter_choice[:, 0], "dp", axis=1, tiled=False)
+    def column_block(weight, index):
+        split = weight.reshape(weight.shape[0], groups, -1)
+        return lax.dynamic_index_in_dim(split, index, 1, keepdims=False)
+
+    def row_sub(weight, index):
+        split = weight.reshape(groups, -1, weight.shape[1])
+        return lax.dynamic_index_in_dim(split, index, 0, keepdims=False).T
+
+    column_set = (query_weight, key_matrix, value_matrix)
+    row_set = (output_weight,)
+    ffw_columns = (gate_weight, up_weight)
+    ffw_rows = (down_weight,)
+
+    def swapped(columns, rows_in):
+        def block(index):
+            return jnp.concatenate(
+                [column_block(w, index) for w in columns] + [row_sub(w, index) for w in rows_in], axis=1
+            )
+
+        mine = block(own)
+        out = lax.dynamic_update_index_in_dim(jnp.zeros((groups,) + mine.shape, mine.dtype), mine, own, 0)
+        for step in range(1, groups):
+            got = shift(block((own + step) % groups), "dp", groups, step)
+            out = lax.dynamic_update_index_in_dim(out, got, (own - step) % groups, 0)
+        return out.reshape(-1, out.shape[-1])
+
+    seq_index = lax.axis_index("seq")
+    attention_full = ring_gather(swapped(column_set, row_set), ring, seq_index)
+    ffw_full = ring_gather(swapped(ffw_columns, ffw_rows), ring, seq_index)
+    cut = [0, query_local, key_local, key_local, query_local]
+    edges = np.cumsum(cut).tolist()
+    query_full = attention_full[:, edges[0] : edges[1]]
+    key_full = attention_full[:, edges[1] : edges[2]]
+    value_full = attention_full[:, edges[2] : edges[3]]
+    output_full = attention_full[:, edges[3] : edges[4]]
+    gate_full = ffw_full[:, :hidden_local]
+    up_full = ffw_full[:, hidden_local : 2 * hidden_local]
+    down_full = ffw_full[:, 2 * hidden_local :]
+
+    sources_all = jnp.swapaxes(gather_pairs(inputs[:, 0], "dp", groups, own), 0, 1)
+    prefix_all = gather_pairs(prefix_lengths[:, 0], "dp", groups, own).T
+    choices = jnp.swapaxes(gather_pairs(adapter_choice[:, 0], "dp", groups, own), 0, 1)
 
     def column_forward(inputs_low, weight, down_part, up_part):
         main = jnp.dot(permute(inputs_low).reshape(tokens, MODEL_WIDTH), weight, preferred_element_type=WIDE)
@@ -201,7 +347,9 @@
 
     def row_forward(inputs_low, weight, down_part, up_own):
         width = inputs_low.shape[-1]
-        main_part = jnp.dot(inputs_low.reshape(tokens, width), weight, preferred_element_type=WIDE)
+        main_part = jnp.einsum(
+            "tq,dq->td", inputs_low.reshape(tokens, width), weight, preferred_element_type=WIDE
+        )
         inner_part = jnp.einsum("etq,erq->etr", inputs_low, down_part, preferred_element_type=WIDE)
         both = jnp.concatenate([main_part.reshape(groups, rows, MODEL_WIDTH), inner_part], axis=-1)
         both = to_owner(both)
@@ -222,7 +370,7 @@
     def row_back(grad_all, grad_own, weight, down_part, up_part, inputs_low, inner_own):
         inner_grad = jnp.einsum("etd,erd->etr", grad_all, up_part, preferred_element_type=WIDE)
         back = jnp.einsum(
-            "td,qd->tq", permute(grad_all).reshape(tokens, MODEL_WIDTH), weight, preferred_element_type=WIDE
+            "td,dq->tq", permute(grad_all).reshape(tokens, MODEL_WIDTH), weight, preferred_element_type=WIDE
         )
         back = back.reshape(groups, rows, -1)
         back = back + jnp.einsum("etr,erq->etq", inner_grad, down_part.astype(WIDE), precision=HIGH)
@@ -295,7 +443,7 @@
         attention_out, inner_output = row_forward(head_stack, output_full, down_output, up_output_own)
         middle = source + normalize(attention_out, post_attention)
         normed_ffw_own = normalize(middle, pre_feedforward).astype(NARROW)
-        normed_ffw = lax.all_gather(normed_ffw_own, "dp", axis=0, tiled=False)
+        normed_ffw = gather_pairs(normed_ffw_own, "dp", groups, own)
         gate, inner_gate = column_forward(normed_ffw, gate_full, down_gate, up_gate)
         upper, inner_upper = column_forward(normed_ffw, up_full, down_up, up_upper)
         hidden = activate(gate, upper).astype(NARROW)
@@ -306,7 +454,7 @@
         grad_up = jnp.zeros((groups,) + adapter_up.shape[1:], WIDE)
         seed_grad = cotangent[batch, 0].astype(WIDE)
         grad_ffw_own = normalize_back(ffw_out, post_feedforward, seed_grad).astype(NARROW)
-        grad_ffw = lax.all_gather(grad_ffw_own, "dp", axis=0, tiled=False)
+        grad_ffw = gather_pairs(grad_ffw_own, "dp", groups, own)
         grad_hidden, piece_down, piece_up = row_back(
             grad_ffw, grad_ffw_own, down_full, down_down, up_down, hidden, inner_down
         )
@@ -329,7 +477,7 @@
         grad_normed_ffw = to_owner(back_gate + back_upper)
         grad_middle = seed_grad + normalize_back(middle, pre_feedforward, grad_normed_ffw)
         grad_attention_own = normalize_back(attention_out, post_attention, grad_middle).astype(NARROW)
-        grad_attention = lax.all_gather(grad_attention_own, "dp", axis=0, tiled=False)
+        grad_attention = gather_pairs(grad_attention_own, "dp", groups, own)
         grad_heads, piece_down, piece_up = row_back(
             grad_attention,
             grad_attention_own,
@@ -399,23 +547,32 @@
         grad_down = place(grad_down, piece_down, 2 * MODEL_WIDTH)
         grad_up = place(grad_up, piece_up, out_value)
         grad_normed = to_owner(back_query + back_key + back_value)
-        down_list.append(grad_down)
-        up_list.append(grad_up)
+        own_down = scatter_pairs(grad_down, "dp", groups, own)
+        own_up = scatter_pairs(grad_up, "dp", groups, own)
+        down_part, up_part = settle(own_down, own_up, slots)
+        down_list.append(down_part)
+        up_list.append(up_part)
         input_grads.append(
             (grad_middle + normalize_back(source, pre_attention, grad_normed)).astype(NARROW)
         )
-    down_widths = (MODEL_WIDTH, MODEL_WIDTH, MODEL_WIDTH, query_width, MODEL_WIDTH, MODEL_WIDTH, FF)
-    up_widths = (query_width, key_span_width, key_span_width, MODEL_WIDTH, FF, FF, MODEL_WIDTH)
-    down_total = settle(jnp.stack(down_list), choices, down_widths, adapter_down.shape[0])
-    up_total = settle(jnp.stack(up_list), choices, up_widths, adapter_up.shape[0])
+    down_total = down_list[0]
+    up_total = up_list[0]
+    for extra in range(1, len(down_list)):
+        down_total = down_total + down_list[extra]
+        up_total = up_total + up_list[extra]
     outputs = jnp.stack(results)[:, None]
     input_gradient = jnp.stack(input_grads)[:, None]
     return (outputs, input_gradient, down_total, up_total)
 
 
 def solution(mesh):
+    ring = ring_order(mesh)
+
+    def body(*args):
+        return shards(ring, *args)
+
     return jax.shard_map(
-        shards,
+        body,
         mesh=mesh,
         in_specs=(
             P(None, "dp", "seq", None),

time: 1940 us -> 1480 us (0.76)
  waiting for transfers between devices: 1190 us -> 672 us
  blocking collectives: 116 us -> 0 us
  starting transfers between devices: 6.81 us -> 65.4 us
  local copies, waits for them, and re-layouts: 279 us -> 321 us
  between operations: 80.2 us -> 115 us
    all_gather x14 -> x0, waiting for transfers between devices: 553 us -> none  [the longest x5 312 us: column_weight(): return lax.all_gather(swapped, 'seq', axis=0, tiled=True)]
    ppermute x0 -> x61, waiting for transfers between devices: none -> 474 us  [the longest x14 242 us: ring_gather(): ahead = lax.ppermute(ahead, 'seq', forward)]
    reduce_scatter x10 -> x2, waiting for transfers between devices: 337 us -> 111 us  [settle(): lax.psum_scatter(both, ('seq', 'mp'), scatter_dimension=2, tiled=True)]
    all_to_all x6 -> x0, blocking collectives: 103 us -> none  [the longest x4 79.6 us: column_weight(): swapped = lax.all_to_all(weight, 'dp', 1, 0, tiled=True)]
    all_gather x2, waiting for transfers between devices: 85.1 us -> 0.01 us  [shards(): lax.all_gather(jnp.stack([rotated_keys, values_low]), 'seq', axis=2, tile...]
    gather x6 -> x0, local copies, waits for them, and re-layouts: 71.3 us -> none  [settle(): jnp.take_along_axis(choices[:, :, None, :], jnp.broadcast_to(seg[None, No...]
    ppermute x0 -> x61, starting transfers between devices: none -> 64.6 us  [the longest x33 32.6 us: shift(): lax.ppermute(value, axis, [(a, (a + step) % size) for a in range(size)])]
    psum x4 -> x0, waiting for transfers between devices: 63.9 us -> none  [to_owner(): return lax.psum(mine, 'mp')]
  transfers between devices with their start and end apart: 33 -> 67, of which waited for: 24 -> 33; matrix products, arithmetic and copies ran while one was open for 23% -> 29% of each run, Pallas kernels for 0% -> 0%
where the time goes in v3:
time: 1480 us; the launch traced here: 1460 us
  waiting for transfers between devices  672 us (45%)
  local copies, waits for them, and re-layouts  321 us (22%)
  matrix products  211 us (14%)
  between operations  115 us (8%)
  other arithmetic  79.9 us (5%)
  starting transfers between devices  65.4 us (4%)
    ppermute x14, waiting for transfers between devices, ring_gather(): ahead = lax.ppermute(ahead, 'seq', forward)  242 us
    ppermute x33, waiting for transfers between devices, shift(): lax.ppermute(value, axis, [(a, (a + step) % size) for a in range(size)])  222 us
    reduce_scatter x2, waiting for transfers between devices, settle(): lax.psum_scatter(both, ('seq', 'mp'), scatter_dimension=2, tiled=True)  111 us
    reduce_scatter x2, waiting for transfers between devices, shards(): lax.psum_scatter(jnp.stack([grad_key_part.reshape(groups, length, key_loc...  87.1 us
    reshape x14, local copies, waits for them, and re-layouts, unpermute(): return jnp.swapaxes(moved, -3, -2).reshape(lead + (MODEL_WIDTH,))  44 us
    dot_general x10, matrix products, column_forward(): jnp.dot(permute(inputs_low).reshape(tokens, MODEL_WIDTH), weight, preferr...  40.3 us
    ppermute x33, starting transfers between devices, shift(): lax.ppermute(value, axis, [(a, (a + step) % size) for a in range(size)])  32.6 us
    unnamed x713, local copies, waits for them, and re-layouts  31.5 us
  transfers between devices with their start and end apart: 67, of which 33 were waited for; matrix products, arithmetic and copies ran while one was open for 29% of the time, Pallas kernels for 0%

profile of v3, /device:TPU:0, one launch (start us, length us, event | category | flops | bytes accessed | tf_op | source)
XLA Modules:
  0.0 1464.0 jit_solution(15932161223860392351)
XLA Ops:
  226.1 8.6 collective-permute-done.10
  236.9 9.8 collective-permute-done.12
  268.9 10.9 broadcast_in_dim.645
  295.8 39.6 %collective-permute-done.22 = bf16[144,6912]{1,0:T(8,128)(2,1)} collective-permute-done((bf16[144,6912]{1,0:T(8,128)(2,1)}, bf16[144,6912]{1,0:T(8,128)(2,1)}, u32[]{:S(2)}, u32[]{:S(2)}) %collective-permute-start.22) | collective-permute-done | bytes 1990688 | tf_op jit(solution)/shard_map/ppermute | solution.py:190
  344.2 62.0 %collective-permute-done.24 = bf16[144,6912]{1,0:T(8,128)(2,1)} collective-permute-done((bf16[144,6912]{1,0:T(8,128)(2,1)}, bf16[144,6912]{1,0:T(8,128)(2,1)}, u32[]{:S(2)}, u32[]{:S(2)}) %collective-permute-start.24) | collective-permute-done | bytes 1990688 | tf_op jit(solution)/shard_map/ppermute | solution.py:190
  438.5 11.0 collective-permute-done.26
  494.3 9.6 collective-permute-done.40
  513.0 14.5 collective-permute-done.30
  536.0 35.6 %collective-permute-done.32 = bf16[144,6912]{1,0:T(8,128)(2,1)S(1)} collective-permute-done((bf16[144,6912]{1,0:T(8,128)(2,1)}, bf16[144,6912]{1,0:T(8,128)(2,1)S(1)}, u32[]{:S(2)}, u32[]{:S(2)}) %collective-permute-start.32) | collective-permute-done | bytes 1990688 | tf_op jit(solution)/shard_map/ppermute | solution.py:190
  579.0 35.7 %collective-permute-done.34 = bf16[144,6912]{1,0:T(8,128)(2,1)S(1)} collective-permute-done((bf16[144,6912]{1,0:T(8,128)(2,1)S(1)}, bf16[144,6912]{1,0:T(8,128)(2,1)S(1)}, u32[]{:S(2)}, u32[]{:S(2)}) %collective-permute-start.34) | collective-permute-done | bytes 1990688 | tf_op jit(solution)/shard_map/ppermute | solution.py:190
  628.4 9.9 multiply_convert_fusion.4
  650.8 9.9 multiply_convert_fusion.2
  685.4 16.8 %collective-permute-done.36 = f32[128,2320]{0,1:T(8,128)} collective-permute-done((f32[128,2320]{0,1:T(8,128)}, f32[128,2320]{0,1:T(8,128)}, u32[]{:S(2)}, u32[]{:S(2)}) %collective-permute-start.36) | collective-permute-done | bytes 1187872 | tf_op jit(solution)/shard_map/ppermute | solution.py:148
  703.9 19.8 %collective-permute-done.41 = f32[128,2320]{0,1:T(8,128)} collective-permute-done((f32[128,2320]{0,1:T(8,128)}, f32[128,2320]{0,1:T(8,128)}, u32[]{:S(2)}, u32[]{:S(2)}) %collective-permute-start.41) | collective-permute-done | bytes 1187872 | tf_op jit(solution)/shard_map/ppermute | solution.py:148
  725.3 15.8 %fusion.349 = (bf16[2304,2304]{1,0:T(8,128)(2,1)}, bf16[2304,2304]{1,0:T(8,128)(2,1)}) fusion(bf16[2304,6912]{1,0:T(8,128)(2,1)} %bitcast.987), kind=kLoop, calls=%fused_computation.780 | loop fusion | bytes 42467328 | tf_op jit(solution)/shard_map/slice | solution.py:334
  860.7 9.7 collective-permute-done.50
  872.0 21.8 %collective-permute-done.44 = f32[128,2304]{1,0:T(8,128)S(1)} collective-permute-done((f32[128,2304]{1,0:T(8,128)S(1)}, f32[128,2304]{1,0:T(8,128)S(1)}, u32[]{:S(2)}, u32[]{:S(2)}) %collective-permute-start.44) | collective-permute-done | bytes 1179680 | tf_op jit(solution)/shard_map/ppermute | solution.py:148
  902.2 13.4 collective-permute-done.52
  933.2 11.8 collective-permute-done.46
  1021.0 87.1 %reduce-scatter.5.cloned.1.call-done = f32[2,2,128,256]{3,2,1,0:T(8,128)} async-done(((f32[2,2,1024,256]{3,2,1,0:T(8,128)}), f32[2,2,128,256]{3,2,1,0:T(8,128)}) %reduce-scatter.5.cloned.1.call-update) | async-done | bytes 524304 | tf_op jit(solution)/shard_map/reduce_scatter | solution.py:509
  1147.9 13.4 copy.805
  1185.4 97.6 %collective-permute-done.53 = f32[128,2304]{1,0:T(8,128)} collective-permute-done((f32[128,2304]{1,0:T(8,128)}, f32[128,2304]{1,0:T(8,128)}, u32[]{:S(2)}, u32[]{:S(2)}) %collective-permute-start.53) | collective-permute-done | bytes 1179680 | tf_op jit(solution)/shard_map/ppermute | solution.py:148
  1335.7 43.3 %reduce-scatter.11.cloned.1.call-done = f32[16,2,1,1560]{3,0,1,2:T(8,128)} async-done(((f32[16,2,16,1560]{3,0,1,2:T(8,128)}), f32[16,2,1,1560]{3,0,1,2:T(8,128)}) %reduce-scatter.11.cloned.1.call-update) | async-done | bytes 199696 | tf_op jit(solution)/shard_map/reduce_scatter | solution.py:268
  1381.4 67.8 %reduce-scatter.9.cloned.1.call-done = f32[16,2,1,1560]{3,0,1,2:T(8,128)} async-done(((f32[16,2,16,1560]{3,0,1,2:T(8,128)}), f32[16,2,1,1560]{3,0,1,2:T(8,128)}) %reduce-scatter.9.cloned.1.call-update) | async-done | bytes 199696 | tf_op jit(solution)/shard_map/reduce_scatter | solution.py:268
  (1258 shorter events, 674.0 us)
Async XLA Ops:
  7.2 407.6 %all-gather.5.cloned.1.call-start = ((), (), s32[]{:S(2)}) async-start(), calls=%async_computation.5 | async-start | bytes 2359296 | tf_op jit(solution)/shard_map/all_gather | solution.py:421
  30.4 185.4 %collective-permute-start.21 = (bf16[144,6912]{1,0:T(8,128)(2,1)}, bf16[144,6912]{1,0:T(8,128)(2,1)}, u32[]{:S(2)}, u32[]{:S(2)}) collective-permute-start(bf16[144,6912]{1,0:T(8,128)(2,1)} %pad_maximum_fusion.4), channel_id=1, source_target_pairs={{0,16},{16,0},{1,17},{17,1},{2,18},{18,2},{3,19},{19,3},{4,20},{20... | collective-permute-start | bytes 5971976 | tf_op jit(solution)/shard_map/ppermute | solution.py:148
  39.5 138.2 %collective-permute-start.1 = (bf16[144,1536]{1,0:T(8,128)(2,1)}, bf16[144,1536]{1,0:T(8,128)(2,1)}, u32[]{:S(2)}, u32[]{:S(2)}) collective-permute-start(bf16[144,1536]{1,0:T(8,128)(2,1)} %pad_maximum_fusion.5), channel_id=1, source_target_pairs={{0,16},{16,0},{1,17},{17,1},{2,18},{18,2},{3,19},{19,3},{4,20},{20... | collective-permute-start | bytes 1327112 | tf_op jit(solution)/shard_map/ppermute | solution.py:148
  39.5 76.2 %collective-permute-start.16 = (s32[2,7]{1,0:T(2,128)S(1)}, s32[2,7]{1,0:T(2,128)}, u32[]{:S(2)}, u32[]{:S(2)}) collective-permute-start(s32[2,7]{1,0:T(2,128)S(1)} %bitcast.1118), channel_id=1, source_target_pairs={{0,16},{16,0},{1,17},{17,1},{2,18},{18,2},{3,19},{19,3},{4,20},{20... | collective-permute-start | bytes 176 | tf_op jit(solution)/shard_map/ppermute | solution.py:148
  42.9 149.5 %collective-permute-start = (bf16[2,128,2304]{1,2,0:T(8,128)(2,1)}, bf16[2,128,2304]{1,2,0:T(8,128)(2,1)}, u32[]{:S(2)}, u32[]{:S(2)}) collective-permute-start(bf16[2,128,2304]{1,2,0:T(8,128)(2,1)} %bitcast.1058), channel_id=1, source_target_pairs={{0,16},{16,0},{1,17},{17,1},{2,18},{18,2},{3,19},{19,3},{4,20},{20... | collective-permute-start | bytes 3538952 | tf_op jit(solution)/shard_map/ppermute | solution.py:148
  42.9 69.0 %collective-permute-start.17 = (s32[2]{0:T(128)}, s32[2]{0:T(128)}, u32[]{:S(2)}, u32[]{:S(2)}) collective-permute-start(s32[2]{0:T(128)} %bitcast.79), channel_id=1, source_target_pairs={{0,16},{16,0},{1,17},{17,1},{2,18},{18,2},{3,19},{19,3},{4,20},{20... | collective-permute-start | bytes 32 | tf_op jit(solution)/shard_map/ppermute | solution.py:148
  261.9 165.9 %all-gather.3.cloned.1.call-start = ((), (), s32[]{:S(2)}) async-start(), calls=%async_computation.4 | async-start | bytes 2359296 | tf_op jit(solution)/shard_map/all_gather | solution.py:421
  266.5 68.9 %collective-permute-start.22 = (bf16[144,6912]{1,0:T(8,128)(2,1)}, bf16[144,6912]{1,0:T(8,128)(2,1)}, u32[]{:S(2)}, u32[]{:S(2)}) collective-permute-start(bf16[144,6912]{1,0:T(8,128)(2,1)} %get-tuple-element.127), channel_id=1, source_target_pairs={{0,4},{4,8},{8,12},{12,14},{14,10},{10,6},{6,2},{2,0},{1,5},{5,9},... | collective-permute-start | bytes 5971976 | tf_op jit(solution)/shard_map/ppermute | solution.py:190
  268.1 72.8 %collective-permute-start.23 = (bf16[144,6912]{1,0:T(8,128)(2,1)}, bf16[144,6912]{1,0:T(8,128)(2,1)}, u32[]{:S(2)}, u32[]{:S(2)}) collective-permute-start(bf16[144,6912]{1,0:T(8,128)(2,1)} %get-tuple-element.126), channel_id=1, source_target_pairs={{4,0},{8,4},{12,8},{14,12},{10,14},{6,10},{2,6},{0,2},{5,1},{9,5},... | collective-permute-start | bytes 5971976 | tf_op jit(solution)/shard_map/ppermute | solution.py:191
  294.9 724.3 %reduce-scatter.7.cloned.1.call-start = ((), (), s32[]{:S(2)}) async-start(), calls=%async_computation.7 | async-start | bytes 4718592 | tf_op jit(solution)/shard_map/reduce_scatter | solution.py:509
  335.4 70.8 %collective-permute-start.24 = (bf16[144,6912]{1,0:T(8,128)(2,1)}, bf16[144,6912]{1,0:T(8,128)(2,1)}, u32[]{:S(2)}, u32[]{:S(2)}) collective-permute-start(bf16[144,6912]{1,0:T(8,128)(2,1)} %collective-permute-done.22), channel_id=1, source_target_pairs={{0,4},{4,8},{8,12},{12,14},{14,10},{10,6},{6,2},{2,0},{1,5},{5,9},... | collective-permute-start | bytes 5971976 | tf_op jit(solution)/shard_map/ppermute | solution.py:190
  340.8 70.8 %collective-permute-start.25 = (bf16[144,6912]{1,0:T(8,128)(2,1)}, bf16[144,6912]{1,0:T(8,128)(2,1)}, u32[]{:S(2)}, u32[]{:S(2)}) collective-permute-start(bf16[144,6912]{1,0:T(8,128)(2,1)} %collective-permute-done.23), channel_id=1, source_target_pairs={{4,0},{8,4},{12,8},{14,12},{10,14},{6,10},{2,6},{0,2},{5,1},{9,5},... | collective-permute-start | bytes 5971976 | tf_op jit(solution)/shard_map/ppermute | solution.py:191
  482.5 45.1 %collective-permute-start.30 = (bf16[144,6912]{1,0:T(8,128)(2,1)}, bf16[144,6912]{1,0:T(8,128)(2,1)}, u32[]{:S(2)}, u32[]{:S(2)}) collective-permute-start(bf16[144,6912]{1,0:T(8,128)(2,1)} %collective-permute-done.28), channel_id=1, source_target_pairs={{0,4},{4,8},{8,12},{12,14},{14,10},{10,6},{6,2},{2,0},{1,5},{5,9},... | collective-permute-start | bytes 5971976 | tf_op jit(solution)/shard_map/ppermute | solution.py:190
  487.8 45.2 %collective-permute-start.31 = (bf16[144,6912]{1,0:T(8,128)(2,1)}, bf16[144,6912]{1,0:T(8,128)(2,1)}, u32[]{:S(2)}, u32[]{:S(2)}) collective-permute-start(bf16[144,6912]{1,0:T(8,128)(2,1)} %collective-permute-done.29), channel_id=1, source_target_pairs={{4,0},{8,4},{12,8},{14,12},{10,14},{6,10},{2,6},{0,2},{5,1},{9,5},... | collective-permute-start | bytes 5971976 | tf_op jit(solution)/shard_map/ppermute | solution.py:191
  676.9 46.9 %collective-permute-start.41 = (f32[128,2320]{0,1:T(8,128)}, f32[128,2320]{0,1:T(8,128)}, u32[]{:S(2)}, u32[]{:S(2)}) collective-permute-start(f32[128,2320]{0,1:T(8,128)} %bitcast.1091), channel_id=1, source_target_pairs={{0,16},{16,0},{1,17},{17,1},{2,18},{18,2},{3,19},{19,3},{4,20},{20... | collective-permute-start | bytes 3563528 | tf_op jit(solution)/shard_map/ppermute | solution.py:148
  928.5 179.5 %reduce-scatter.5.cloned.1.call-start = ((), (), s32[]{:S(2)}) async-start(), calls=%async_computation.6 | async-start | bytes 4718592 | tf_op jit(solution)/shard_map/reduce_scatter | solution.py:509
  957.3 421.7 %reduce-scatter.11.cloned.1.call-start = ((), (), s32[]{:S(2)}) async-start(), calls=%async_computation.9 | async-start | bytes 3620864 | tf_op jit(solution)/shard_map/reduce_scatter | solution.py:268
  1118.4 168.6 %collective-permute-start.58 = (f32[16,22784]{1,0:T(8,128)}, f32[16,22784]{1,0:T(8,128)}, u32[]{:S(2)}, u32[]{:S(2)}) collective-permute-start(f32[16,22784]{1,0:T(8,128)} %dynamic-slice_bitcast_fusion.2), channel_id=1, source_target_pairs={{0,16},{16,0},{1,17},{17,1},{2,18},{18,2},{3,19},{19,3},{4,20},{20... | collective-permute-start | bytes 4374536 | tf_op jit(solution)/shard_map/ppermute | solution.py:148
  1124.2 177.5 %collective-permute-start.59 = (f32[16,27136]{1,0:T(8,128)}, f32[16,27136]{1,0:T(8,128)}, u32[]{:S(2)}, u32[]{:S(2)}) collective-permute-start(f32[16,27136]{1,0:T(8,128)} %dynamic-slice_bitcast_fusion), channel_id=1, source_target_pairs={{0,16},{16,0},{1,17},{17,1},{2,18},{18,2},{3,19},{19,3},{4,20},{20... | collective-permute-start | bytes 5210120 | tf_op jit(solution)/shard_map/ppermute | solution.py:148
  1132.3 158.1 %collective-permute-start.55 = (f32[16,22784]{1,0:T(8,128)}, f32[16,22784]{1,0:T(8,128)}, u32[]{:S(2)}, u32[]{:S(2)}) collective-permute-start(f32[16,22784]{1,0:T(8,128)} %dynamic-slice_bitcast_fusion.3), channel_id=1, source_target_pairs={{0,16},{16,0},{1,17},{17,1},{2,18},{18,2},{3,19},{19,3},{4,20},{20... | collective-permute-start | bytes 4374536 | tf_op jit(solution)/shard_map/ppermute | solution.py:148
  1138.0 174.3 %collective-permute-start.56 = (f32[16,27136]{1,0:T(8,128)}, f32[16,27136]{1,0:T(8,128)}, u32[]{:S(2)}, u32[]{:S(2)}) collective-permute-start(f32[16,27136]{1,0:T(8,128)} %dynamic-slice_bitcast_fusion.1), channel_id=1, source_target_pairs={{0,16},{16,0},{1,17},{17,1},{2,18},{18,2},{3,19},{19,3},{4,20},{20... | collective-permute-start | bytes 5210120 | tf_op jit(solution)/shard_map/ppermute | solution.py:148
  1167.0 116.1 %collective-permute-start.53 = (f32[128,2304]{1,0:T(8,128)}, f32[128,2304]{1,0:T(8,128)}, u32[]{:S(2)}, u32[]{:S(2)}) collective-permute-start(f32[128,2304]{1,0:T(8,128)} %dynamic-slice_bitcast_fusion.4), channel_id=1, source_target_pairs={{0,16},{16,0},{1,17},{17,1},{2,18},{18,2},{3,19},{19,3},{4,20},{20... | collective-permute-start | bytes 3538952 | tf_op jit(solution)/shard_map/ppermute | solution.py:148
  1312.1 137.1 %reduce-scatter.9.cloned.1.call-start = ((), (), s32[]{:S(2)}) async-start(), calls=%async_computation.8 | async-start | bytes 3620864 | tf_op jit(solution)/shard_map/reduce_scatter | solution.py:268
  1379.9 73.4 %collective-permute-start.60 = (f32[16,1560]{1,0:T(8,128)S(1)}, f32[16,1560]{1,0:T(8,128)S(1)}, u32[]{:S(2)}, u32[]{:S(2)}) collective-permute-start(f32[16,1560]{1,0:T(8,128)S(1)} %dynamic-slice_bitcast_fusion.8), channel_id=1, source_target_pairs={{0,16},{16,0},{1,17},{17,1},{2,18},{18,2},{3,19},{19,3},{4,20},{20... | collective-permute-start | bytes 299528 | tf_op jit(solution)/shard_map/ppermute | solution.py:148
  (391 other events, 4889.3 us)
Sparse Core Ops, SparseCore 0:
  262.1 65.8 all-gather.4
  330.8 69.6 all-gather.2
  928.7 87.5 reduce-scatter.6
  1019.7 88.3 reduce-scatter.4
  1312.2 66.7 reduce-scatter.10
  1382.7 66.3 reduce-scatter.8

commit v4 on v3

--- a/solution.py
+++ b/solution.py
@@ -58,7 +58,9 @@
 
 
 def pick(table, index, start_index, size):
-    return lax.dynamic_slice(table, (index, 0, start_index), (1, table.shape[1], size))[0]
+    window = lax.dynamic_slice_in_dim(table, start_index, size, axis=2)
+    hit = jnp.arange(table.shape[0], dtype=jnp.int32) == index
+    return jnp.sum(jnp.where(hit[:, None, None], window.astype(WIDE), 0.0), axis=0).astype(table.dtype)
 
 
 def picks(table, slots, start_index, size):
@@ -144,6 +146,10 @@
     return [lookup[tuple(point)] for point in order]
 
 
+def wrap(index, step, size):
+    return jnp.array([(a + step) % size for a in range(size)], jnp.int32)[index]
+
+
 def shift(value, axis, size, step):
     return lax.ppermute(value, axis, [(a, (a + step) % size) for a in range(size)])
 
@@ -153,14 +159,14 @@
     out = lax.dynamic_update_index_in_dim(out, value, me, 0)
     for step in range(1, size):
         got = shift(value, axis, size, step)
-        out = lax.dynamic_update_index_in_dim(out, got, (me - step) % size, 0)
+        out = lax.dynamic_update_index_in_dim(out, got, wrap(me, -step, size), 0)
     return out
 
 
 def scatter_pairs(partial, axis, size, me):
     mine = lax.dynamic_index_in_dim(partial, me, 0, keepdims=False)
     for step in range(1, size):
-        send = lax.dynamic_index_in_dim(partial, (me + step) % size, 0, keepdims=False)
+        send = lax.dynamic_index_in_dim(partial, wrap(me, step, size), 0, keepdims=False)
         mine = mine + shift(send, axis, size, step)
     return mine
 
@@ -177,8 +183,12 @@
     places = [0] * count
     for k, member in enumerate(ring):
         places[member] = k
-    ring_table = jnp.array(ring, jnp.int32)
-    here = jnp.array(places, jnp.int32)[me]
+    ahead_from = jnp.array(
+        [[ring[(places[j] - s) % count] for s in range(count)] for j in range(count)], jnp.int32
+    )[me]
+    behind_from = jnp.array(
+        [[ring[(places[j] + s) % count] for s in range(count)] for j in range(count)], jnp.int32
+    )[me]
     forward = [(ring[k], ring[(k + 1) % count]) for k in range(count)]
     backward = [(ring[(k + 1) % count], ring[k]) for k in range(count)]
     rows = value.shape[0]
@@ -189,8 +199,8 @@
     for step in range(1, count):
         ahead = lax.ppermute(ahead, "seq", forward)
         behind = lax.ppermute(behind, "seq", backward)
-        source_a = ring_table[(here - step) % count]
-        source_b = ring_table[(here + step) % count]
+        source_a = ahead_from[step]
+        source_b = behind_from[step]
         out = lax.dynamic_update_slice(out, ahead[None], (source_a, 0, 0))
         out = lax.dynamic_update_slice(out, behind[None], (source_b, half_rows, 0))
     return out.reshape((count * rows,) + value.shape[1:])
@@ -271,9 +281,9 @@
             jnp.zeros_like(reduced), lax.dynamic_index_in_dim(reduced, own, 0, keepdims=False), own, 0
         )
         for step in range(1, groups):
-            send = lax.dynamic_index_in_dim(reduced, (own + step) % groups, 0, keepdims=False)
+            send = lax.dynamic_index_in_dim(reduced, wrap(own, step, groups), 0, keepdims=False)
             got = shift(send, "dp", groups, step)
-            mine = lax.dynamic_update_index_in_dim(mine, got, (own - step) % groups, 0)
+            mine = lax.dynamic_update_index_in_dim(mine, got, wrap(own, -step, groups), 0)
         flat = lax.axis_index(("dp", "seq", "mp"))
         down_part = spread(
             mine[:, :, :down_chunk], choices_now, down_widths, adapter_down.shape[0], flat * down_chunk
@@ -318,8 +328,8 @@
         mine = block(own)
         out = lax.dynamic_update_index_in_dim(jnp.zeros((groups,) + mine.shape, mine.dtype), mine, own, 0)
         for step in range(1, groups):
-            got = shift(block((own + step) % groups), "dp", groups, step)
-            out = lax.dynamic_update_index_in_dim(out, got, (own - step) % groups, 0)
+            got = shift(block(wrap(own, step, groups)), "dp", groups, step)
+            out = lax.dynamic_update_index_in_dim(out, got, wrap(own, -step, groups), 0)
         return out.reshape(-1, out.shape[-1])
 
     seq_index = lax.axis_index("seq")

time: 1480 us -> 1430 us (0.966)
  between operations: 115 us -> 46.8 us
  other arithmetic: 79.9 us -> 121 us
    reduce_sum x0 -> x8, other arithmetic: none -> 22 us  [pick(): jnp.sum(jnp.where(hit[:, None, None], window.astype(WIDE), 0.0), axis=0)]
    eq x0 -> x18, other arithmetic: none -> 20 us  [pick(): hit = jnp.arange(table.shape[0], dtype=jnp.int32) == index]
  transfers between devices with their start and end apart: 67 -> 67, of which waited for: 33 -> 32; matrix products, arithmetic and copies ran while one was open for 29% -> 34% of each run, Pallas kernels for 0% -> 0%
where the time goes in v4:
time: 1430 us; the launch traced here: 1420 us
  waiting for transfers between devices  667 us (47%)
  local copies, waits for them, and re-layouts  310 us (22%)
  matrix products  215 us (15%)
  other arithmetic  121 us (8%)
  starting transfers between devices  62 us (4%)
  between operations  46.8 us (3%)
    ppermute x14, waiting for transfers between devices, ring_gather(): ahead = lax.ppermute(ahead, 'seq', forward)  239 us
    ppermute x33, waiting for transfers between devices, shift(): lax.ppermute(value, axis, [(a, (a + step) % size) for a in range(size)])  221 us
    reduce_scatter x2, waiting for transfers between devices, settle(): lax.psum_scatter(both, ('seq', 'mp'), scatter_dimension=2, tiled=True)  111 us
    reduce_scatter x2, waiting for transfers between devices, shards(): lax.psum_scatter(jnp.stack([grad_key_part.reshape(groups, length, key_loc...  87.1 us
    reshape x14, local copies, waits for them, and re-layouts, unpermute(): return jnp.swapaxes(moved, -3, -2).reshape(lead + (MODEL_WIDTH,))  45 us
    dot_general x10, matrix products, column_forward(): jnp.dot(permute(inputs_low).reshape(tokens, MODEL_WIDTH), weight, preferr...  42.2 us
    unnamed x713, local copies, waits for them, and re-layouts  31.7 us
    ppermute x33, starting transfers between devices, shift(): lax.ppermute(value, axis, [(a, (a + step) % size) for a in range(size)])  28.8 us
  transfers between devices with their start and end apart: 67, of which 32 were waited for; matrix products, arithmetic and copies ran while one was open for 34% of the time, Pallas kernels for 0%

profile of v4, /device:TPU:0, one launch (start us, length us, event | category | flops | bytes accessed | tf_op | source)
XLA Modules:
  0.0 1420.7 jit_solution(8879984016065139433)
XLA Ops:
  90.4 20.9 %collective-permute-done.17 = s32[2]{0:T(128)} collective-permute-done((s32[2]{0:T(128)}, s32[2]{0:T(128)}, u32[]{:S(2)}, u32[]{:S(2)}) %collective-permute-start.17) | collective-permute-done | bytes 40 | tf_op jit(solution)/shard_map/ppermute | solution.py:154
  202.5 8.7 collective-permute-done.10
  213.3 9.8 collective-permute-done.12
  245.5 10.9 broadcast_in_dim.1077
  272.3 39.5 %collective-permute-done.22 = bf16[144,6912]{1,0:T(8,128)(2,1)} collective-permute-done((bf16[144,6912]{1,0:T(8,128)(2,1)}, bf16[144,6912]{1,0:T(8,128)(2,1)}, u32[]{:S(2)}, u32[]{:S(2)}) %collective-permute-start.22) | collective-permute-done | bytes 1990688 | tf_op jit(solution)/shard_map/ppermute | solution.py:200
  320.7 61.9 %collective-permute-done.24 = bf16[144,6912]{1,0:T(8,128)(2,1)} collective-permute-done((bf16[144,6912]{1,0:T(8,128)(2,1)}, bf16[144,6912]{1,0:T(8,128)(2,1)}, u32[]{:S(2)}, u32[]{:S(2)}) %collective-permute-start.24) | collective-permute-done | bytes 1990688 | tf_op jit(solution)/shard_map/ppermute | solution.py:200
  414.8 11.1 collective-permute-done.26
  471.4 9.6 collective-permute-done.40
  493.3 11.4 collective-permute-done.30
  513.4 35.3 %collective-permute-done.32 = bf16[144,6912]{1,0:T(8,128)(2,1)S(1)} collective-permute-done((bf16[144,6912]{1,0:T(8,128)(2,1)}, bf16[144,6912]{1,0:T(8,128)(2,1)S(1)}, u32[]{:S(2)}, u32[]{:S(2)}) %collective-permute-start.32) | collective-permute-done | bytes 1990688 | tf_op jit(solution)/shard_map/ppermute | solution.py:200
  556.2 35.6 %collective-permute-done.34 = bf16[144,6912]{1,0:T(8,128)(2,1)S(1)} collective-permute-done((bf16[144,6912]{1,0:T(8,128)(2,1)S(1)}, bf16[144,6912]{1,0:T(8,128)(2,1)S(1)}, u32[]{:S(2)}, u32[]{:S(2)}) %collective-permute-start.34) | collective-permute-done | bytes 1990688 | tf_op jit(solution)/shard_map/ppermute | solution.py:200
  605.2 9.8 multiply_convert_fusion.4
  635.7 9.8 multiply_convert_fusion.2
  662.0 20.0 %collective-permute-done.41 = f32[128,2320]{0,1:T(8,128)} collective-permute-done((f32[128,2320]{0,1:T(8,128)}, f32[128,2320]{0,1:T(8,128)}, u32[]{:S(2)}, u32[]{:S(2)}) %collective-permute-start.41) | collective-permute-done | bytes 1187872 | tf_op jit(solution)/shard_map/ppermute | solution.py:154
  683.5 16.1 %fusion.397 = (bf16[2304,2304]{1,0:T(8,128)(2,1)}, bf16[2304,2304]{1,0:T(8,128)(2,1)}) fusion(bf16[2304,6912]{1,0:T(8,128)(2,1)} %bitcast.1128), kind=kLoop, calls=%fused_computation.922 | loop fusion | bytes 42467328 | tf_op jit(solution)/shard_map/slice | solution.py:344
  816.6 10.8 collective-permute-done.50
  828.9 21.8 %collective-permute-done.44 = f32[128,2304]{1,0:T(8,128)S(1)} collective-permute-done((f32[128,2304]{1,0:T(8,128)S(1)}, f32[128,2304]{1,0:T(8,128)S(1)}, u32[]{:S(2)}, u32[]{:S(2)}) %collective-permute-start.44) | collective-permute-done | bytes 1179680 | tf_op jit(solution)/shard_map/ppermute | solution.py:154
  858.1 14.4 %collective-permute-done.52 = bf16[128,2304]{1,0:T(8,128)(2,1)} collective-permute-done((bf16[128,2304]{1,0:T(8,128)(2,1)S(1)}, bf16[128,2304]{1,0:T(8,128)(2,1)}, u32[]{:S(2)}, u32[]{:S(2)}) %collective-permute-start.52) | collective-permute-done | bytes 589856 | tf_op jit(solution)/shard_map/ppermute | solution.py:154
  889.1 12.7 collective-permute-done.46
  977.9 87.1 %reduce-scatter.5.cloned.1.call-done = f32[2,2,128,256]{3,2,1,0:T(8,128)} async-done(((f32[2,2,1024,256]{3,2,1,0:T(8,128)}), f32[2,2,128,256]{3,2,1,0:T(8,128)}) %reduce-scatter.5.cloned.1.call-update) | async-done | bytes 524304 | tf_op jit(solution)/shard_map/reduce_scatter | solution.py:519
  1104.8 13.5 copy.834
  1142.3 97.7 %collective-permute-done.53 = f32[128,2304]{1,0:T(8,128)} collective-permute-done((f32[128,2304]{1,0:T(8,128)}, f32[128,2304]{1,0:T(8,128)}, u32[]{:S(2)}, u32[]{:S(2)}) %collective-permute-start.53) | collective-permute-done | bytes 1179680 | tf_op jit(solution)/shard_map/ppermute | solution.py:154
  1292.6 43.2 %reduce-scatter.11.cloned.1.call-done = f32[16,2,1,1560]{3,0,1,2:T(8,128)} async-done(((f32[16,2,16,1560]{3,0,1,2:T(8,128)}), f32[16,2,1,1560]{3,0,1,2:T(8,128)}) %reduce-scatter.11.cloned.1.call-update) | async-done | bytes 199696 | tf_op jit(solution)/shard_map/reduce_scatter | solution.py:278
  1338.2 67.6 %reduce-scatter.9.cloned.1.call-done = f32[16,2,1,1560]{3,0,1,2:T(8,128)} async-done(((f32[16,2,16,1560]{3,0,1,2:T(8,128)}), f32[16,2,1,1560]{3,0,1,2:T(8,128)}) %reduce-scatter.9.cloned.1.call-update) | async-done | bytes 199696 | tf_op jit(solution)/shard_map/reduce_scatter | solution.py:278
  (1276 shorter events, 694.6 us)
Async XLA Ops:
  7.2 384.0 %all-gather.5.cloned.1.call-start = ((), (), s32[]{:S(2)}) async-start(), calls=%async_computation.5 | async-start | bytes 2359296 | tf_op jit(solution)/shard_map/all_gather | solution.py:431
  29.9 162.2 %collective-permute-start.21 = (bf16[144,6912]{1,0:T(8,128)(2,1)}, bf16[144,6912]{1,0:T(8,128)(2,1)}, u32[]{:S(2)}, u32[]{:S(2)}) collective-permute-start(bf16[144,6912]{1,0:T(8,128)(2,1)} %pad_maximum_fusion.4), channel_id=1, source_target_pairs={{0,16},{16,0},{1,17},{17,1},{2,18},{18,2},{3,19},{19,3},{4,20},{20... | collective-permute-start | bytes 5971976 | tf_op jit(solution)/shard_map/ppermute | solution.py:154
  38.3 115.9 %collective-permute-start.1 = (bf16[144,1536]{1,0:T(8,128)(2,1)}, bf16[144,1536]{1,0:T(8,128)(2,1)}, u32[]{:S(2)}, u32[]{:S(2)}) collective-permute-start(bf16[144,1536]{1,0:T(8,128)(2,1)} %pad_maximum_fusion.5), channel_id=1, source_target_pairs={{0,16},{16,0},{1,17},{17,1},{2,18},{18,2},{3,19},{19,3},{4,20},{20... | collective-permute-start | bytes 1327112 | tf_op jit(solution)/shard_map/ppermute | solution.py:154
  38.3 76.7 %collective-permute-start.16 = (s32[2,7]{1,0:T(2,128)S(1)}, s32[2,7]{1,0:T(2,128)}, u32[]{:S(2)}, u32[]{:S(2)}) collective-permute-start(s32[2,7]{1,0:T(2,128)S(1)} %bitcast.1363), channel_id=1, source_target_pairs={{0,16},{16,0},{1,17},{17,1},{2,18},{18,2},{3,19},{19,3},{4,20},{20... | collective-permute-start | bytes 176 | tf_op jit(solution)/shard_map/ppermute | solution.py:154
  41.9 126.8 %collective-permute-start = (bf16[2,128,2304]{1,2,0:T(8,128)(2,1)}, bf16[2,128,2304]{1,2,0:T(8,128)(2,1)}, u32[]{:S(2)}, u32[]{:S(2)}) collective-permute-start(bf16[2,128,2304]{1,2,0:T(8,128)(2,1)} %bitcast.1199), channel_id=1, source_target_pairs={{0,16},{16,0},{1,17},{17,1},{2,18},{18,2},{3,19},{19,3},{4,20},{20... | collective-permute-start | bytes 3538952 | tf_op jit(solution)/shard_map/ppermute | solution.py:154
  42.0 69.4 %collective-permute-start.17 = (s32[2]{0:T(128)}, s32[2]{0:T(128)}, u32[]{:S(2)}, u32[]{:S(2)}) collective-permute-start(s32[2]{0:T(128)} %bitcast.74), channel_id=1, source_target_pairs={{0,16},{16,0},{1,17},{17,1},{2,18},{18,2},{3,19},{19,3},{4,20},{20... | collective-permute-start | bytes 32 | tf_op jit(solution)/shard_map/ppermute | solution.py:154
  238.4 165.9 %all-gather.3.cloned.1.call-start = ((), (), s32[]{:S(2)}) async-start(), calls=%async_computation.4 | async-start | bytes 2359296 | tf_op jit(solution)/shard_map/all_gather | solution.py:431
  243.0 68.8 %collective-permute-start.22 = (bf16[144,6912]{1,0:T(8,128)(2,1)}, bf16[144,6912]{1,0:T(8,128)(2,1)}, u32[]{:S(2)}, u32[]{:S(2)}) collective-permute-start(bf16[144,6912]{1,0:T(8,128)(2,1)} %get-tuple-element.131), channel_id=1, source_target_pairs={{0,4},{4,8},{8,12},{12,14},{14,10},{10,6},{6,2},{2,0},{1,5},{5,9},... | collective-permute-start | bytes 5971976 | tf_op jit(solution)/shard_map/ppermute | solution.py:200
  244.6 72.8 %collective-permute-start.23 = (bf16[144,6912]{1,0:T(8,128)(2,1)}, bf16[144,6912]{1,0:T(8,128)(2,1)}, u32[]{:S(2)}, u32[]{:S(2)}) collective-permute-start(bf16[144,6912]{1,0:T(8,128)(2,1)} %get-tuple-element.130), channel_id=1, source_target_pairs={{4,0},{8,4},{12,8},{14,12},{10,14},{6,10},{2,6},{0,2},{5,1},{9,5},... | collective-permute-start | bytes 5971976 | tf_op jit(solution)/shard_map/ppermute | solution.py:201
  271.5 704.8 %reduce-scatter.7.cloned.1.call-start = ((), (), s32[]{:S(2)}) async-start(), calls=%async_computation.7 | async-start | bytes 4718592 | tf_op jit(solution)/shard_map/reduce_scatter | solution.py:519
  311.8 70.8 %collective-permute-start.24 = (bf16[144,6912]{1,0:T(8,128)(2,1)}, bf16[144,6912]{1,0:T(8,128)(2,1)}, u32[]{:S(2)}, u32[]{:S(2)}) collective-permute-start(bf16[144,6912]{1,0:T(8,128)(2,1)} %collective-permute-done.22), channel_id=1, source_target_pairs={{0,4},{4,8},{8,12},{12,14},{14,10},{10,6},{6,2},{2,0},{1,5},{5,9},... | collective-permute-start | bytes 5971976 | tf_op jit(solution)/shard_map/ppermute | solution.py:200
  317.4 70.7 %collective-permute-start.25 = (bf16[144,6912]{1,0:T(8,128)(2,1)}, bf16[144,6912]{1,0:T(8,128)(2,1)}, u32[]{:S(2)}, u32[]{:S(2)}) collective-permute-start(bf16[144,6912]{1,0:T(8,128)(2,1)} %collective-permute-done.23), channel_id=1, source_target_pairs={{4,0},{8,4},{12,8},{14,12},{10,14},{6,10},{2,6},{0,2},{5,1},{9,5},... | collective-permute-start | bytes 5971976 | tf_op jit(solution)/shard_map/ppermute | solution.py:201
  459.6 45.1 %collective-permute-start.30 = (bf16[144,6912]{1,0:T(8,128)(2,1)}, bf16[144,6912]{1,0:T(8,128)(2,1)}, u32[]{:S(2)}, u32[]{:S(2)}) collective-permute-start(bf16[144,6912]{1,0:T(8,128)(2,1)} %collective-permute-done.28), channel_id=1, source_target_pairs={{0,4},{4,8},{8,12},{12,14},{14,10},{10,6},{6,2},{2,0},{1,5},{5,9},... | collective-permute-start | bytes 5971976 | tf_op jit(solution)/shard_map/ppermute | solution.py:200
  465.1 45.3 %collective-permute-start.31 = (bf16[144,6912]{1,0:T(8,128)(2,1)}, bf16[144,6912]{1,0:T(8,128)(2,1)}, u32[]{:S(2)}, u32[]{:S(2)}) collective-permute-start(bf16[144,6912]{1,0:T(8,128)(2,1)} %collective-permute-done.29), channel_id=1, source_target_pairs={{4,0},{8,4},{12,8},{14,12},{10,14},{6,10},{2,6},{0,2},{5,1},{9,5},... | collective-permute-start | bytes 5971976 | tf_op jit(solution)/shard_map/ppermute | solution.py:201
  510.4 44.2 %collective-permute-start.33 = (bf16[144,6912]{1,0:T(8,128)(2,1)}, bf16[144,6912]{1,0:T(8,128)(2,1)S(1)}, u32[]{:S(2)}, u32[]{:S(2)}) collective-permute-start(bf16[144,6912]{1,0:T(8,128)(2,1)} %collective-permute-done.31), channel_id=1, source_target_pairs={{4,0},{8,4},{12,8},{14,12},{10,14},{6,10},{2,6},{0,2},{5,1},{9,5},... | collective-permute-start | bytes 5971976 | tf_op jit(solution)/shard_map/ppermute | solution.py:201
  885.4 179.6 %reduce-scatter.5.cloned.1.call-start = ((), (), s32[]{:S(2)}) async-start(), calls=%async_computation.6 | async-start | bytes 4718592 | tf_op jit(solution)/shard_map/reduce_scatter | solution.py:519
  914.2 421.6 %reduce-scatter.11.cloned.1.call-start = ((), (), s32[]{:S(2)}) async-start(), calls=%async_computation.9 | async-start | bytes 3620864 | tf_op jit(solution)/shard_map/reduce_scatter | solution.py:278
  1075.4 168.5 %collective-permute-start.58 = (f32[16,22784]{1,0:T(8,128)}, f32[16,22784]{1,0:T(8,128)}, u32[]{:S(2)}, u32[]{:S(2)}) collective-permute-start(f32[16,22784]{1,0:T(8,128)} %dynamic-slice_bitcast_fusion.2), channel_id=1, source_target_pairs={{0,16},{16,0},{1,17},{17,1},{2,18},{18,2},{3,19},{19,3},{4,20},{20... | collective-permute-start | bytes 4374536 | tf_op jit(solution)/shard_map/ppermute | solution.py:154
  1081.2 177.4 %collective-permute-start.59 = (f32[16,27136]{1,0:T(8,128)}, f32[16,27136]{1,0:T(8,128)}, u32[]{:S(2)}, u32[]{:S(2)}) collective-permute-start(f32[16,27136]{1,0:T(8,128)} %dynamic-slice_bitcast_fusion), channel_id=1, source_target_pairs={{0,16},{16,0},{1,17},{17,1},{2,18},{18,2},{3,19},{19,3},{4,20},{20... | collective-permute-start | bytes 5210120 | tf_op jit(solution)/shard_map/ppermute | solution.py:154
  1089.2 158.0 %collective-permute-start.55 = (f32[16,22784]{1,0:T(8,128)}, f32[16,22784]{1,0:T(8,128)}, u32[]{:S(2)}, u32[]{:S(2)}) collective-permute-start(f32[16,22784]{1,0:T(8,128)} %dynamic-slice_bitcast_fusion.3), channel_id=1, source_target_pairs={{0,16},{16,0},{1,17},{17,1},{2,18},{18,2},{3,19},{19,3},{4,20},{20... | collective-permute-start | bytes 4374536 | tf_op jit(solution)/shard_map/ppermute | solution.py:154
  1095.0 174.2 %collective-permute-start.56 = (f32[16,27136]{1,0:T(8,128)}, f32[16,27136]{1,0:T(8,128)}, u32[]{:S(2)}, u32[]{:S(2)}) collective-permute-start(f32[16,27136]{1,0:T(8,128)} %dynamic-slice_bitcast_fusion.1), channel_id=1, source_target_pairs={{0,16},{16,0},{1,17},{17,1},{2,18},{18,2},{3,19},{19,3},{4,20},{20... | collective-permute-start | bytes 5210120 | tf_op jit(solution)/shard_map/ppermute | solution.py:154
  1124.0 116.0 %collective-permute-start.53 = (f32[128,2304]{1,0:T(8,128)}, f32[128,2304]{1,0:T(8,128)}, u32[]{:S(2)}, u32[]{:S(2)}) collective-permute-start(f32[128,2304]{1,0:T(8,128)} %dynamic-slice_bitcast_fusion.4), channel_id=1, source_target_pairs={{0,16},{16,0},{1,17},{17,1},{2,18},{18,2},{3,19},{19,3},{4,20},{20... | collective-permute-start | bytes 3538952 | tf_op jit(solution)/shard_map/ppermute | solution.py:154
  1268.9 136.9 %reduce-scatter.9.cloned.1.call-start = ((), (), s32[]{:S(2)}) async-start(), calls=%async_computation.8 | async-start | bytes 3620864 | tf_op jit(solution)/shard_map/reduce_scatter | solution.py:278
  1336.7 73.3 %collective-permute-start.60 = (f32[16,1560]{1,0:T(8,128)S(1)}, f32[16,1560]{1,0:T(8,128)S(1)}, u32[]{:S(2)}, u32[]{:S(2)}) collective-permute-start(f32[16,1560]{1,0:T(8,128)S(1)} %dynamic-slice_bitcast_fusion.8), channel_id=1, source_target_pairs={{0,16},{16,0},{1,17},{17,1},{2,18},{18,2},{3,19},{19,3},{4,20},{20... | collective-permute-start | bytes 299528 | tf_op jit(solution)/shard_map/ppermute | solution.py:154
  (391 other events, 4835.1 us)
Sparse Core Ops, SparseCore 0:
  238.5 65.8 all-gather.4
  307.2 69.6 all-gather.2
  885.5 87.5 reduce-scatter.6
  976.6 88.3 reduce-scatter.4
  1269.0 66.7 reduce-scatter.10
  1339.5 66.2 reduce-scatter.8

commit v5 on v4

--- a/solution.py
+++ b/solution.py
@@ -371,8 +371,8 @@
         inner_grad = jnp.einsum("eto,ero->etr", grad_out, up_part, preferred_element_type=WIDE)
         width = grad_out.shape[-1]
         back = jnp.einsum("to,do->td", grad_out.reshape(tokens, width), weight, preferred_element_type=WIDE)
-        back = unpermute(back.reshape(groups, rows, MODEL_WIDTH))
-        back = back + jnp.einsum("etr,erd->etd", inner_grad, down_part.astype(WIDE), precision=HIGH)
+        back = back.reshape(groups, rows, MODEL_WIDTH)
+        back = back + jnp.einsum("etr,erd->etd", inner_grad, permute(down_part).astype(WIDE), precision=HIGH)
         down_grad = jnp.einsum("etr,etd->erd", inner_grad, inputs_low.astype(WIDE), precision=HIGH)
         up_grad = jnp.einsum("etr,eto->ero", inner_low, grad_out, preferred_element_type=WIDE)
         return (back, down_grad, up_grad)
@@ -484,7 +484,7 @@
         )
         grad_down = place(grad_down, piece_down, in_up)
         grad_up = place(grad_up, piece_up, out_up)
-        grad_normed_ffw = to_owner(back_gate + back_upper)
+        grad_normed_ffw = unpermute(to_owner(back_gate + back_upper))
         grad_middle = seed_grad + normalize_back(middle, pre_feedforward, grad_normed_ffw)
         grad_attention_own = normalize_back(attention_out, post_attention, grad_middle).astype(NARROW)
         grad_attention = gather_pairs(grad_attention_own, "dp", groups, own)
@@ -556,7 +556,7 @@
         )
         grad_down = place(grad_down, piece_down, 2 * MODEL_WIDTH)
         grad_up = place(grad_up, piece_up, out_value)
-        grad_normed = to_owner(back_query + back_key + back_value)
+        grad_normed = unpermute(to_owner(back_query + back_key + back_value))
         own_down = scatter_pairs(grad_down, "dp", groups, own)
         own_up = scatter_pairs(grad_up, "dp", groups, own)
         down_part, up_part = settle(own_down, own_up, slots)

time: 1430 us -> 1370 us (0.958)
  waiting for transfers between devices: 667 us -> 592 us
  other arithmetic: 121 us -> 136 us
    reduce_scatter x2, waiting for transfers between devices: 111 us -> 55 us  [settle(): lax.psum_scatter(both, ('seq', 'mp'), scatter_dimension=2, tiled=True)]
    reshape x14 -> x8, local copies, waits for them, and re-layouts: 45 us -> 12.2 us  [unpermute(): return jnp.swapaxes(moved, -3, -2).reshape(lead + (MODEL_WIDTH,))]
    reduce_scatter x2, waiting for transfers between devices: 87.1 us -> 64.2 us  [shards(): lax.psum_scatter(jnp.stack([grad_key_part.reshape(groups, length, key_loc...]
    slice x3 -> x0, local copies, waits for them, and re-layouts: 20.7 us -> none  [the longest x1 16.1 us: shards(): gate_full = ffw_full[:, :hidden_local]]
    reshape x0 -> x10, local copies, waits for them, and re-layouts: none -> 19.5 us  [permute(): return jnp.swapaxes(moved, -3, -2).reshape(lead + (MODEL_WIDTH,))]
    dot_general x10, matrix products: 22.2 us -> 39.8 us  [column_back(): jnp.einsum('to,do->td', grad_out.reshape(tokens, width), weight, preferre...]
    convert_element_type x2 -> x20, local copies, waits for them, and re-layouts: 3.58 us -> 20.5 us  [pick(): jnp.sum(jnp.where(hit[:, None, None], window.astype(WIDE), 0.0), axis=0)]
    transpose x8 -> x18, local copies, waits for them, and re-layouts: 3.07 us -> 17.9 us  [permute(): return jnp.swapaxes(moved, -3, -2).reshape(lead + (MODEL_WIDTH,))]
  transfers between devices with their start and end apart: 67 -> 67, of which waited for: 32 -> 32; matrix products, arithmetic and copies ran while one was open for 34% -> 39% of each run, Pallas kernels for 0% -> 0%
where the time goes in v5:
time: 1370 us; the launch traced here: 1360 us
  waiting for transfers between devices  592 us (43%)
  local copies, waits for them, and re-layouts  301 us (22%)
  matrix products  213 us (16%)
  other arithmetic  136 us (10%)
  starting transfers between devices  65.3 us (5%)
  between operations  47.8 us (3%)
    ppermute x14, waiting for transfers between devices, ring_gather(): ahead = lax.ppermute(ahead, 'seq', forward)  239 us
    ppermute x33, waiting for transfers between devices, shift(): lax.ppermute(value, axis, [(a, (a + step) % size) for a in range(size)])  225 us
    reduce_scatter x2, waiting for transfers between devices, shards(): lax.psum_scatter(jnp.stack([grad_key_part.reshape(groups, length, key_loc...  64.2 us
    reduce_scatter x2, waiting for transfers between devices, settle(): lax.psum_scatter(both, ('seq', 'mp'), scatter_dimension=2, tiled=True)  55 us
    dot_general x10, matrix products, column_forward(): jnp.dot(permute(inputs_low).reshape(tokens, MODEL_WIDTH), weight, preferr...  42.2 us
    dot_general x10, matrix products, column_back(): jnp.einsum('to,do->td', grad_out.reshape(tokens, width), weight, preferre...  39.8 us
    ppermute x33, starting transfers between devices, shift(): lax.ppermute(value, axis, [(a, (a + step) % size) for a in range(size)])  31.5 us
    unnamed x723, local copies, waits for them, and re-layouts  30.2 us
  transfers between devices with their start and end apart: 67, of which 32 were waited for; matrix products, arithmetic and copies ran while one was open for 39% of the time, Pallas kernels for 0%

profile of v5, /device:TPU:0, one launch (start us, length us, event | category | flops | bytes accessed | tf_op | source)
XLA Modules:
  0.0 1355.9 jit_solution(2337048288772378765)
XLA Ops:
  91.5 20.0 %collective-permute-done.17 = s32[2]{0:T(128)} collective-permute-done((s32[2]{0:T(128)}, s32[2]{0:T(128)}, u32[]{:S(2)}, u32[]{:S(2)}) %collective-permute-start.17) | collective-permute-done | bytes 40 | tf_op jit(solution)/shard_map/ppermute | solution.py:154
  182.1 8.2 collective-permute-done.6
  202.7 8.7 collective-permute-done.10
  213.5 9.8 collective-permute-done.12
  245.5 10.9 broadcast_in_dim.1077
  272.4 39.7 %collective-permute-done.22 = bf16[144,6912]{1,0:T(8,128)(2,1)} collective-permute-done((bf16[144,6912]{1,0:T(8,128)(2,1)}, bf16[144,6912]{1,0:T(8,128)(2,1)}, u32[]{:S(2)}, u32[]{:S(2)}) %collective-permute-start.22) | collective-permute-done | bytes 1990688 | tf_op jit(solution)/shard_map/ppermute | solution.py:200
  321.0 61.9 %collective-permute-done.24 = bf16[144,6912]{1,0:T(8,128)(2,1)} collective-permute-done((bf16[144,6912]{1,0:T(8,128)(2,1)}, bf16[144,6912]{1,0:T(8,128)(2,1)}, u32[]{:S(2)}, u32[]{:S(2)}) %collective-permute-start.24) | collective-permute-done | bytes 1990688 | tf_op jit(solution)/shard_map/ppermute | solution.py:200
  415.2 11.0 collective-permute-done.26
  472.0 9.5 collective-permute-done.40
  493.8 11.4 collective-permute-done.30
  513.7 35.6 %collective-permute-done.32 = bf16[144,6912]{1,0:T(8,128)(2,1)S(1)} collective-permute-done((bf16[144,6912]{1,0:T(8,128)(2,1)}, bf16[144,6912]{1,0:T(8,128)(2,1)S(1)}, u32[]{:S(2)}, u32[]{:S(2)}) %collective-permute-start.32) | collective-permute-done | bytes 1990688 | tf_op jit(solution)/shard_map/ppermute | solution.py:200
  556.7 35.6 %collective-permute-done.34 = bf16[144,6912]{1,0:T(8,128)(2,1)S(1)} collective-permute-done((bf16[144,6912]{1,0:T(8,128)(2,1)S(1)}, bf16[144,6912]{1,0:T(8,128)(2,1)S(1)}, u32[]{:S(2)}, u32[]{:S(2)}) %collective-permute-start.34) | collective-permute-done | bytes 1990688 | tf_op jit(solution)/shard_map/ppermute | solution.py:200
  606.0 9.8 multiply_convert_fusion.4
  636.9 9.8 multiply_convert_fusion.2
  664.5 18.9 %collective-permute-done.41 = f32[128,2320]{0,1:T(8,128)} collective-permute-done((f32[128,2320]{0,1:T(8,128)}, f32[128,2320]{0,1:T(8,128)}, u32[]{:S(2)}, u32[]{:S(2)}) %collective-permute-start.41) | collective-permute-done | bytes 1187872 | tf_op jit(solution)/shard_map/ppermute | solution.py:154
  811.5 23.7 %collective-permute-done.44 = f32[128,2304]{1,0:T(8,128)S(1)} collective-permute-done((f32[128,2304]{1,0:T(8,128)S(1)}, f32[128,2304]{1,0:T(8,128)S(1)}, u32[]{:S(2)}, u32[]{:S(2)}) %collective-permute-start.44) | collective-permute-done | bytes 1179680 | tf_op jit(solution)/shard_map/ppermute | solution.py:154
  859.8 13.7 %collective-permute-done.52 = bf16[128,2304]{1,0:T(8,128)(2,1)} collective-permute-done((bf16[128,2304]{1,0:T(8,128)(2,1)S(1)}, bf16[128,2304]{1,0:T(8,128)(2,1)}, u32[]{:S(2)}, u32[]{:S(2)}) %collective-permute-start.52) | collective-permute-done | bytes 589856 | tf_op jit(solution)/shard_map/ppermute | solution.py:154
  909.6 9.7 collective-permute-done.46
  1004.8 64.2 %reduce-scatter.5.cloned.1.call-done = f32[2,2,128,256]{3,2,1,0:T(8,128)} async-done(((f32[2,2,1024,256]{3,2,1,0:T(8,128)}), f32[2,2,128,256]{3,2,1,0:T(8,128)}) %reduce-scatter.5.cloned.1.call-update) | async-done | bytes 524304 | tf_op jit(solution)/shard_map/reduce_scatter | solution.py:519
  1118.7 64.3 %collective-permute-done.55 = f32[16,22784]{1,0:T(8,128)S(1)} collective-permute-done((f32[16,22784]{1,0:T(8,128)S(1)}, f32[16,22784]{1,0:T(8,128)S(1)}, u32[]{:S(2)}, u32[]{:S(2)}) %collective-permute-start.55) | collective-permute-done | bytes 1458208 | tf_op jit(solution)/shard_map/ppermute | solution.py:154
  1203.7 16.6 %collective-permute-done.56 = f32[16,27136]{1,0:T(8,128)} collective-permute-done((f32[16,27136]{1,0:T(8,128)}, f32[16,27136]{1,0:T(8,128)}, u32[]{:S(2)}, u32[]{:S(2)}) %collective-permute-start.56) | collective-permute-done | bytes 1736736 | tf_op jit(solution)/shard_map/ppermute | solution.py:154
  1230.8 14.8 %collective-permute-done.53 = f32[128,2304]{1,0:T(8,128)} collective-permute-done((f32[128,2304]{1,0:T(8,128)}, f32[128,2304]{1,0:T(8,128)}, u32[]{:S(2)}, u32[]{:S(2)}) %collective-permute-start.53) | collective-permute-done | bytes 1179680 | tf_op jit(solution)/shard_map/ppermute | solution.py:154
  1247.2 22.1 %collective-permute-done.47 = f32[128,2304]{1,0:T(8,128)} collective-permute-done((f32[128,2304]{1,0:T(8,128)}, f32[128,2304]{1,0:T(8,128)}, u32[]{:S(2)}, u32[]{:S(2)}) %collective-permute-start.47) | collective-permute-done | bytes 1179680 | tf_op jit(solution)/shard_map/ppermute | solution.py:154
  1285.8 55.0 %reduce-scatter.9.cloned.1.call-done = f32[16,2,1,1560]{3,0,1,2:T(8,128)} async-done(((f32[16,2,16,1560]{3,0,1,2:T(8,128)}), f32[16,2,1,1560]{3,0,1,2:T(8,128)}) %reduce-scatter.9.cloned.1.call-update) | async-done | bytes 199696 | tf_op jit(solution)/shard_map/reduce_scatter | solution.py:278
  (1326 shorter events, 723.1 us)
Async XLA Ops:
  7.2 384.3 %all-gather.5.cloned.1.call-start = ((), (), s32[]{:S(2)}) async-start(), calls=%async_computation.5 | async-start | bytes 2359296 | tf_op jit(solution)/shard_map/all_gather | solution.py:431
  29.9 162.5 %collective-permute-start.21 = (bf16[144,6912]{1,0:T(8,128)(2,1)}, bf16[144,6912]{1,0:T(8,128)(2,1)}, u32[]{:S(2)}, u32[]{:S(2)}) collective-permute-start(bf16[144,6912]{1,0:T(8,128)(2,1)} %pad_maximum_fusion.4), channel_id=1, source_target_pairs={{0,16},{16,0},{1,17},{17,1},{2,18},{18,2},{3,19},{19,3},{4,20},{20... | collective-permute-start | bytes 5971976 | tf_op jit(solution)/shard_map/ppermute | solution.py:154
  38.4 116.0 %collective-permute-start.1 = (bf16[144,1536]{1,0:T(8,128)(2,1)}, bf16[144,1536]{1,0:T(8,128)(2,1)}, u32[]{:S(2)}, u32[]{:S(2)}) collective-permute-start(bf16[144,1536]{1,0:T(8,128)(2,1)} %pad_maximum_fusion.5), channel_id=1, source_target_pairs={{0,16},{16,0},{1,17},{17,1},{2,18},{18,2},{3,19},{19,3},{4,20},{20... | collective-permute-start | bytes 1327112 | tf_op jit(solution)/shard_map/ppermute | solution.py:154
  38.4 76.7 %collective-permute-start.16 = (s32[2,7]{1,0:T(2,128)S(1)}, s32[2,7]{1,0:T(2,128)}, u32[]{:S(2)}, u32[]{:S(2)}) collective-permute-start(s32[2,7]{1,0:T(2,128)S(1)} %bitcast.1203), channel_id=1, source_target_pairs={{0,16},{16,0},{1,17},{17,1},{2,18},{18,2},{3,19},{19,3},{4,20},{20... | collective-permute-start | bytes 176 | tf_op jit(solution)/shard_map/ppermute | solution.py:154
  42.0 127.0 %collective-permute-start = (bf16[2,128,2304]{1,2,0:T(8,128)(2,1)}, bf16[2,128,2304]{1,2,0:T(8,128)(2,1)}, u32[]{:S(2)}, u32[]{:S(2)}) collective-permute-start(bf16[2,128,2304]{1,2,0:T(8,128)(2,1)} %bitcast.1056), channel_id=1, source_target_pairs={{0,16},{16,0},{1,17},{17,1},{2,18},{18,2},{3,19},{19,3},{4,20},{20... | collective-permute-start | bytes 3538952 | tf_op jit(solution)/shard_map/ppermute | solution.py:154
  42.2 69.3 %collective-permute-start.17 = (s32[2]{0:T(128)}, s32[2]{0:T(128)}, u32[]{:S(2)}, u32[]{:S(2)}) collective-permute-start(s32[2]{0:T(128)} %bitcast.74), channel_id=1, source_target_pairs={{0,16},{16,0},{1,17},{17,1},{2,18},{18,2},{3,19},{19,3},{4,20},{20... | collective-permute-start | bytes 32 | tf_op jit(solution)/shard_map/ppermute | solution.py:154
  238.8 165.8 %all-gather.3.cloned.1.call-start = ((), (), s32[]{:S(2)}) async-start(), calls=%async_computation.4 | async-start | bytes 2359296 | tf_op jit(solution)/shard_map/all_gather | solution.py:431
  243.3 68.8 %collective-permute-start.22 = (bf16[144,6912]{1,0:T(8,128)(2,1)}, bf16[144,6912]{1,0:T(8,128)(2,1)}, u32[]{:S(2)}, u32[]{:S(2)}) collective-permute-start(bf16[144,6912]{1,0:T(8,128)(2,1)} %get-tuple-element.127), channel_id=1, source_target_pairs={{0,4},{4,8},{8,12},{12,14},{14,10},{10,6},{6,2},{2,0},{1,5},{5,9},... | collective-permute-start | bytes 5971976 | tf_op jit(solution)/shard_map/ppermute | solution.py:200
  244.9 72.7 %collective-permute-start.23 = (bf16[144,6912]{1,0:T(8,128)(2,1)}, bf16[144,6912]{1,0:T(8,128)(2,1)}, u32[]{:S(2)}, u32[]{:S(2)}) collective-permute-start(bf16[144,6912]{1,0:T(8,128)(2,1)} %get-tuple-element.126), channel_id=1, source_target_pairs={{4,0},{8,4},{12,8},{14,12},{10,14},{6,10},{2,6},{0,2},{5,1},{9,5},... | collective-permute-start | bytes 5971976 | tf_op jit(solution)/shard_map/ppermute | solution.py:201
  271.5 732.3 %reduce-scatter.7.cloned.1.call-start = ((), (), s32[]{:S(2)}) async-start(), calls=%async_computation.7 | async-start | bytes 4718592 | tf_op jit(solution)/shard_map/reduce_scatter | solution.py:519
  312.1 70.8 %collective-permute-start.24 = (bf16[144,6912]{1,0:T(8,128)(2,1)}, bf16[144,6912]{1,0:T(8,128)(2,1)}, u32[]{:S(2)}, u32[]{:S(2)}) collective-permute-start(bf16[144,6912]{1,0:T(8,128)(2,1)} %collective-permute-done.22), channel_id=1, source_target_pairs={{0,4},{4,8},{8,12},{12,14},{14,10},{10,6},{6,2},{2,0},{1,5},{5,9},... | collective-permute-start | bytes 5971976 | tf_op jit(solution)/shard_map/ppermute | solution.py:200
  317.6 70.9 %collective-permute-start.25 = (bf16[144,6912]{1,0:T(8,128)(2,1)}, bf16[144,6912]{1,0:T(8,128)(2,1)}, u32[]{:S(2)}, u32[]{:S(2)}) collective-permute-start(bf16[144,6912]{1,0:T(8,128)(2,1)} %collective-permute-done.23), channel_id=1, source_target_pairs={{4,0},{8,4},{12,8},{14,12},{10,14},{6,10},{2,6},{0,2},{5,1},{9,5},... | collective-permute-start | bytes 5971976 | tf_op jit(solution)/shard_map/ppermute | solution.py:201
  465.6 45.1 %collective-permute-start.31 = (bf16[144,6912]{1,0:T(8,128)(2,1)}, bf16[144,6912]{1,0:T(8,128)(2,1)}, u32[]{:S(2)}, u32[]{:S(2)}) collective-permute-start(bf16[144,6912]{1,0:T(8,128)(2,1)} %collective-permute-done.29), channel_id=1, source_target_pairs={{4,0},{8,4},{12,8},{14,12},{10,14},{6,10},{2,6},{0,2},{5,1},{9,5},... | collective-permute-start | bytes 5971976 | tf_op jit(solution)/shard_map/ppermute | solution.py:201
  664.4 50.0 %collective-permute-start.37 = (f32[128,2320]{0,1:T(8,128)S(1)}, f32[128,2320]{0,1:T(8,128)}, u32[]{:S(2)}, u32[]{:S(2)}) collective-permute-start(f32[128,2320]{0,1:T(8,128)S(1)} %bitcast_add_fusion.6), channel_id=1, source_target_pairs={{0,1},{1,0},{2,3},{3,2},{4,5},{5,4},{6,7},{7,6},{8,9},{9,8},{10,11... | collective-permute-start | bytes 3563528 | tf_op jit(solution)/shard_map/ppermute | solution.py:154
  730.7 47.5 %collective-permute-start.43 = (bf16[128,2304]{1,0:T(8,128)(2,1)}, bf16[128,2304]{1,0:T(8,128)(2,1)}, u32[]{:S(2)}, u32[]{:S(2)}) collective-permute-start(bf16[128,2304]{1,0:T(8,128)(2,1)} %get-tuple-element.151), channel_id=1, source_target_pairs={{0,16},{16,0},{1,17},{17,1},{2,18},{18,2},{3,19},{19,3},{4,20},{20... | collective-permute-start | bytes 1769480 | tf_op jit(solution)/shard_map/ppermute | solution.py:154
  888.8 180.1 %reduce-scatter.5.cloned.1.call-start = ((), (), s32[]{:S(2)}) async-start(), calls=%async_computation.6 | async-start | bytes 4718592 | tf_op jit(solution)/shard_map/reduce_scatter | solution.py:519
  934.9 348.5 %reduce-scatter.11.cloned.1.call-start = ((), (), s32[]{:S(2)}) async-start(), calls=%async_computation.9 | async-start | bytes 3620864 | tf_op jit(solution)/shard_map/reduce_scatter | solution.py:278
  1085.5 107.5 %collective-permute-start.59 = (f32[16,27136]{1,0:T(8,128)}, f32[16,27136]{1,0:T(8,128)}, u32[]{:S(2)}, u32[]{:S(2)}) collective-permute-start(f32[16,27136]{1,0:T(8,128)} %dynamic-slice_bitcast_fusion), channel_id=1, source_target_pairs={{0,16},{16,0},{1,17},{17,1},{2,18},{18,2},{3,19},{19,3},{4,20},{20... | collective-permute-start | bytes 5210120 | tf_op jit(solution)/shard_map/ppermute | solution.py:154
  1088.8 94.2 %collective-permute-start.55 = (f32[16,22784]{1,0:T(8,128)S(1)}, f32[16,22784]{1,0:T(8,128)S(1)}, u32[]{:S(2)}, u32[]{:S(2)}) collective-permute-start(f32[16,22784]{1,0:T(8,128)S(1)} %dynamic-slice_bitcast_fusion.3), channel_id=1, source_target_pairs={{0,16},{16,0},{1,17},{17,1},{2,18},{18,2},{3,19},{19,3},{4,20},{20... | collective-permute-start | bytes 4374536 | tf_op jit(solution)/shard_map/ppermute | solution.py:154
  1094.6 125.7 %collective-permute-start.56 = (f32[16,27136]{1,0:T(8,128)}, f32[16,27136]{1,0:T(8,128)}, u32[]{:S(2)}, u32[]{:S(2)}) collective-permute-start(f32[16,27136]{1,0:T(8,128)} %dynamic-slice_bitcast_fusion.1), channel_id=1, source_target_pairs={{0,16},{16,0},{1,17},{17,1},{2,18},{18,2},{3,19},{19,3},{4,20},{20... | collective-permute-start | bytes 5210120 | tf_op jit(solution)/shard_map/ppermute | solution.py:154
  1102.5 143.1 %collective-permute-start.53 = (f32[128,2304]{1,0:T(8,128)}, f32[128,2304]{1,0:T(8,128)}, u32[]{:S(2)}, u32[]{:S(2)}) collective-permute-start(f32[128,2304]{1,0:T(8,128)} %dynamic-slice_bitcast_fusion.4), channel_id=1, source_target_pairs={{0,16},{16,0},{1,17},{17,1},{2,18},{18,2},{3,19},{19,3},{4,20},{20... | collective-permute-start | bytes 3538952 | tf_op jit(solution)/shard_map/ppermute | solution.py:154
  1114.5 154.8 %collective-permute-start.47 = (f32[128,2304]{1,0:T(8,128)}, f32[128,2304]{1,0:T(8,128)}, u32[]{:S(2)}, u32[]{:S(2)}) collective-permute-start(f32[128,2304]{1,0:T(8,128)} %dynamic-slice_bitcast_fusion.6), channel_id=1, source_target_pairs={{0,16},{16,0},{1,17},{17,1},{2,18},{18,2},{3,19},{19,3},{4,20},{20... | collective-permute-start | bytes 3538952 | tf_op jit(solution)/shard_map/ppermute | solution.py:154
  1203.4 137.4 %reduce-scatter.9.cloned.1.call-start = ((), (), s32[]{:S(2)}) async-start(), calls=%async_computation.8 | async-start | bytes 3620864 | tf_op jit(solution)/shard_map/reduce_scatter | solution.py:278
  1284.3 60.8 %collective-permute-start.60 = (f32[16,1560]{1,0:T(8,128)S(1)}, f32[16,1560]{1,0:T(8,128)S(1)}, u32[]{:S(2)}, u32[]{:S(2)}) collective-permute-start(f32[16,1560]{1,0:T(8,128)S(1)} %dynamic-slice_bitcast_fusion.8), channel_id=1, source_target_pairs={{0,16},{16,0},{1,17},{17,1},{2,18},{18,2},{3,19},{19,3},{4,20},{20... | collective-permute-start | bytes 299528 | tf_op jit(solution)/shard_map/ppermute | solution.py:154
  (396 other events, 5210.1 us)
Sparse Core Ops, SparseCore 0:
  238.9 65.8 all-gather.4
  307.5 69.6 all-gather.2
  888.9 88.1 reduce-scatter.6
  980.6 88.3 reduce-scatter.4
  1203.5 67.1 reduce-scatter.10
  1274.4 66.3 reduce-scatter.8

commit v6 on v5

--- a/solution.py
+++ b/solution.py
@@ -293,6 +293,46 @@
         )
         return down_part, up_part
 
+    def exchange_adapters(grad_down, grad_up):
+        if groups != 2:
+            return scatter_pairs(grad_down, "dp", groups, own), scatter_pairs(grad_up, "dp", groups, own)
+        other = wrap(own, 1, groups)
+        sender = part * groups + other
+
+        def spans(which):
+            if which == "down":
+                return [
+                    (0, 3 * MODEL_WIDTH),
+                    (in_gate, 2 * MODEL_WIDTH),
+                    (3 * MODEL_WIDTH + which_quarter * query_local, query_local),
+                    (5 * MODEL_WIDTH + query_width + which_quarter * hidden_local, hidden_local),
+                ]
+            return [
+                (which_quarter * query_local, query_local),
+                (query_width + which_quarter * key_local, key_local),
+                (query_width + key_span_width + which_quarter * key_local, key_local),
+                (query_width + 2 * key_span_width + MODEL_WIDTH + which_quarter * hidden_local, hidden_local),
+                (query_width + 2 * key_span_width + MODEL_WIDTH + FF + which_quarter * hidden_local, hidden_local),
+            ]
+
+        results = []
+        for which, table in (("down", grad_down), ("up", grad_up)):
+            which_quarter = quarter
+            send = lax.dynamic_index_in_dim(table, other, 0, keepdims=False)
+            packed = jnp.concatenate(
+                [lax.dynamic_slice_in_dim(send, start, size, axis=1) for start, size in spans(which)], axis=1
+            )
+            got = shift(packed, "dp", groups, 1)
+            which_quarter = sender
+            total = lax.dynamic_index_in_dim(table, own, 0, keepdims=False)
+            landed = jnp.zeros_like(total)
+            offset = 0
+            for start, size in spans(which):
+                landed = lax.dynamic_update_slice_in_dim(landed, got[:, offset : offset + size], start, axis=1)
+                offset += size
+            results.append(total + landed)
+        return results[0], results[1]
+
     def to_owner(partial):
         return sum_pairs(scatter_pairs(partial, "dp", groups, own), "mp", parts)
 
@@ -557,8 +597,7 @@
         grad_down = place(grad_down, piece_down, 2 * MODEL_WIDTH)
         grad_up = place(grad_up, piece_up, out_value)
         grad_normed = unpermute(to_owner(back_query + back_key + back_value))
-        own_down = scatter_pairs(grad_down, "dp", groups, own)
-        own_up = scatter_pairs(grad_up, "dp", groups, own)
+        own_down, own_up = exchange_adapters(grad_down, grad_up)
         down_part, up_part = settle(own_down, own_up, slots)
         down_list.append(down_part)
         up_list.append(up_part)

time: 1370 us -> 1340 us (0.978)
  waiting for transfers between devices: 592 us -> 551 us
    ppermute x33, waiting for transfers between devices: 225 us -> 150 us  [shift(): lax.ppermute(value, axis, [(a, (a + step) % size) for a in range(size)])]
    reduce_scatter x2, waiting for transfers between devices: 55 us -> 92.5 us  [settle(): lax.psum_scatter(both, ('seq', 'mp'), scatter_dimension=2, tiled=True)]
    unnamed x723 -> x729, local copies, waits for them, and re-layouts: 30.2 us -> 34.9 us
where the time goes in v6:
time: 1340 us; the launch traced here: 1320 us
  waiting for transfers between devices  551 us (41%)
  local copies, waits for them, and re-layouts  314 us (23%)
  matrix products  208 us (16%)
  other arithmetic  135 us (10%)
  starting transfers between devices  65.4 us (5%)
  between operations  47.7 us (4%)
    ppermute x14, waiting for transfers between devices, ring_gather(): ahead = lax.ppermute(ahead, 'seq', forward)  239 us
    ppermute x33, waiting for transfers between devices, shift(): lax.ppermute(value, axis, [(a, (a + step) % size) for a in range(size)])  150 us
    reduce_scatter x2, waiting for transfers between devices, settle(): lax.psum_scatter(both, ('seq', 'mp'), scatter_dimension=2, tiled=True)  92.5 us
    reduce_scatter x2, waiting for transfers between devices, shards(): lax.psum_scatter(jnp.stack([grad_key_part.reshape(groups, length, key_loc...  61.5 us
    dot_general x10, matrix products, column_forward(): jnp.dot(permute(inputs_low).reshape(tokens, MODEL_WIDTH), weight, preferr...  42.2 us
    unnamed x729, local copies, waits for them, and re-layouts  34.9 us
    dot_general x10, matrix products, column_back(): jnp.einsum('to,do->td', grad_out.reshape(tokens, width), weight, preferre...  34.3 us
    ppermute x33, starting transfers between devices, shift(): lax.ppermute(value, axis, [(a, (a + step) % size) for a in range(size)])  31.5 us
  transfers between devices with their start and end apart: 67, of which 32 were waited for; matrix products, arithmetic and copies ran while one was open for 39% of the time, Pallas kernels for 0%

profile of v6, /device:TPU:0, one launch (start us, length us, event | category | flops | bytes accessed | tf_op | source)
XLA Modules:
  0.0 1321.5 jit_solution(12913157705558829241)
XLA Ops:
  90.3 20.9 %collective-permute-done.17 = s32[2]{0:T(128)} collective-permute-done((s32[2]{0:T(128)}, s32[2]{0:T(128)}, u32[]{:S(2)}, u32[]{:S(2)}) %collective-permute-start.17) | collective-permute-done | bytes 40 | tf_op jit(solution)/shard_map/ppermute | solution.py:154
  181.9 8.2 collective-permute-done.6
  202.6 8.7 collective-permute-done.10
  213.4 9.8 collective-permute-done.12
  245.4 10.9 broadcast_in_dim.1077
  272.4 39.6 %collective-permute-done.22 = bf16[144,6912]{1,0:T(8,128)(2,1)} collective-permute-done((bf16[144,6912]{1,0:T(8,128)(2,1)}, bf16[144,6912]{1,0:T(8,128)(2,1)}, u32[]{:S(2)}, u32[]{:S(2)}) %collective-permute-start.22) | collective-permute-done | bytes 1990688 | tf_op jit(solution)/shard_map/ppermute | solution.py:200
  321.0 61.9 %collective-permute-done.24 = bf16[144,6912]{1,0:T(8,128)(2,1)} collective-permute-done((bf16[144,6912]{1,0:T(8,128)(2,1)}, bf16[144,6912]{1,0:T(8,128)(2,1)}, u32[]{:S(2)}, u32[]{:S(2)}) %collective-permute-start.24) | collective-permute-done | bytes 1990688 | tf_op jit(solution)/shard_map/ppermute | solution.py:200
  415.2 10.9 collective-permute-done.26
  471.8 9.5 collective-permute-done.40
  493.5 11.5 collective-permute-done.30
  513.6 35.6 %collective-permute-done.32 = bf16[144,6912]{1,0:T(8,128)(2,1)S(1)} collective-permute-done((bf16[144,6912]{1,0:T(8,128)(2,1)}, bf16[144,6912]{1,0:T(8,128)(2,1)S(1)}, u32[]{:S(2)}, u32[]{:S(2)}) %collective-permute-start.32) | collective-permute-done | bytes 1990688 | tf_op jit(solution)/shard_map/ppermute | solution.py:200
  556.7 35.6 %collective-permute-done.34 = bf16[144,6912]{1,0:T(8,128)(2,1)S(1)} collective-permute-done((bf16[144,6912]{1,0:T(8,128)(2,1)S(1)}, bf16[144,6912]{1,0:T(8,128)(2,1)S(1)}, u32[]{:S(2)}, u32[]{:S(2)}) %collective-permute-start.34) | collective-permute-done | bytes 1990688 | tf_op jit(solution)/shard_map/ppermute | solution.py:200
  606.0 9.8 multiply_convert_fusion.4
  636.9 9.8 multiply_convert_fusion.2
  664.5 18.9 %collective-permute-done.41 = f32[128,2320]{0,1:T(8,128)} collective-permute-done((f32[128,2320]{0,1:T(8,128)}, f32[128,2320]{0,1:T(8,128)}, u32[]{:S(2)}, u32[]{:S(2)}) %collective-permute-start.41) | collective-permute-done | bytes 1187872 | tf_op jit(solution)/shard_map/ppermute | solution.py:154
  811.4 23.7 %collective-permute-done.44 = f32[128,2304]{1,0:T(8,128)S(1)} collective-permute-done((f32[128,2304]{1,0:T(8,128)S(1)}, f32[128,2304]{1,0:T(8,128)S(1)}, u32[]{:S(2)}, u32[]{:S(2)}) %collective-permute-start.44) | collective-permute-done | bytes 1179680 | tf_op jit(solution)/shard_map/ppermute | solution.py:154
  859.6 13.7 %collective-permute-done.52 = bf16[128,2304]{1,0:T(8,128)(2,1)} collective-permute-done((bf16[128,2304]{1,0:T(8,128)(2,1)S(1)}, bf16[128,2304]{1,0:T(8,128)(2,1)}, u32[]{:S(2)}, u32[]{:S(2)}) %collective-permute-start.52) | collective-permute-done | bytes 589856 | tf_op jit(solution)/shard_map/ppermute | solution.py:154
  910.2 9.7 collective-permute-done.46
  1006.8 61.5 %reduce-scatter.5.cloned.1.call-done = f32[2,2,128,256]{3,2,1,0:T(8,128)} async-done(((f32[2,2,1024,256]{3,2,1,0:T(8,128)}), f32[2,2,128,256]{3,2,1,0:T(8,128)}) %reduce-scatter.5.cloned.1.call-update) | async-done | bytes 524304 | tf_op jit(solution)/shard_map/reduce_scatter | solution.py:559
  1108.9 10.0 collective-permute-done.59
  1122.0 24.3 %collective-permute-done.56 = f32[16,5632]{1,0:T(8,128)S(1)} collective-permute-done((f32[16,5632]{1,0:T(8,128)S(1)}, f32[16,5632]{1,0:T(8,128)S(1)}, u32[]{:S(2)}, u32[]{:S(2)}) %collective-permute-start.56) | collective-permute-done | bytes 360480 | tf_op jit(solution)/shard_map/ppermute | solution.py:154
  1185.9 9.5 collective-permute-done.47
  1211.6 24.8 %reduce-scatter.11.cloned.1.call-done = f32[16,2,1,1560]{3,0,1,2:T(8,128)} async-done(((f32[16,2,16,1560]{3,0,1,2:T(8,128)}), f32[16,2,1,1560]{3,0,1,2:T(8,128)}) %reduce-scatter.11.cloned.1.call-update) | async-done | bytes 199696 | tf_op jit(solution)/shard_map/reduce_scatter | solution.py:278
  1238.8 67.7 %reduce-scatter.9.cloned.1.call-done = f32[16,2,1,1560]{3,0,1,2:T(8,128)} async-done(((f32[16,2,16,1560]{3,0,1,2:T(8,128)}), f32[16,2,1,1560]{3,0,1,2:T(8,128)}) %reduce-scatter.9.cloned.1.call-update) | async-done | bytes 199696 | tf_op jit(solution)/shard_map/reduce_scatter | solution.py:278
  (1367 shorter events, 727.0 us)
Async XLA Ops:
  7.2 384.3 %all-gather.5.cloned.1.call-start = ((), (), s32[]{:S(2)}) async-start(), calls=%async_computation.5 | async-start | bytes 2359296 | tf_op jit(solution)/shard_map/all_gather | solution.py:471
  29.7 162.6 %collective-permute-start.21 = (bf16[144,6912]{1,0:T(8,128)(2,1)}, bf16[144,6912]{1,0:T(8,128)(2,1)}, u32[]{:S(2)}, u32[]{:S(2)}) collective-permute-start(bf16[144,6912]{1,0:T(8,128)(2,1)} %pad_maximum_fusion.4), channel_id=1, source_target_pairs={{0,16},{16,0},{1,17},{17,1},{2,18},{18,2},{3,19},{19,3},{4,20},{20... | collective-permute-start | bytes 5971976 | tf_op jit(solution)/shard_map/ppermute | solution.py:154
  38.1 116.1 %collective-permute-start.1 = (bf16[144,1536]{1,0:T(8,128)(2,1)}, bf16[144,1536]{1,0:T(8,128)(2,1)}, u32[]{:S(2)}, u32[]{:S(2)}) collective-permute-start(bf16[144,1536]{1,0:T(8,128)(2,1)} %pad_maximum_fusion.7), channel_id=1, source_target_pairs={{0,16},{16,0},{1,17},{17,1},{2,18},{18,2},{3,19},{19,3},{4,20},{20... | collective-permute-start | bytes 1327112 | tf_op jit(solution)/shard_map/ppermute | solution.py:154
  38.1 76.8 %collective-permute-start.16 = (s32[2,7]{1,0:T(2,128)S(1)}, s32[2,7]{1,0:T(2,128)}, u32[]{:S(2)}, u32[]{:S(2)}) collective-permute-start(s32[2,7]{1,0:T(2,128)S(1)} %bitcast.1241), channel_id=1, source_target_pairs={{0,16},{16,0},{1,17},{17,1},{2,18},{18,2},{3,19},{19,3},{4,20},{20... | collective-permute-start | bytes 176 | tf_op jit(solution)/shard_map/ppermute | solution.py:154
  41.8 127.1 %collective-permute-start = (bf16[2,128,2304]{1,2,0:T(8,128)(2,1)}, bf16[2,128,2304]{1,2,0:T(8,128)(2,1)}, u32[]{:S(2)}, u32[]{:S(2)}) collective-permute-start(bf16[2,128,2304]{1,2,0:T(8,128)(2,1)} %bitcast.1094), channel_id=1, source_target_pairs={{0,16},{16,0},{1,17},{17,1},{2,18},{18,2},{3,19},{19,3},{4,20},{20... | collective-permute-start | bytes 3538952 | tf_op jit(solution)/shard_map/ppermute | solution.py:154
  41.8 69.4 %collective-permute-start.17 = (s32[2]{0:T(128)}, s32[2]{0:T(128)}, u32[]{:S(2)}, u32[]{:S(2)}) collective-permute-start(s32[2]{0:T(128)} %bitcast.74), channel_id=1, source_target_pairs={{0,16},{16,0},{1,17},{17,1},{2,18},{18,2},{3,19},{19,3},{4,20},{20... | collective-permute-start | bytes 32 | tf_op jit(solution)/shard_map/ppermute | solution.py:154
  238.7 166.0 %all-gather.3.cloned.1.call-start = ((), (), s32[]{:S(2)}) async-start(), calls=%async_computation.4 | async-start | bytes 2359296 | tf_op jit(solution)/shard_map/all_gather | solution.py:471
  243.2 68.8 %collective-permute-start.22 = (bf16[144,6912]{1,0:T(8,128)(2,1)}, bf16[144,6912]{1,0:T(8,128)(2,1)}, u32[]{:S(2)}, u32[]{:S(2)}) collective-permute-start(bf16[144,6912]{1,0:T(8,128)(2,1)} %get-tuple-element.127), channel_id=1, source_target_pairs={{0,4},{4,8},{8,12},{12,14},{14,10},{10,6},{6,2},{2,0},{1,5},{5,9},... | collective-permute-start | bytes 5971976 | tf_op jit(solution)/shard_map/ppermute | solution.py:200
  244.8 72.7 %collective-permute-start.23 = (bf16[144,6912]{1,0:T(8,128)(2,1)}, bf16[144,6912]{1,0:T(8,128)(2,1)}, u32[]{:S(2)}, u32[]{:S(2)}) collective-permute-start(bf16[144,6912]{1,0:T(8,128)(2,1)} %get-tuple-element.126), channel_id=1, source_target_pairs={{4,0},{8,4},{12,8},{14,12},{10,14},{6,10},{2,6},{0,2},{5,1},{9,5},... | collective-permute-start | bytes 5971976 | tf_op jit(solution)/shard_map/ppermute | solution.py:201
  271.5 734.2 %reduce-scatter.7.cloned.1.call-start = ((), (), s32[]{:S(2)}) async-start(), calls=%async_computation.7 | async-start | bytes 4718592 | tf_op jit(solution)/shard_map/reduce_scatter | solution.py:559
  312.0 70.8 %collective-permute-start.24 = (bf16[144,6912]{1,0:T(8,128)(2,1)}, bf16[144,6912]{1,0:T(8,128)(2,1)}, u32[]{:S(2)}, u32[]{:S(2)}) collective-permute-start(bf16[144,6912]{1,0:T(8,128)(2,1)} %collective-permute-done.22), channel_id=1, source_target_pairs={{0,4},{4,8},{8,12},{12,14},{14,10},{10,6},{6,2},{2,0},{1,5},{5,9},... | collective-permute-start | bytes 5971976 | tf_op jit(solution)/shard_map/ppermute | solution.py:200
  317.5 70.8 %collective-permute-start.25 = (bf16[144,6912]{1,0:T(8,128)(2,1)}, bf16[144,6912]{1,0:T(8,128)(2,1)}, u32[]{:S(2)}, u32[]{:S(2)}) collective-permute-start(bf16[144,6912]{1,0:T(8,128)(2,1)} %collective-permute-done.23), channel_id=1, source_target_pairs={{4,0},{8,4},{12,8},{14,12},{10,14},{6,10},{2,6},{0,2},{5,1},{9,5},... | collective-permute-start | bytes 5971976 | tf_op jit(solution)/shard_map/ppermute | solution.py:201
  459.9 45.1 %collective-permute-start.30 = (bf16[144,6912]{1,0:T(8,128)(2,1)}, bf16[144,6912]{1,0:T(8,128)(2,1)}, u32[]{:S(2)}, u32[]{:S(2)}) collective-permute-start(bf16[144,6912]{1,0:T(8,128)(2,1)} %collective-permute-done.28), channel_id=1, source_target_pairs={{0,4},{4,8},{8,12},{12,14},{14,10},{10,6},{6,2},{2,0},{1,5},{5,9},... | collective-permute-start | bytes 5971976 | tf_op jit(solution)/shard_map/ppermute | solution.py:200
  664.4 50.0 %collective-permute-start.37 = (f32[128,2320]{0,1:T(8,128)S(1)}, f32[128,2320]{0,1:T(8,128)}, u32[]{:S(2)}, u32[]{:S(2)}) collective-permute-start(f32[128,2320]{0,1:T(8,128)S(1)} %bitcast_add_fusion.6), channel_id=1, source_target_pairs={{0,1},{1,0},{2,3},{3,2},{4,5},{5,4},{6,7},{7,6},{8,9},{9,8},{10,11... | collective-permute-start | bytes 3563528 | tf_op jit(solution)/shard_map/ppermute | solution.py:154
  730.6 47.4 %collective-permute-start.43 = (bf16[128,2304]{1,0:T(8,128)(2,1)}, bf16[128,2304]{1,0:T(8,128)(2,1)}, u32[]{:S(2)}, u32[]{:S(2)}) collective-permute-start(bf16[128,2304]{1,0:T(8,128)(2,1)} %get-tuple-element.151), channel_id=1, source_target_pairs={{0,16},{16,0},{1,17},{17,1},{2,18},{18,2},{3,19},{19,3},{4,20},{20... | collective-permute-start | bytes 1769480 | tf_op jit(solution)/shard_map/ppermute | solution.py:154
  888.8 179.5 %reduce-scatter.5.cloned.1.call-start = ((), (), s32[]{:S(2)}) async-start(), calls=%async_computation.6 | async-start | bytes 4718592 | tf_op jit(solution)/shard_map/reduce_scatter | solution.py:559
  935.4 301.0 %reduce-scatter.11.cloned.1.call-start = ((), (), s32[]{:S(2)}) async-start(), calls=%async_computation.9 | async-start | bytes 3620864 | tf_op jit(solution)/shard_map/reduce_scatter | solution.py:278
  1087.7 67.3 %collective-permute-start.58 = (f32[16,14336]{1,0:T(8,128)}, f32[16,14336]{1,0:T(8,128)}, u32[]{:S(2)}, u32[]{:S(2)}) collective-permute-start(f32[16,14336]{1,0:T(8,128)} %pad_maximum_fusion.6), channel_id=1, source_target_pairs={{0,16},{16,0},{1,17},{17,1},{2,18},{18,2},{3,19},{19,3},{4,20},{20... | collective-permute-start | bytes 2752520 | tf_op jit(solution)/shard_map/ppermute | solution.py:154
  1091.8 77.6 %collective-permute-start.55 = (f32[16,14336]{1,0:T(8,128)}, f32[16,14336]{1,0:T(8,128)}, u32[]{:S(2)}, u32[]{:S(2)}) collective-permute-start(f32[16,14336]{1,0:T(8,128)} %pad_maximum_fusion.5), channel_id=1, source_target_pairs={{0,16},{16,0},{1,17},{17,1},{2,18},{18,2},{3,19},{19,3},{4,20},{20... | collective-permute-start | bytes 2752520 | tf_op jit(solution)/shard_map/ppermute | solution.py:154
  1093.8 52.5 %collective-permute-start.56 = (f32[16,5632]{1,0:T(8,128)S(1)}, f32[16,5632]{1,0:T(8,128)S(1)}, u32[]{:S(2)}, u32[]{:S(2)}) collective-permute-start(f32[16,5632]{1,0:T(8,128)S(1)} %bitcast_dynamic-update-slice_fusion.36), channel_id=1, source_target_pairs={{0,16},{16,0},{1,17},{17,1},{2,18},{18,2},{3,19},{19,3},{4,20},{20... | collective-permute-start | bytes 1081352 | tf_op jit(solution)/shard_map/ppermute | solution.py:154
  1101.0 81.5 %collective-permute-start.53 = (f32[128,2304]{1,0:T(8,128)}, f32[128,2304]{1,0:T(8,128)}, u32[]{:S(2)}, u32[]{:S(2)}) collective-permute-start(f32[128,2304]{1,0:T(8,128)} %dynamic-slice_bitcast_fusion.2), channel_id=1, source_target_pairs={{0,16},{16,0},{1,17},{17,1},{2,18},{18,2},{3,19},{19,3},{4,20},{20... | collective-permute-start | bytes 3538952 | tf_op jit(solution)/shard_map/ppermute | solution.py:154
  1118.9 76.5 %collective-permute-start.47 = (f32[128,2304]{1,0:T(8,128)}, f32[128,2304]{1,0:T(8,128)}, u32[]{:S(2)}, u32[]{:S(2)}) collective-permute-start(f32[128,2304]{1,0:T(8,128)} %dynamic-slice_bitcast_fusion.4), channel_id=1, source_target_pairs={{0,16},{16,0},{1,17},{17,1},{2,18},{18,2},{3,19},{19,3},{4,20},{20... | collective-permute-start | bytes 3538952 | tf_op jit(solution)/shard_map/ppermute | solution.py:154
  1169.1 137.4 %reduce-scatter.9.cloned.1.call-start = ((), (), s32[]{:S(2)}) async-start(), calls=%async_computation.8 | async-start | bytes 3620864 | tf_op jit(solution)/shard_map/reduce_scatter | solution.py:278
  1237.3 73.4 %collective-permute-start.60 = (f32[16,1560]{1,0:T(8,128)S(1)}, f32[16,1560]{1,0:T(8,128)S(1)}, u32[]{:S(2)}, u32[]{:S(2)}) collective-permute-start(f32[16,1560]{1,0:T(8,128)S(1)} %dynamic-slice_bitcast_fusion.8), channel_id=1, source_target_pairs={{0,16},{16,0},{1,17},{17,1},{2,18},{18,2},{3,19},{19,3},{4,20},{20... | collective-permute-start | bytes 299528 | tf_op jit(solution)/shard_map/ppermute | solution.py:154
  (397 other events, 5027.5 us)
Sparse Core Ops, SparseCore 0:
  238.8 65.8 all-gather.4
  307.4 69.6 all-gather.2
  888.9 87.5 reduce-scatter.6
  980.0 88.2 reduce-scatter.4
  1169.2 67.1 reduce-scatter.10
  1240.1 66.3 reduce-scatter.8
